TPU v7x, 32 devices: a whole 2x2x4 slice. The times are simulated.
32 devices in a mesh: ctx: 4 (over z), exp: 8 (over y, x, core).
Axes of the slice: x: 2, y: 2, z: 4, core: 2. Of those that a mesh axis runs over, the one named last changes fastest.
Arguments:
- hidden_in: bfloat16 [8, 512, 2048], P('exp', 'ctx'), may hold values from -40 to 40
- expert_ids: int32 [8, 512, 8], P('exp', 'ctx'), may hold values from 0 to 31, all different within a row; in each aligned block of 128 rows (0 to 127, 128 to 255, ..., all dimensions but the last counted through in order) at most 42 rows name the same one
- gate_weights: float32 [8, 512, 8], P('exp', 'ctx'), may hold values from 0.1 to 0.4
- attn_gain: bfloat16 [2048], P('exp'), may hold values from 0.5 to 1.5
- w_query: bfloat16 [2048, 4096], P('exp'), may hold values from -0.125 to 0.125
- key_projection: bfloat16 [2048, 512], P('exp'), may hold values from -0.125 to 0.125
- value_projection: bfloat16 [2048, 512], P('exp'), may hold values from -0.125 to 0.125
- query_gain: bfloat16 [128], P('exp'), may hold values from 0.5 to 1.5
- key_norm_gain: bfloat16 [128], P('exp'), may hold values from 0.5 to 1.5
- w_output: bfloat16 [4096, 2048], P('exp'), may hold values from -0.75 to 0.75
- mlp_gain: bfloat16 [2048], P('exp'), may hold values from 0.5 to 1.5
- w_gate: bfloat16 [32, 2048, 768], P(('ctx', 'exp')), may hold values from -0.125 to 0.125
- w_up: bfloat16 [32, 2048, 768], P(('ctx', 'exp')), may hold values from -0.125 to 0.125
- w_down: bfloat16 [32, 768, 2048], P(('ctx', 'exp')), may hold values from -0.4375 to 0.4375
- grad_out: bfloat16 [8, 512, 2048], P('exp', 'ctx'), may hold values from -6 to 6
Outputs:
- hidden_out: bfloat16 [8, 512, 2048], P('exp', 'ctx')
- grad_in: float32 [8, 512, 2048], P('exp', 'ctx')
- grad_attn_gain: float32 [2048], P('exp')
- grad_w_query: float32 [2048, 4096], P('exp')
- grad_w_key: float32 [2048, 512], P('exp')
- grad_w_value: float32 [2048, 512], P('exp')
- grad_query_gain: float32 [128], P('exp')
- grad_key_gain: float32 [128], P('exp')
- grad_w_output: float32 [4096, 2048], P('exp')
- grad_mlp_gain: float32 [2048], P('exp')
- grad_w_gate: float32 [32, 2048, 768], P(('ctx', 'exp'))
- grad_w_up: float32 [32, 2048, 768], P(('ctx', 'exp'))
- grad_w_down: float32 [32, 768, 2048], P(('ctx', 'exp'))
Inputs may be any that keep to these rules, and one draw needn't show every extreme that they name: `expert_ids`: each row names 8 different experts; among the 128 rows of one device no expert is named more than 42 times, a bound that some block reaches.
All inputs are finite; a program needn't handle non-finite values.
Results may differ from a plain program's by a relative error of at most 0.023.
Values may be sent and summed in bfloat16 or wider, within the bound.
A program may use at most 320 MiB of HBM per device.

v0:
```python
import jax
import jax.numpy as jnp
from jax import lax
from jax.sharding import PartitionSpec as P

MODEL_WIDTH = 2048
QUERY_HEADS = 32
KEY_VALUE_HEADS = 4
HEAD_SIZE = 128
TOPK = 8


EPSILON = 1e-06
THETA = 1000000.0


def rms_scale(tensor):
    return lax.rsqrt(jnp.mean(tensor * tensor, axis=-1, keepdims=True) + EPSILON)


def norm_backward(cotangent, tensor, factor, weight):
    scaled = cotangent * weight
    unit_form = tensor * factor
    return factor * (scaled - unit_form * jnp.mean(scaled * unit_form, axis=-1, keepdims=True))


def rope_tables(positions):
    halfway = HEAD_SIZE // 2
    frequency = THETA ** (-(jnp.arange(halfway, dtype=jnp.float32) * (2.0 / HEAD_SIZE)))
    angles = positions.astype(jnp.float32)[:, None] * frequency[None, :]
    cosine_lookup = jnp.concatenate([jnp.cos(angles), jnp.cos(angles)], axis=-1)[:, None, :]
    sine_lookup = jnp.concatenate([jnp.sin(angles), jnp.sin(angles)], axis=-1)[:, None, :]
    return (cosine_lookup, sine_lookup)


def rotate(tensor, cosine_lookup, sine_lookup):
    halfway = tensor.shape[-1] // 2
    turned = jnp.concatenate([-tensor[..., halfway:], tensor[..., :halfway]], axis=-1)
    return tensor * cosine_lookup + turned * sine_lookup


def rotation_backward(cotangent, cosine_lookup, sine_lookup):
    halfway = cotangent.shape[-1] // 2
    sine_part = cotangent * sine_lookup
    turned = jnp.concatenate([sine_part[..., halfway:], -sine_part[..., :halfway]], axis=-1)
    return cotangent * cosine_lookup + turned


def project_heads(
    wide_in,
    attn_gain,
    w_query,
    key_projection,
    value_projection,
    query_gain,
    key_norm_gain,
    cosine_lookup,
    sine_lookup,
):
    row_total_count = wide_in.shape[0]
    first_scale = rms_scale(wide_in)
    normalized_input = (wide_in * first_scale * attn_gain.astype(jnp.float32)).astype(jnp.bfloat16)
    queries = jnp.dot(normalized_input, w_query, preferred_element_type=jnp.float32).reshape(
        row_total_count, QUERY_HEADS, HEAD_SIZE
    )
    key_unnormed = jnp.dot(
        normalized_input, key_projection, preferred_element_type=jnp.float32
    ).reshape(row_total_count, KEY_VALUE_HEADS, HEAD_SIZE)
    values_raw = jnp.dot(normalized_input, value_projection, preferred_element_type=jnp.float32)
    query_scale = rms_scale(queries)
    key_rms_factor = rms_scale(key_unnormed)
    query_rotated = rotate(
        queries * query_scale * query_gain.astype(jnp.float32), cosine_lookup, sine_lookup
    ).astype(jnp.bfloat16)
    key_rotated = rotate(
        key_unnormed * key_rms_factor * key_norm_gain.astype(jnp.float32),
        cosine_lookup,
        sine_lookup,
    ).astype(jnp.bfloat16)
    value_row_block = values_raw.astype(jnp.bfloat16)
    return (
        first_scale,
        normalized_input,
        queries,
        query_scale,
        key_unnormed,
        key_rms_factor,
        query_rotated,
        key_rotated,
        value_row_block,
    )


def per_device(
    hidden_in,
    expert_ids,
    gate_weights,
    attn_gain,
    w_query,
    key_projection,
    value_projection,
    query_gain,
    key_norm_gain,
    w_output,
    mlp_gain,
    w_gate,
    w_up,
    w_down,
    grad_out,
):
    local_length = hidden_in.shape[1]
    ctx_index = lax.axis_index("ctx")
    ctx_count = lax.axis_size("ctx")
    expert_count = ctx_count * lax.axis_size("exp")
    capacity = max(2, local_length * TOPK * 4 // (3 * expert_count))
    query_group_width = QUERY_HEADS // KEY_VALUE_HEADS
    factor = HEAD_SIZE ** (-0.5)
    shards = (
        attn_gain,
        w_query,
        key_projection,
        value_projection,
        query_gain,
        key_norm_gain,
        w_output,
        mlp_gain,
    )
    gathered = (
        lax.all_gather(shards[0], "exp", axis=0, tiled=True),
        lax.all_gather(shards[1], "exp", axis=0, tiled=True),
        lax.all_gather(shards[2], "exp", axis=0, tiled=True),
        lax.all_gather(shards[3], "exp", axis=0, tiled=True),
        lax.all_gather(shards[4], "exp", axis=0, tiled=True),
        lax.all_gather(shards[5], "exp", axis=0, tiled=True),
        lax.all_gather(shards[6], "exp", axis=0, tiled=True),
        lax.all_gather(shards[7], "exp", axis=0, tiled=True),
    )
    positions = ctx_index * local_length + jnp.arange(local_length, dtype=jnp.int32)
    cosine_lookup, sine_lookup = rope_tables(positions)
    wide_in = hidden_in[0].astype(jnp.float32)
    (
        first_scale,
        normalized_input,
        queries,
        query_scale,
        key_unnormed,
        key_rms_factor,
        query_rotated,
        key_rotated,
        value_row_block,
    ) = project_heads(
        wide_in,
        gathered[0],
        gathered[1],
        gathered[2],
        gathered[3],
        gathered[4],
        gathered[5],
        cosine_lookup,
        sine_lookup,
    )
    key_row_block = key_rotated.reshape(local_length, KEY_VALUE_HEADS * HEAD_SIZE)
    query_fourfold = query_rotated.reshape(
        local_length, KEY_VALUE_HEADS, query_group_width, HEAD_SIZE
    )
    last_pos = ctx_index * local_length + local_length - 1
    start_fold = (
        jnp.zeros((KEY_VALUE_HEADS, query_group_width, local_length, HEAD_SIZE), jnp.float32),
        jnp.zeros((KEY_VALUE_HEADS, query_group_width, local_length), jnp.float32),
    )
    key_portion = lax.all_gather(key_row_block, "ctx", axis=0, tiled=True)
    value_portion = lax.all_gather(value_row_block, "ctx", axis=0, tiled=True)
    key_total_count = key_portion.shape[0]

    def attend_piece(current):
        key_threefold = key_portion.reshape(key_total_count, KEY_VALUE_HEADS, HEAD_SIZE)
        value_threefold = value_portion.reshape(key_total_count, KEY_VALUE_HEADS, HEAD_SIZE)
        scores = (
            jnp.einsum(
                "qkgd,tkd->kgqt", query_fourfold, key_threefold, preferred_element_type=jnp.float32
            )
            * factor
        )
        key_pos = jnp.arange(key_total_count, dtype=jnp.int32)
        causal = key_pos[None, :] <= positions[:, None]
        expos = jnp.where(causal, jnp.exp(scores), 0.0)
        acc_sum = jnp.einsum(
            "kgqt,tkd->kgqd",
            expos.astype(jnp.bfloat16),
            value_threefold,
            preferred_element_type=jnp.float32,
        )
        return (acc_sum, jnp.sum(expos, axis=-1))

    acc_sum, total_sum = lax.cond(
        jnp.int32(0) <= last_pos, attend_piece, lambda current: current, start_fold
    )
    attention_rows = (
        jnp.transpose(acc_sum / total_sum[..., None], (2, 0, 1, 3))
        .reshape(local_length, QUERY_HEADS * HEAD_SIZE)
        .astype(jnp.bfloat16)
    )
    mid = wide_in + jnp.dot(attention_rows, gathered[6], preferred_element_type=jnp.float32)
    second_scale = rms_scale(mid)
    mlp_in = (mid * second_scale * gathered[7].astype(jnp.float32)).astype(jnp.bfloat16)
    flat_ids = expert_ids[0].reshape(-1)
    onehot = (flat_ids[:, None] == jnp.arange(expert_count, dtype=jnp.int32)[None, :]).astype(
        jnp.int32
    )
    earlier = jnp.cumsum(onehot, axis=0) - onehot
    slot_rank = jnp.sum(earlier * onehot, axis=1)
    dest_rows = flat_ids * capacity + slot_rank
    matches = (
        jnp.arange(expert_count * capacity, dtype=jnp.int32)[:, None] == dest_rows[None, :]
    ).reshape(expert_count * capacity, local_length, TOPK)
    spread = jnp.any(matches, axis=2).astype(jnp.bfloat16)
    slot_gates = jnp.sum(jnp.where(matches, gate_weights[0][None, :, :], 0.0), axis=(1, 2))
    outbound = (
        jnp.dot(spread, mlp_in, preferred_element_type=jnp.float32)
        .astype(jnp.bfloat16)
        .reshape(expert_count, capacity, MODEL_WIDTH)
    )
    arrived = lax.all_to_all(
        outbound, ("ctx", "exp"), split_axis=0, concat_axis=0, tiled=True
    ).reshape(-1, MODEL_WIDTH)
    gate_pre = jnp.dot(arrived, w_gate[0], preferred_element_type=jnp.float32)
    up_pre = jnp.dot(arrived, w_up[0], preferred_element_type=jnp.float32)
    sigmoid_gate = jax.nn.sigmoid(gate_pre)
    silu_gate = gate_pre * sigmoid_gate
    inner = (silu_gate * up_pre).astype(jnp.bfloat16)
    expert_out = (
        jnp.dot(inner, w_down[0], preferred_element_type=jnp.float32)
        .astype(jnp.bfloat16)
        .reshape(expert_count, capacity, MODEL_WIDTH)
    )
    returned = lax.all_to_all(
        expert_out, ("ctx", "exp"), split_axis=0, concat_axis=0, tiled=True
    ).reshape(-1, MODEL_WIDTH)
    picked = returned[dest_rows].reshape(local_length, TOPK, MODEL_WIDTH)
    mixed = jnp.sum(gate_weights[0][:, :, None] * picked.astype(jnp.float32), axis=1)
    hidden_out = (mid + mixed).astype(jnp.bfloat16)
    weights_back = (
        lax.all_gather(shards[0], "exp", axis=0, tiled=True),
        lax.all_gather(shards[1], "exp", axis=0, tiled=True),
        lax.all_gather(shards[2], "exp", axis=0, tiled=True),
        lax.all_gather(shards[3], "exp", axis=0, tiled=True),
        lax.all_gather(shards[4], "exp", axis=0, tiled=True),
        lax.all_gather(shards[5], "exp", axis=0, tiled=True),
        lax.all_gather(shards[6], "exp", axis=0, tiled=True),
        lax.all_gather(shards[7], "exp", axis=0, tiled=True),
    )
    (
        first_gain,
        query_weight,
        key_weight,
        value_weight,
        query_norm,
        key_norm,
        out_weight,
        second_gain,
    ) = weights_back
    gradient_widened = grad_out[0].astype(jnp.float32)
    slot_grads = jnp.dot(spread, grad_out[0], preferred_element_type=jnp.float32)
    sends = (
        (slot_gates[:, None] * slot_grads)
        .astype(jnp.bfloat16)
        .reshape(expert_count, capacity, MODEL_WIDTH)
    )
    grad_arrived = lax.all_to_all(
        sends, ("ctx", "exp"), split_axis=0, concat_axis=0, tiled=True
    ).reshape(-1, MODEL_WIDTH)
    grad_inner = jnp.dot(grad_arrived, w_down[0].T, preferred_element_type=jnp.float32)
    grad_down = jnp.dot(inner.T, grad_arrived, preferred_element_type=jnp.float32)
    grad_gate_pre = (
        grad_inner * up_pre * sigmoid_gate * (1.0 + gate_pre * (1.0 - sigmoid_gate))
    ).astype(jnp.bfloat16)
    grad_up_pre = (grad_inner * silu_gate).astype(jnp.bfloat16)
    grad_gate_mat = jnp.dot(arrived.T, grad_gate_pre, preferred_element_type=jnp.float32)
    grad_up_mat = jnp.dot(arrived.T, grad_up_pre, preferred_element_type=jnp.float32)
    grad_expert_in = (
        (
            jnp.dot(grad_gate_pre, w_gate[0].T, preferred_element_type=jnp.float32)
            + jnp.dot(grad_up_pre, w_up[0].T, preferred_element_type=jnp.float32)
        )
        .astype(jnp.bfloat16)
        .reshape(expert_count, capacity, MODEL_WIDTH)
    )
    grad_returned = lax.all_to_all(
        grad_expert_in, ("ctx", "exp"), split_axis=0, concat_axis=0, tiled=True
    ).reshape(-1, MODEL_WIDTH)
    grad_mlp = jnp.sum(
        grad_returned[dest_rows].reshape(local_length, TOPK, MODEL_WIDTH).astype(jnp.float32),
        axis=1,
    )
    mlp_gain_part = jnp.sum(grad_mlp * mid * second_scale, axis=0)
    grad_mid = gradient_widened + norm_backward(
        grad_mlp, mid, second_scale, second_gain.astype(jnp.float32)
    )
    grad_branch = grad_mid.astype(jnp.bfloat16)
    attention_gradient = jnp.dot(
        grad_branch, out_weight.T, preferred_element_type=jnp.float32
    ).astype(jnp.bfloat16)
    keys_all, values_all = (
        lax.all_gather(key_row_block, "ctx", axis=0, tiled=True),
        lax.all_gather(value_row_block, "ctx", axis=0, tiled=True),
    )
    gradient_fourfold = attention_gradient.reshape(
        local_length, KEY_VALUE_HEADS, query_group_width, HEAD_SIZE
    )
    deltas = jnp.transpose(
        jnp.sum(
            gradient_fourfold.astype(jnp.float32)
            * attention_rows.reshape(
                local_length, KEY_VALUE_HEADS, query_group_width, HEAD_SIZE
            ).astype(jnp.float32),
            axis=-1,
        ),
        (1, 2, 0),
    )
    query_gradient_running = jnp.zeros(
        (KEY_VALUE_HEADS, query_group_width, local_length, HEAD_SIZE), jnp.float32
    )
    key_terms = []
    value_terms = []
    for column in range(ctx_count):
        key_block = keys_all[column * local_length : (column + 1) * local_length].reshape(
            local_length, KEY_VALUE_HEADS, HEAD_SIZE
        )
        value_block = values_all[column * local_length : (column + 1) * local_length].reshape(
            local_length, KEY_VALUE_HEADS, HEAD_SIZE
        )

        def block_work(running):
            scores = (
                jnp.einsum(
                    "qkgd,tkd->kgqt", query_fourfold, key_block, preferred_element_type=jnp.float32
                )
                * factor
            )
            key_pos = column * local_length + jnp.arange(local_length, dtype=jnp.int32)
            causal = key_pos[None, :] <= positions[:, None]
            probs = jnp.where(causal, jnp.exp(scores), 0.0) / total_sum[..., None]
            value_gradient = jnp.einsum(
                "kgqt,qkgd->tkd",
                probs.astype(jnp.bfloat16),
                gradient_fourfold,
                preferred_element_type=jnp.float32,
            )
            grad_probs = jnp.einsum(
                "qkgd,tkd->kgqt", gradient_fourfold, value_block, preferred_element_type=jnp.float32
            )
            grad_scores = (probs * (grad_probs - deltas[..., None]) * factor).astype(jnp.bfloat16)
            running = running + jnp.einsum(
                "kgqt,tkd->kgqd", grad_scores, key_block, preferred_element_type=jnp.float32
            )
            key_gradient = jnp.einsum(
                "kgqt,qkgd->tkd", grad_scores, query_fourfold, preferred_element_type=jnp.float32
            )
            return (
                running,
                key_gradient.reshape(local_length, KEY_VALUE_HEADS * HEAD_SIZE),
                value_gradient.reshape(local_length, KEY_VALUE_HEADS * HEAD_SIZE),
            )

        def block_skip(running):
            empty_rows = jnp.zeros((local_length, KEY_VALUE_HEADS * HEAD_SIZE), jnp.float32)
            return (running, empty_rows, empty_rows)

        query_gradient_running, key_term, value_term = lax.cond(
            column <= ctx_index, block_work, block_skip, query_gradient_running
        )
        key_terms.append(key_term)
        value_terms.append(value_term)
    key_gradient_list, value_grads = (
        lax.psum_scatter(
            jnp.concatenate(key_terms, axis=0), "ctx", scatter_dimension=0, tiled=True
        ),
        lax.psum_scatter(
            jnp.concatenate(value_terms, axis=0), "ctx", scatter_dimension=0, tiled=True
        ),
    )
    grad_queries = rotation_backward(
        jnp.transpose(query_gradient_running, (2, 0, 1, 3)).reshape(
            local_length, QUERY_HEADS, HEAD_SIZE
        ),
        cosine_lookup,
        sine_lookup,
    )
    key_gradient = rotation_backward(
        key_gradient_list.reshape(local_length, KEY_VALUE_HEADS, HEAD_SIZE),
        cosine_lookup,
        sine_lookup,
    )
    query_gain_part = jnp.sum(grad_queries * queries * query_scale, axis=(0, 1))
    key_gain_part = jnp.sum(key_gradient * key_unnormed * key_rms_factor, axis=(0, 1))
    grad_query_rows = (
        norm_backward(grad_queries, queries, query_scale, query_norm.astype(jnp.float32))
        .reshape(local_length, QUERY_HEADS * HEAD_SIZE)
        .astype(jnp.bfloat16)
    )
    key_row_gradient = (
        norm_backward(key_gradient, key_unnormed, key_rms_factor, key_norm.astype(jnp.float32))
        .reshape(local_length, KEY_VALUE_HEADS * HEAD_SIZE)
        .astype(jnp.bfloat16)
    )
    value_row_gradient = value_grads.astype(jnp.bfloat16)
    grad_normed = (
        jnp.dot(grad_query_rows, query_weight.T, preferred_element_type=jnp.float32)
        + jnp.dot(key_row_gradient, key_weight.T, preferred_element_type=jnp.float32)
        + jnp.dot(value_row_gradient, value_weight.T, preferred_element_type=jnp.float32)
    )
    attn_gain_part = jnp.sum(grad_normed * wide_in * first_scale, axis=0)
    grad_in = grad_mid + norm_backward(
        grad_normed, wide_in, first_scale, first_gain.astype(jnp.float32)
    )
    grad_wout = jnp.dot(attention_rows.T, grad_branch, preferred_element_type=jnp.float32)
    grad_wq = jnp.dot(normalized_input.T, grad_query_rows, preferred_element_type=jnp.float32)
    grad_wk = jnp.dot(normalized_input.T, key_row_gradient, preferred_element_type=jnp.float32)
    grad_wv = jnp.dot(normalized_input.T, value_row_gradient, preferred_element_type=jnp.float32)
    owner_parts = (
        lax.psum_scatter(attn_gain_part, "exp", scatter_dimension=0, tiled=True),
        lax.psum_scatter(grad_wq, "exp", scatter_dimension=0, tiled=True),
        lax.psum_scatter(grad_wk, "exp", scatter_dimension=0, tiled=True),
        lax.psum_scatter(grad_wv, "exp", scatter_dimension=0, tiled=True),
        lax.psum_scatter(query_gain_part, "exp", scatter_dimension=0, tiled=True),
        lax.psum_scatter(key_gain_part, "exp", scatter_dimension=0, tiled=True),
        lax.psum_scatter(grad_wout, "exp", scatter_dimension=0, tiled=True),
        lax.psum_scatter(mlp_gain_part, "exp", scatter_dimension=0, tiled=True),
    )
    final_parts = lax.psum(
        (
            owner_parts[0],
            owner_parts[1],
            owner_parts[2],
            owner_parts[3],
            owner_parts[4],
            owner_parts[5],
            owner_parts[6],
            owner_parts[7],
        ),
        "ctx",
    )
    return (
        hidden_out[None],
        grad_in[None],
        final_parts[0],
        final_parts[1],
        final_parts[2],
        final_parts[3],
        final_parts[4],
        final_parts[5],
        final_parts[6],
        final_parts[7],
        grad_gate_mat[None],
        grad_up_mat[None],
        grad_down[None],
    )


def solution(mesh):
    in_specs = (
        P("exp", "ctx", None),
        P("exp", "ctx", None),
        P("exp", "ctx", None),
        P("exp"),
        P("exp", None),
        P("exp", None),
        P("exp", None),
        P("exp"),
        P("exp"),
        P("exp", None),
        P("exp"),
        P(("ctx", "exp"), None, None),
        P(("ctx", "exp"), None, None),
        P(("ctx", "exp"), None, None),
        P("exp", "ctx", None),
    )
    out_specs = (
        P("exp", "ctx", None),
        P("exp", "ctx", None),
        P("exp"),
        P("exp", None),
        P("exp", None),
        P("exp", None),
        P("exp"),
        P("exp"),
        P("exp", None),
        P("exp"),
        P(("ctx", "exp"), None, None),
        P(("ctx", "exp"), None, None),
        P(("ctx", "exp"), None, None),
    )
    return jax.shard_map(
        per_device, mesh=mesh, in_specs=in_specs, out_specs=out_specs, check_vma=False
    )
```

profile of v0, /device:TPU:0, one launch (start us, length us, event | category | flops | bytes accessed | tf_op | source)
XLA Modules:
  0.0 1853.9 jit_solution(5465493550912503165)
XLA Ops:
  10.3 9.0 reduce-window.6
  20.0 4.9 fusion.35
  24.9 10.1 select_reduce_fusion
  35.0 5.1 multiply_convert_fusion
  40.0 8.0 reshape.366
  48.0 7.4 all-to-all-start.2
  55.5 54.0 %all-gather = bf16[8,1,256]{2,1,0:T(2,128)(2,1)S(1)} all-gather(bf16[1,1,256]{2,1,0:T(2,128)(2,1)S(1)} %reshape.398), channel_id=1, replica_groups=mesh['ctx'=4,'exp'=8] {'exp'}, dimensions={0}, use_global_device_ids=true | all-gather | bytes 4608 | tf_op jit(solution)/shard_map/all_gather | solution.py:129
  111.3 20.3 %all-reduce.9 = (bf16[128]{0:T(256)(128)(2,1)S(1)}, bf16[128]{0:T(256)(128)(2,1)S(1)}) all-reduce(bf16[128]{0:T(256)(128)(2,1)S(1)} %dynamic-update-slice, bf16[128]{0:T(256)(128)(2,1)S(1)} %dynamic-update-slice.1), channel_id=1, replica_groups=mesh['ctx'=4,'exp'=8] {'exp'}, use_global_device_ids=true, to_apply=%add | all-reduce | flops 256 | bytes 1024
  132.2 13.0 all-gather.1
  146.8 3.9 copy.213
  154.1 54.6 %all_gather.43 = bf16[512,512]{0,1:T(8,128)(2,1)} all-gather(bf16[128,512]{0,1:T(8,128)(2,1)S(1)} %bitcast.398), channel_id=1, replica_groups=mesh['ctx'=4,'exp'=8] {'ctx'}, dimensions={0}, use_global_device_ids=true | all-gather | bytes 655360 | tf_op jit(solution)/shard_map/all_gather | solution.py:171
  210.9 18.4 all_gather.47
  229.3 21.9 %copy.214 = bf16[4096,2048]{1,0:T(8,128)(2,1)} copy(bf16[4096,2048]{0,1:T(8,128)(2,1)} %bitcast.360) | data formatting | bytes 33554432 | tf_op jit(solution)/shard_map/dot_general | solution.py:63
  251.2 8.4 multiply_reduce_fusion.3
  262.6 16.8 conditional.5
  262.6 8.5 fusion
  273.1 6.3 fusion.2
  279.4 2.9 divide_convert_fusion
  282.3 33.6 %all-gather.13.cloned.1.call-done = bf16[4096,2048]{1,0:T(8,128)(2,1)} async-done(((bf16[512,2048]{1,0:T(8,128)(2,1)}), bf16[4096,2048]{1,0:T(8,128)(2,1)}) %all-gather.13.cloned.1.call-update) | async-done | bytes 16777232 | tf_op jit(solution)/shard_map/all_gather | solution.py:135
  315.9 8.5 multiply_reduce_fusion.6
  325.5 4.1 convolution_convert_fusion.1
  329.6 8.0 reshape.362
  337.5 4.9 all-to-all-start
  342.5 8.0 reshape.367
  350.5 131.8 %all-to-all-done = bf16[32,42,2048]{2,1,0:T(8,128)(2,1)} async-done(((bf16[32,42,2048]{2,1,0:T(8,128)(2,1)}), bf16[32,42,2048]{2,1,0:T(8,128)(2,1)}, u32[]{:S(2)}, u32[]{:S(2)}) %all-to-all-start) | async-done | bytes 5505056 | tf_op jit(solution)/shard_map/all_to_all | solution.py:223
  482.2 8.0 reshape.363
  490.3 7.5 fusion.45
  497.8 6.0 fusion.41
  503.8 9.1 multiply_convert_fusion.1
  512.9 7.2 fusion.43
  520.2 8.9 add_convert_fusion
  529.1 8.0 reshape.368
  537.0 4.0 all-to-all-start.3
  541.1 7.8 convolution_convert_fusion
  548.8 8.0 reshape.364
  556.8 124.0 %all-to-all-done.3 = bf16[32,42,2048]{2,1,0:T(8,128)(2,1)} async-done(((bf16[32,42,2048]{2,1,0:T(8,128)(2,1)}), bf16[32,42,2048]{2,1,0:T(8,128)(2,1)}, u32[]{:S(2)}, u32[]{:S(2)}) %all-to-all-start.3) | async-done | bytes 5505056 | tf_op jit(solution)/shard_map/all_to_all | solution.py:288
  680.8 3.6 all-to-all-start.1
  684.8 8.1 reshape.369
  692.9 12.1 gather_fusion.1
  704.9 5.1 convert_reduce_fusion
  711.0 113.3 %all-to-all-done.1 = bf16[32,42,2048]{2,1,0:T(8,128)(2,1)} async-done(((bf16[32,42,2048]{2,1,0:T(8,128)(2,1)}), bf16[32,42,2048]{2,1,0:T(8,128)(2,1)}, u32[]{:S(2)}, u32[]{:S(2)}) %all-to-all-start.1) | async-done | bytes 5505056 | tf_op jit(solution)/shard_map/all_to_all | solution.py:236
  824.2 8.1 reshape.365
  832.3 12.2 gather_fusion
  844.6 6.6 fusion.34
  852.4 11.8 fusion.49
  867.5 12.4 conditional.6
  868.4 3.2 fusion.13
  889.2 65.0 %reduce-scatter.7.cloned.1.call-done = f32[128,512]{0,1:T(8,128)} async-done(((f32[512,512]{0,1:T(8,128)}), f32[128,512]{0,1:T(8,128)}) %reduce-scatter.7.cloned.1.call-update) | async-done | bytes 262160 | tf_op jit(solution)/shard_map/reduce_scatter | solution.py:375
  959.4 23.3 %reduce-scatter.9.cloned.1.call-done = f32[128,512]{0,1:T(8,128)} async-done(((f32[512,512]{0,1:T(8,128)}), f32[128,512]{0,1:T(8,128)}) %reduce-scatter.9.cloned.1.call-update) | async-done | bytes 262160 | tf_op jit(solution)/shard_map/reduce_scatter | solution.py:378
  982.7 3.8 fusion.84
  995.4 13.9 fusion.75
  1010.9 13.5 fusion.81
  1024.4 11.9 reduce-scatter.13.cloned.1.call-done
  1036.3 55.1 %reduce-scatter.15.cloned.1.call-done = f32[256,512]{1,0:T(8,128)} async-done(((f32[2048,512]{1,0:T(8,128)}), f32[256,512]{1,0:T(8,128)}) %reduce-scatter.15.cloned.1.call-update) | async-done | bytes 524304 | tf_op jit(solution)/shard_map/reduce_scatter | solution.py:424
  1091.4 209.1 %reduce-scatter.11.cloned.1.call-done = f32[256,4096]{1,0:T(8,128)} async-done(((f32[2048,4096]{1,0:T(8,128)}), f32[256,4096]{1,0:T(8,128)}) %reduce-scatter.11.cloned.1.call-update) | async-done | bytes 4194320 | tf_op jit(solution)/shard_map/reduce_scatter | solution.py:422
  1300.5 208.9 %reduce-scatter.17.cloned.1.call-done = f32[512,2048]{1,0:T(8,128)} async-done(((f32[4096,2048]{1,0:T(8,128)}), f32[512,2048]{1,0:T(8,128)}) %reduce-scatter.17.cloned.1.call-update) | async-done | bytes 4194320 | tf_op jit(solution)/shard_map/reduce_scatter | solution.py:427
  1510.8 9.8 convolution_bitcast_fusion.2
  1520.6 9.7 convolution_bitcast_fusion.1
  1530.3 7.1 convolution_bitcast_fusion
  1537.4 12.6 fusion.106
  1553.9 24.6 %all-reduce.6 = (f32[2048]{0:T(1024)S(1)}, f32[128]{0:T(128)S(1)}, f32[128]{0:T(128)S(1)}, f32[2048]{0:T(1024)S(1)}) all-reduce(f32[2048]{0:T(1024)S(1)} %get-tuple-element.310, f32[128]{0:T(128)S(1)} %get-tuple-element.306, f32[128]{0:T(128)S(1)} %get-tuple-element.312, ...), channel_id=4, replica_groups=mesh['ctx'=4,'exp'=8] {'exp'}, use_global_device_ids=true, to_apply=%region_30.31.clone | all-reduce | flops 4352 | bytes 34816
  1578.8 12.8 all-reduce.7
  1592.9 244.4 %all-reduce.12.cloned.1.call-done = (f32[256,4096]{1,0:T(8,128)}, f32[256,512]{1,0:T(8,128)}, f32[256,512]{1,0:T(8,128)}, f32[512,2048]{1,0:T(8,128)}) async-done(((f32[256,4096]{1,0:T(8,128)}, f32[256,512]{1,0:T(8,128)}, f32[256,512]{1,0:T(8,128)}, f32[512,2048]{1,0:T(8,128)}), (f32[256,4096]{1,0:T(8,128)}, f32[256,512]{1,0:T(8,128)}, f32[256,512]{1,0:T(8,128)}, ...) | async-done | bytes 9437200 | tf_op jit(solution)/shard_map/psum | solution.py:430
  1837.3 4.8 copy.350
  (255 shorter events, 72.8 us)
Async XLA Ops:
  7.2 496.6 %copy-start = (bf16[1,768,2048]{2,1,0:T(8,128)(2,1)S(1)}, bf16[1,768,2048]{2,1,0:T(8,128)(2,1)}, u32[]{:S(2)}) copy-start(bf16[1,768,2048]{2,1,0:T(8,128)(2,1)} %param.38) | copy-start | bytes 9437188
  7.2 139.6 %all-gather.7.cloned.1.call-start = ((), (), s32[]{:S(2)}) async-start(), calls=%async_computation.10 | async-start | bytes 2359296 | tf_op jit(solution)/shard_map/all_gather | solution.py:131
  7.9 200.7 %all-gather.11.cloned.1.call-start = ((), (), s32[]{:S(2)}) async-start(), calls=%async_computation.12 | async-start | bytes 2359296 | tf_op jit(solution)/shard_map/all_gather | solution.py:132
  8.7 220.6 %all-gather.9.cloned.1.call-start = ((), (), s32[]{:S(2)}) async-start(), calls=%async_computation.11 | async-start | bytes 18874368 | tf_op jit(solution)/shard_map/all_gather | solution.py:130
  9.4 15.5 copy-start.53
  9.4 306.5 %all-gather.13.cloned.1.call-start = ((), (), s32[]{:S(2)}) async-start(), calls=%async_computation.13 | async-start | bytes 18874368 | tf_op jit(solution)/shard_map/all_gather | solution.py:135
  48.0 7.5 copy-start.64
  48.0 61.6 %copy-start.61 = (u32[32]{0:T(128)S(1)}, u32[32]{0:T(128)}, u32[]{:S(2)}) copy-start(u32[32]{0:T(128)} %constant.101) | copy-start | bytes 388
  48.0 62.8 %copy-start.65 = (bf16[16]{0:T(256)(128)(2,1)S(1)}, bf16[16]{0:T(256)(128)(2,1)}, u32[]{:S(2)}) copy-start(bf16[16]{0:T(256)(128)(2,1)} %param.33) | copy-start | bytes 100
  48.0 63.1 %copy-start.66 = (bf16[16]{0:T(256)(128)(2,1)S(1)}, bf16[16]{0:T(256)(128)(2,1)}, u32[]{:S(2)}) copy-start(bf16[16]{0:T(256)(128)(2,1)} %param.32) | copy-start | bytes 100
  48.0 84.2 %copy-start.67 = (bf16[256]{0:T(256)(128)(2,1)S(1)}, bf16[256]{0:T(256)(128)(2,1)}, u32[]{:S(2)}) copy-start(bf16[256]{0:T(256)(128)(2,1)} %param.35) | copy-start | bytes 1540
  48.0 289.5 %all-to-all-start.2 = ((bf16[32,42,2048]{2,1,0:T(8,128)(2,1)}), bf16[32,42,2048]{2,1,0:T(8,128)(2,1)}, u32[]{:S(2)}, u32[]{:S(2)}) async-start(bf16[32,42,2048]{2,1,0:T(8,128)(2,1)} %reshape.366), calls=%async_computation.2 | async-start | bytes 12582912 | tf_op jit(solution)/shard_map/all_to_all | solution.py:269
  109.5 141.7 %copy-start.35 = (f32[8,1,256]{2,1,0:T(1,128)}, f32[8,1,256]{2,1,0:T(1,128)S(1)}, u32[]{:S(2)}) copy-start(f32[8,1,256]{2,1,0:T(1,128)S(1)} %convert_element_type.238) | copy-start | bytes 24580
  131.6 21.8 %copy-start.56 = (f32[128]{0:T(128)}, f32[128]{0:T(128)S(1)}, u32[]{:S(2)}) copy-start(f32[128]{0:T(128)S(1)} %convert_element_type.195) | copy-start | bytes 1540
  145.2 117.4 %copy-start.54 = (s32[128]{0:T(128)}, s32[128]{0:T(128)S(1)}, u32[]{:S(2)}) copy-start(s32[128]{0:T(128)S(1)} %iota_add_fusion.3) | copy-start | bytes 1540
  145.4 114.8 %copy-start.30 = (f32[128,128]{0,1:T(8,128)}, f32[128,128]{0,1:T(8,128)S(1)}, u32[]{:S(2)}) copy-start(f32[128,128]{0,1:T(8,128)S(1)} %get-tuple-element.356) | copy-start | bytes 196612
  145.4 114.8 %copy-start.32 = (f32[128,128]{0,1:T(8,128)}, f32[128,128]{0,1:T(8,128)S(1)}, u32[]{:S(2)}) copy-start(f32[128,128]{0,1:T(8,128)S(1)} %get-tuple-element.357) | copy-start | bytes 196612
  146.7 104.5 %copy-start.51 = (f32[128]{0:T(128)}, f32[128]{0:T(128)S(1)}, u32[]{:S(2)}) copy-start(f32[128]{0:T(128)S(1)} %add_rsqrt_fusion.3) | copy-start | bytes 1540
  153.3 57.6 %copy-start.48 = (f32[128,4]{0,1:T(4,128)}, f32[128,4]{0,1:T(4,128)S(1)}, u32[]{:S(2)}) copy-start(f32[128,4]{0,1:T(4,128)S(1)} %add_rsqrt_fusion.1) | copy-start | bytes 6148
  251.2 8.5 copy-start.58
  279.4 600.4 %copy-start.47 = (f32[4,8,128]{2,1,0:T(8,128)}, f32[4,8,128]{2,1,0:T(8,128)S(1)}, u32[]{:S(2)}) copy-start(f32[4,8,128]{2,1,0:T(8,128)S(1)} %get-tuple-element.152) | copy-start | bytes 49156
  337.5 144.7 %all-to-all-start = ((bf16[32,42,2048]{2,1,0:T(8,128)(2,1)}), bf16[32,42,2048]{2,1,0:T(8,128)(2,1)}, u32[]{:S(2)}, u32[]{:S(2)}) async-start(bf16[32,42,2048]{2,1,0:T(8,128)(2,1)} %reshape.362), calls=%async_computation | async-start | bytes 12582912 | tf_op jit(solution)/shard_map/all_to_all | solution.py:223
  490.3 7.5 copy-start.23
  490.3 7.5 copy-start.63
  490.3 13.5 slice-start
  497.8 6.0 slice-start.1
  503.8 9.1 copy-start.62
  512.9 7.2 copy-start.69
  512.9 7.2 copy-start.70
  537.0 143.8 %all-to-all-start.3 = ((bf16[32,42,2048]{2,1,0:T(8,128)(2,1)}), bf16[32,42,2048]{2,1,0:T(8,128)(2,1)}, u32[]{:S(2)}, u32[]{:S(2)}) async-start(bf16[32,42,2048]{2,1,0:T(8,128)(2,1)} %reshape.368), calls=%async_computation.3 | async-start | bytes 12582912 | tf_op jit(solution)/shard_map/all_to_all | solution.py:288
  680.8 143.4 %all-to-all-start.1 = ((bf16[32,42,2048]{2,1,0:T(8,128)(2,1)}), bf16[32,42,2048]{2,1,0:T(8,128)(2,1)}, u32[]{:S(2)}, u32[]{:S(2)}) async-start(bf16[32,42,2048]{2,1,0:T(8,128)(2,1)} %reshape.364), calls=%async_computation.1 | async-start | bytes 12582912 | tf_op jit(solution)/shard_map/all_to_all | solution.py:236
  684.5 269.7 %reduce-scatter.7.cloned.1.call-start = ((), (), s32[]{:S(2)}) async-start(), calls=%async_computation.14 | async-start | bytes 1310720 | tf_op jit(solution)/shard_map/reduce_scatter | solution.py:375
  704.9 5.1 copy-start.10
  844.6 6.6 copy-start.27
  852.4 11.8 copy-start.7
  868.4 3.2 copy-start.6
  876.2 2.5 copy-start.18
  876.2 2.5 copy-start.22
  886.3 67.8 %copy-start.33 = (f32[128,128]{0,1:T(8,128)S(1)}, f32[128,128]{0,1:T(8,128)}, u32[]{:S(2)}) copy-start(f32[128,128]{0,1:T(8,128)} %copy-done.32) | copy-start | bytes 196612
  886.3 96.3 %reduce-scatter.9.cloned.1.call-start = ((), (), s32[]{:S(2)}) async-start(), calls=%async_computation.15 | async-start | bytes 1310720 | tf_op jit(solution)/shard_map/reduce_scatter | solution.py:378
  886.4 68.8 %copy-start.26 = (f32[128,4,128]{0,2,1:T(8,128)S(1)}, f32[128,4,128]{0,2,1:T(8,128)}, u32[]{:S(2)}) copy-start(f32[128,4,128]{0,2,1:T(8,128)} %copy-done.25) | copy-start | bytes 786436
  886.4 68.8 %copy-start.31 = (f32[128,128]{0,1:T(8,128)S(1)}, f32[128,128]{0,1:T(8,128)}, u32[]{:S(2)}) copy-start(f32[128,128]{0,1:T(8,128)} %copy-done.30) | copy-start | bytes 196612
  886.4 68.8 %copy-start.49 = (f32[128,4]{0,1:T(4,128)S(1)}, f32[128,4]{0,1:T(4,128)}, u32[]{:S(2)}) copy-start(f32[128,4]{0,1:T(4,128)} %copy-done.48) | copy-start | bytes 6148
  886.4 68.8 %copy-start.57 = (f32[128]{0:T(128)S(1)}, f32[128]{0:T(128)}, u32[]{:S(2)}) copy-start(f32[128]{0:T(128)} %copy-done.56) | copy-start | bytes 1540
  888.7 67.7 %copy-start.4 = (bf16[1,128,2048]{2,1,0:T(8,128)(2,1)S(1)}, bf16[1,128,2048]{2,1,0:T(8,128)(2,1)}, u32[]{:S(2)}) copy-start(bf16[1,128,2048]{2,1,0:T(8,128)(2,1)} %param.25) | copy-start | bytes 1572868
  888.7 67.7 %copy-start.36 = (f32[8,1,256]{2,1,0:T(1,128)S(1)}, f32[8,1,256]{2,1,0:T(1,128)}, u32[]{:S(2)}) copy-start(f32[8,1,256]{2,1,0:T(1,128)} %copy-done.35) | copy-start | bytes 24580
  888.7 67.7 %copy-start.52 = (f32[128]{0:T(128)S(1)}, f32[128]{0:T(128)}, u32[]{:S(2)}) copy-start(f32[128]{0:T(128)} %copy-done.51) | copy-start | bytes 1540
  888.7 147.6 %reduce-scatter.13.cloned.1.call-start = ((), (), s32[]{:S(2)}) async-start(), calls=%async_computation.17 | async-start | bytes 4718592 | tf_op jit(solution)/shard_map/reduce_scatter | solution.py:423
  959.3 132.1 %reduce-scatter.15.cloned.1.call-start = ((), (), s32[]{:S(2)}) async-start(), calls=%async_computation.18 | async-start | bytes 4718592 | tf_op jit(solution)/shard_map/reduce_scatter | solution.py:424
  986.5 314.0 %reduce-scatter.11.cloned.1.call-start = ((), (), s32[]{:S(2)}) async-start(), calls=%async_computation.16 | async-start | bytes 37748736 | tf_op jit(solution)/shard_map/reduce_scatter | solution.py:422
  990.1 2.4 copy-start.5
  1009.4 500.1 %reduce-scatter.17.cloned.1.call-start = ((), (), s32[]{:S(2)}) async-start(), calls=%async_computation.19 | async-start | bytes 37748736 | tf_op jit(solution)/shard_map/reduce_scatter | solution.py:427
  1024.4 812.9 %all-reduce.12.cloned.1.call-start = ((), (), s32[]{:S(2)}) async-start(), calls=%async_computation.20 | async-start | bytes 18874368 | tf_op jit(solution)/shard_map/psum | solution.py:430
  1510.8 9.8 copy-start.71
  1510.8 19.5 %slice-start.2 = ((s8[5505024]{0:T(1024)(128)(4,1)}), s8[4194304]{0:T(1024)(128)(4,1)S(1)}, s32[]{:S(2)}) async-start(s8[5505024]{0:T(1024)(128)(4,1)} %bitcast.374), calls=%async_computation.23 | async-start | bytes 8388608
  1520.6 9.7 slice-start.3
  1520.6 9.7 copy-start.68
  1530.3 7.1 copy-start.13
  1549.9 2.9 copy-start.29
  1549.9 2.9 copy-start.34
  1837.3 4.8 copy-start.38
  1837.3 5.6 copy-start.37
  1837.3 6.4 copy-start.24
  1843.7 3.4 copy-start.1
  (15 other events, 21.1 us)
Sparse Core Ops, SparseCore 0:
  9.9 30.5 all-gather.6
  42.4 52.5 all-gather.10
  96.8 129.3 all-gather.8
  228.0 87.8 all-gather.12
  886.5 67.6 reduce-scatter.6
  956.9 25.7 reduce-scatter.8
  986.6 49.6 reduce-scatter.12
  1040.2 51.1 reduce-scatter.14
  1095.0 205.4 reduce-scatter.10
  1303.9 205.4 reduce-scatter.16
  1512.3 324.9 all-reduce.11
where the time goes:
time: 1870 us; the launch traced here: 1850 us
  waiting for transfers between devices  1220 us (65%)
  blocking collectives  198 us (11%)
  matrix products  190 us (10%)
  local copies, waits for them, and re-layouts  146 us (8%)
  other arithmetic  59.3 us (3%)
  starting transfers between devices  20.9 us (1%)
    psum x1, waiting for transfers between devices, per_device(): lax.psum((owner_parts[0], owner_parts[1], owner_parts[2], owner_parts[3],...  244 us
    reduce_scatter x1, waiting for transfers between devices, per_device(): lax.psum_scatter(grad_wq, 'exp', scatter_dimension=0, tiled=True)  209 us
    reduce_scatter x1, waiting for transfers between devices, per_device(): lax.psum_scatter(grad_wout, 'exp', scatter_dimension=0, tiled=True)  209 us
    all_to_all x1, waiting for transfers between devices, per_device(): lax.all_to_all(outbound, ('ctx', 'exp'), split_axis=0, concat_axis=0, til...  132 us
    all_to_all x1, waiting for transfers between devices, per_device(): lax.all_to_all(grad_expert_in, ('ctx', 'exp'), split_axis=0, concat_axis=...  124 us
    all_to_all x1, waiting for transfers between devices, per_device(): lax.all_to_all(expert_out, ('ctx', 'exp'), split_axis=0, concat_axis=0, t...  113 us
    reduce_scatter x1, waiting for transfers between devices, per_device(): lax.psum_scatter(jnp.concatenate(key_terms, axis=0), 'ctx', scatter_dimen...  65 us
    reduce_scatter x1, waiting for transfers between devices, per_device(): lax.psum_scatter(grad_wv, 'exp', scatter_dimension=0, tiled=True)  55.1 us
  transfers between devices with their start and end apart: 15, of which 11 were waited for; matrix products, arithmetic and copies ran while one was open for 14% of the time, Pallas kernels for 0%

commit v1 on v0

v1 whole, which is shorter than its diff:
```python
import jax
import jax.numpy as jnp
from jax import lax
from jax.sharding import PartitionSpec as P

KEY_VALUE_HEADS = 4
HEAD_SIZE = 128
TOPK = 8

EPSILON = 1e-06
THETA = 1000000.0

BF = jnp.bfloat16
F32 = jnp.float32
EVERY = ("ctx", "exp")


def rms_scale(tensor):
    return lax.rsqrt(jnp.mean(tensor * tensor, axis=-1, keepdims=True) + EPSILON)


def norm_backward(cotangent, tensor, factor, weight):
    scaled = cotangent * weight
    unit_form = tensor * factor
    return factor * (scaled - unit_form * jnp.mean(scaled * unit_form, axis=-1, keepdims=True))


def rope_tables(positions):
    halfway = HEAD_SIZE // 2
    frequency = THETA ** (-(jnp.arange(halfway, dtype=F32) * (2.0 / HEAD_SIZE)))
    angles = positions.astype(F32)[:, None] * frequency[None, :]
    cosine = jnp.concatenate([jnp.cos(angles), jnp.cos(angles)], axis=-1)
    sine = jnp.concatenate([jnp.sin(angles), jnp.sin(angles)], axis=-1)
    return cosine, sine


def rotate(tensor, cosine, sine):
    halfway = tensor.shape[-1] // 2
    turned = jnp.concatenate([-tensor[..., halfway:], tensor[..., :halfway]], axis=-1)
    return tensor * cosine + turned * sine


def rotation_backward(cotangent, cosine, sine):
    halfway = cotangent.shape[-1] // 2
    sine_part = cotangent * sine
    turned = jnp.concatenate([sine_part[..., halfway:], -sine_part[..., :halfway]], axis=-1)
    return cotangent * cosine + turned


def dot(a, b, dims):
    return lax.dot_general(a, b, (dims, ((), ())), preferred_element_type=F32)


def after(value, *earlier):
    return lax.optimization_barrier((value,) + earlier)[0]


def round_up(number, multiple):
    return -(-number // multiple) * multiple


def per_device(
    hidden_in,
    expert_ids,
    gate_weights,
    attn_gain,
    w_query,
    key_projection,
    value_projection,
    query_gain,
    key_norm_gain,
    w_output,
    mlp_gain,
    w_gate,
    w_up,
    w_down,
    grad_out,
):
    length, width = hidden_in.shape[1:]
    n_ctx, n_exp = lax.axis_size("ctx"), lax.axis_size("exp")
    n_all = n_ctx * n_exp
    ctx_index = lax.axis_index("ctx")
    rows_own, query_width = w_query.shape
    heads_own = query_width // HEAD_SIZE // n_exp
    own_width = heads_own * HEAD_SIZE
    sharers = n_exp // KEY_VALUE_HEADS
    tokens = n_exp * length
    factor = HEAD_SIZE ** (-0.5)
    w_gate, w_up, w_down = w_gate[0], w_up[0], w_down[0]

    def spread_heads(kv):
        per_head = kv.reshape(rows_own, KEY_VALUE_HEADS, HEAD_SIZE)
        return jnp.repeat(per_head, sharers, axis=1)

    packed = jnp.concatenate(
        [
            w_query.reshape(rows_own, n_exp, own_width),
            spread_heads(key_projection),
            spread_heads(value_projection),
        ],
        axis=2,
    )
    packed_width = own_width + 2 * HEAD_SIZE
    packed = jnp.transpose(packed, (1, 0, 2))
    gains = jnp.concatenate([attn_gain, mlp_gain, query_gain, key_norm_gain])
    gain_rows = round_up(round_up(gains.shape[0], packed_width) // packed_width, 16)
    gains = jnp.pad(gains, (0, gain_rows * packed_width - gains.shape[0]))
    gains = jnp.broadcast_to(gains.reshape(1, gain_rows, packed_width), (n_exp, gain_rows, packed_width))
    hidden_all = lax.all_gather(hidden_in[0], "exp", axis=0, tiled=True)
    heads_in = lax.all_to_all(
        jnp.concatenate([packed, gains], axis=1), "exp", split_axis=0, concat_axis=0, tiled=True
    )
    weight_cols = heads_in[:, :rows_own].reshape(n_exp * rows_own, packed_width)
    gains = heads_in[:, rows_own:].reshape(n_exp, gain_rows * packed_width).astype(F32)
    cut = attn_gain.shape[0]
    small = query_gain.shape[0]
    first_gain = gains[:, :cut].reshape(-1)
    second_gain = gains[:, cut : 2 * cut].reshape(-1)
    q_gain = gains[:, 2 * cut : 2 * cut + small].reshape(-1)
    k_gain = gains[:, 2 * cut + small : 2 * cut + 2 * small].reshape(-1)

    hits = expert_ids[0][:, :, None] == jnp.arange(n_all, dtype=jnp.int32)[None, None, :]
    dense_gates = jnp.sum(jnp.where(hits, gate_weights[0][:, :, None], 0.0), axis=1)
    my_gates = lax.all_to_all(
        jnp.transpose(dense_gates), EVERY, split_axis=0, concat_axis=0, tiled=True
    )
    blocks = 4
    groups = n_all // blocks
    span = blocks * length
    capacity = blocks * max(2, length * TOPK * 4 // (3 * n_all))
    slots = round_up(capacity, 16)
    my_gates = my_gates.reshape(groups, span)
    chosen = my_gates > 0.0
    below = (
        jnp.arange(span, dtype=jnp.int32)[:, None] < jnp.arange(span, dtype=jnp.int32)[None, :]
    ).astype(BF)
    rank = dot(chosen.astype(BF), below, ((1,), (0,))).astype(jnp.int32)
    is_slot = chosen[:, None, :] & (
        rank[:, None, :] == jnp.arange(slots, dtype=jnp.int32)[None, :, None]
    )
    pick = is_slot.astype(BF)
    slot_gates = jnp.sum(jnp.where(is_slot, my_gates[:, None, :], 0.0), axis=2)

    def to_slots(rows):
        return lax.dot_general(
            pick, rows.reshape(groups, span, width), (((2,), (1,)), ((0,), (0,))),
            preferred_element_type=F32,
        )

    def to_tokens(rows):
        return lax.dot_general(
            pick, rows.reshape(groups, slots, width), (((1,), (1,)), ((0,), (0,))),
            preferred_element_type=F32,
        )

    positions = ctx_index * length + jnp.arange(length, dtype=jnp.int32)
    cosine, sine = rope_tables(positions)
    cos_q, sin_q = cosine[None, :, None, :], sine[None, :, None, :]
    cos_k, sin_k = cosine[None], sine[None]
    wide_all = hidden_all.astype(F32)
    normed = (wide_all * rms_scale(wide_all) * first_gain).astype(BF)
    projected = dot(normed, weight_cols, ((1,), (0,)))
    queries = projected[:, :own_width].reshape(n_exp, length, heads_own, HEAD_SIZE)
    keys_raw = projected[:, own_width : own_width + HEAD_SIZE].reshape(n_exp, length, HEAD_SIZE)
    values = projected[:, own_width + HEAD_SIZE :].astype(BF)
    query_scale, key_scale = rms_scale(queries), rms_scale(keys_raw)
    query_rot = rotate(queries * query_scale * q_gain, cos_q, sin_q).astype(BF)
    key_rot = rotate(keys_raw * key_scale * k_gain, cos_k, sin_k).astype(BF)
    key_values = jnp.concatenate([key_rot.reshape(tokens, HEAD_SIZE), values], axis=1)
    key_values = lax.all_gather(key_values, "ctx", axis=0, tiled=False)
    key_values = key_values.reshape(n_ctx, n_exp, length, 2 * HEAD_SIZE)
    key_values = jnp.transpose(key_values, (1, 0, 2, 3)).reshape(n_exp, n_ctx * length, 2 * HEAD_SIZE)
    keys_all, values_all = key_values[..., :HEAD_SIZE], key_values[..., HEAD_SIZE:]

    grad_rows_all = lax.all_gather(after(grad_out[0], key_values), EVERY, axis=0, tiled=True)

    query_rows = jnp.transpose(query_rot, (0, 2, 1, 3)).reshape(n_exp, heads_own * length, HEAD_SIZE)
    key_pos = jnp.arange(n_ctx * length, dtype=jnp.int32)
    causal = key_pos[None, :] <= jnp.tile(positions, heads_own)[:, None]

    def batched(a, b, a_dim, b_dim):
        return lax.dot_general(
            a, b, (((a_dim,), (b_dim,)), ((0,), (0,))), preferred_element_type=F32
        )

    expos = jnp.where(causal, jnp.exp(batched(query_rows, keys_all, 2, 2) * factor), 0.0)
    totals = jnp.sum(expos, axis=-1, keepdims=True)
    attn_heads = (batched(expos.astype(BF), values_all, 2, 1) / totals).astype(BF)
    attn_rows = jnp.transpose(
        attn_heads.reshape(n_exp, heads_own, length, HEAD_SIZE), (0, 2, 1, 3)
    ).reshape(tokens, own_width)
    branch_part = dot(attn_rows, w_output, ((1,), (0,))).astype(BF)
    branch = lax.psum_scatter(branch_part, "exp", scatter_dimension=0, tiled=True)
    wide_in = hidden_in[0].astype(F32)
    mid = wide_in + branch.astype(F32)
    second_scale = rms_scale(mid)
    mlp_in = (mid * second_scale * second_gain).astype(BF)

    mlp_all = lax.all_gather(mlp_in, EVERY, axis=0, tiled=True)
    arrived = to_slots(mlp_all).astype(BF).reshape(groups * slots, width)
    slot_grads = (to_slots(grad_rows_all) * slot_gates[:, :, None]).astype(BF)
    slot_grads = slot_grads.reshape(groups * slots, width)
    gate_pre = dot(arrived, w_gate, ((1,), (0,)))
    up_pre = dot(arrived, w_up, ((1,), (0,)))
    sigmoid_gate = jax.nn.sigmoid(gate_pre)
    silu_gate = gate_pre * sigmoid_gate
    inner = (silu_gate * up_pre).astype(BF)
    grad_inner = dot(slot_grads, w_down, ((1,), (1,)))
    grad_gate_pre = (
        grad_inner * up_pre * sigmoid_gate * (1.0 + gate_pre * (1.0 - sigmoid_gate))
    ).astype(BF)
    grad_up_pre = (grad_inner * silu_gate).astype(BF)
    grad_expert_in = (
        dot(grad_gate_pre, w_gate, ((1,), (1,))) + dot(grad_up_pre, w_up, ((1,), (1,)))
    ).astype(BF)
    grad_mlp = lax.psum_scatter(
        to_tokens(grad_expert_in).astype(BF).reshape(n_all * length, width),
        EVERY, scatter_dimension=0, tiled=True,
    ).astype(F32)

    gradient_wide = grad_out[0].astype(F32)
    mlp_gain_part = jnp.sum(grad_mlp * mid * second_scale, axis=0)
    grad_mid = gradient_wide + norm_backward(grad_mlp, mid, second_scale, second_gain)
    branch_all = lax.all_gather(grad_mid.astype(BF), "exp", axis=0, tiled=True)

    expert_out = dot(inner, w_down, ((1,), (0,))).astype(BF)
    mixed_part = (to_tokens(expert_out) * my_gates[:, :, None]).astype(BF)
    mixed_part = mixed_part.reshape(n_all * length, width)
    mixed = lax.psum_scatter(
        after(mixed_part, branch_all), EVERY, scatter_dimension=0, tiled=True
    ).astype(F32)
    hidden_out = (mid + mixed).astype(BF)
    grad_down = dot(inner, slot_grads, ((0,), (0,)))
    grad_gate_mat = dot(arrived, grad_gate_pre, ((0,), (0,)))
    grad_up_mat = dot(arrived, grad_up_pre, ((0,), (0,)))

    grad_wout = dot(attn_rows, branch_all, ((0,), (0,))).astype(BF)
    attn_grad = dot(branch_all, w_output, ((1,), (1,))).astype(BF)
    grad_heads = jnp.transpose(
        attn_grad.reshape(n_exp, length, heads_own, HEAD_SIZE), (0, 2, 1, 3)
    ).reshape(n_exp, heads_own * length, HEAD_SIZE)
    deltas = jnp.sum(grad_heads.astype(F32) * attn_heads.astype(F32), axis=-1, keepdims=True)
    probs = jnp.where(causal, jnp.exp(batched(query_rows, keys_all, 2, 2) * factor), 0.0) / totals
    grad_scores = (
        probs * (batched(grad_heads, values_all, 2, 2) - deltas) * factor
    ).astype(BF)
    value_part = batched(probs.astype(BF), grad_heads, 1, 1)
    key_part = batched(grad_scores, query_rows, 1, 1)
    kv_part = jnp.concatenate([key_part, value_part], axis=-1).astype(BF)
    kv_part = jnp.transpose(
        kv_part.reshape(n_exp, n_ctx, length, 2 * HEAD_SIZE), (1, 0, 2, 3)
    ).reshape(n_ctx * tokens, 2 * HEAD_SIZE)
    kv_sums = lax.psum_scatter(kv_part, "ctx", scatter_dimension=0, tiled=True).astype(F32)
    grad_query_rot = batched(grad_scores, keys_all, 2, 1)
    grad_query_unit = rotation_backward(
        jnp.transpose(
            grad_query_rot.reshape(n_exp, heads_own, length, HEAD_SIZE), (0, 2, 1, 3)
        ), cos_q, sin_q,
    )
    q_gain_part = jnp.sum(grad_query_unit * queries * query_scale, axis=(0, 1, 2))
    grad_query_rows = norm_backward(grad_query_unit, queries, query_scale, q_gain).astype(BF)
    grad_query_rows = grad_query_rows.reshape(tokens, own_width)
    grad_key_unit = rotation_backward(
        kv_sums[:, :HEAD_SIZE].reshape(n_exp, length, HEAD_SIZE), cos_k, sin_k
    )
    k_gain_part = jnp.sum(grad_key_unit * keys_raw * key_scale, axis=(0, 1))
    grad_key_rows = norm_backward(grad_key_unit, keys_raw, key_scale, k_gain).astype(BF)
    grad_heads_in = jnp.concatenate(
        [
            grad_query_rows,
            grad_key_rows.reshape(tokens, HEAD_SIZE),
            kv_sums[:, HEAD_SIZE:].astype(BF),
        ],
        axis=1,
    )
    normed_part = dot(grad_heads_in, weight_cols, ((1,), (1,))).astype(BF)
    grad_normed = lax.psum_scatter(normed_part, "exp", scatter_dimension=0, tiled=True)
    first_scale = rms_scale(wide_in)
    grad_normed = grad_normed.astype(F32)
    attn_gain_part = jnp.sum(grad_normed * wide_in * first_scale, axis=0)
    grad_in = grad_mid + norm_backward(grad_normed, wide_in, first_scale, first_gain)

    wout_sum = lax.psum_scatter(grad_wout, "ctx", scatter_dimension=0, tiled=True)
    wout_sum = lax.all_gather(wout_sum, "ctx", axis=0, tiled=True).astype(F32)
    grad_cols = dot(normed, grad_heads_in, ((0,), (0,))).astype(BF)
    part_rows = rows_own // n_ctx
    grad_cols = grad_cols.reshape(n_exp, n_ctx, part_rows, packed_width)
    grad_cols = jnp.transpose(grad_cols, (1, 0, 2, 3))
    grad_cols = lax.psum_scatter(
        grad_cols.reshape(n_ctx * n_exp * part_rows, packed_width),
        "ctx", scatter_dimension=0, tiled=True,
    ).reshape(n_exp, part_rows, packed_width)
    grad_cols = lax.all_to_all(grad_cols, "exp", split_axis=0, concat_axis=0, tiled=True)
    to_row = jnp.transpose(grad_cols, (1, 0, 2))

    def join_heads(kv):
        kv = kv.reshape(part_rows, KEY_VALUE_HEADS, sharers, HEAD_SIZE).astype(F32)
        return jnp.sum(kv, axis=2).astype(BF).reshape(part_rows, KEY_VALUE_HEADS * HEAD_SIZE)

    weight_rows = jnp.concatenate(
        [
            to_row[:, :, :own_width].reshape(part_rows, query_width),
            join_heads(to_row[:, :, own_width : own_width + HEAD_SIZE]),
            join_heads(to_row[:, :, own_width + HEAD_SIZE :]),
        ],
        axis=1,
    )
    weight_rows = lax.all_gather(weight_rows, "ctx", axis=0, tiled=True).astype(F32)
    kv_width = KEY_VALUE_HEADS * HEAD_SIZE
    grad_wq = weight_rows[:, :query_width]
    grad_wk = weight_rows[:, query_width : query_width + kv_width]
    grad_wv = weight_rows[:, query_width + kv_width :]

    parts = jnp.concatenate([attn_gain_part, mlp_gain_part, q_gain_part, k_gain_part])
    parts = lax.psum(parts, EVERY)
    exp_index = lax.axis_index("exp")

    def own(start, count):
        return lax.dynamic_slice(parts, (start + exp_index * count,), (count,))

    return (
        hidden_out[None],
        grad_in[None],
        own(0, cut),
        grad_wq,
        grad_wk,
        grad_wv,
        own(2 * width, small),
        own(2 * width + HEAD_SIZE, small),
        wout_sum,
        own(width, cut),
        grad_gate_mat[None],
        grad_up_mat[None],
        grad_down[None],
    )


def solution(mesh):
    rows = P("exp", "ctx", None)
    shard, matrix, expert = P("exp"), P("exp", None), P(("ctx", "exp"), None, None)
    in_specs = (
        rows, rows, rows, shard, matrix, matrix, matrix, shard, shard, matrix, shard,
        expert, expert, expert, rows,
    )
    out_specs = (
        rows, rows, shard, matrix, matrix, matrix, shard, shard, matrix, shard,
        expert, expert, expert,
    )
    return jax.shard_map(
        per_device, mesh=mesh, in_specs=in_specs, out_specs=out_specs, check_vma=False
    )
```

time: 1870 us -> 1270 us (0.68)
  waiting for transfers between devices: 1220 us -> 886 us
  blocking collectives: 198 us -> 70.7 us
  local copies, waits for them, and re-layouts: 146 us -> 49.6 us
    all_to_all x4 -> x1, waiting for transfers between devices: 369 us -> 50.7 us  [per_device(): lax.all_to_all(jnp.concatenate([packed, gains], axis=1), 'exp', split_axi...]
    all_gather x4 -> x7, waiting for transfers between devices: 33.6 us -> 282 us  [the longest x1 103 us: per_device(): mlp_all = lax.all_gather(mlp_in, EVERY, axis=0, tiled=True)]
    psum x1 -> x0, waiting for transfers between devices: 244 us -> none  [per_device(): lax.psum((owner_parts[0], owner_parts[1], owner_parts[2], owner_parts[3],...]
    all_gather x4 -> x0, blocking collectives: 140 us -> none  [the longest x1 54.6 us: per_device(): key_portion = lax.all_gather(key_row_block, 'ctx', axis=0, tiled=True)]
    reshape x10 -> x11, local copies, waits for them, and re-layouts: 67 us -> 12.9 us  [the longest x2 3.76 us: per_device(): attn_grad.reshape(n_exp, length, heads_own, HEAD_SIZE)]
    unnamed x2 -> x0, blocking collectives: 44.9 us -> none
    psum x1, blocking collectives: 12.8 us -> 42.7 us  [per_device(): parts = lax.psum(parts, EVERY)]
    all_to_all x0 -> x2, blocking collectives: none -> 28 us  [the longest x1 16.2 us: per_device(): lax.all_to_all(grad_cols, 'exp', split_axis=0, concat_axis=0, tiled=True)]
  transfers between devices with their start and end apart: 15 -> 15, of which waited for: 11 -> 13; matrix products, arithmetic and copies ran while one was open for 14% -> 13% of each run, Pallas kernels for 0% -> 0%
where the time goes in v1:
time: 1270 us; the launch traced here: 1260 us
  waiting for transfers between devices  886 us (70%)
  matrix products  174 us (14%)
  blocking collectives  70.7 us (6%)
  other arithmetic  58.3 us (5%)
  local copies, waits for them, and re-layouts  49.6 us (4%)
  between operations  15.3 us (1%)
    reduce_scatter x1, waiting for transfers between devices, per_device(): lax.psum_scatter(to_tokens(grad_expert_in).astype(BF).reshape(n_all * len...  181 us
    reduce_scatter x1, waiting for transfers between devices, per_device(): lax.psum_scatter(after(mixed_part, branch_all), EVERY, scatter_dimension=...  178 us
    dot_general x16, matrix products, dot(): return lax.dot_general(a, b, (dims, ((), ())), preferred_element_type=F32)  114 us
    all_gather x1, waiting for transfers between devices, per_device(): mlp_all = lax.all_gather(mlp_in, EVERY, axis=0, tiled=True)  103 us
    all_gather x1, waiting for transfers between devices, per_device(): lax.all_gather(after(grad_out[0], key_values), EVERY, axis=0, tiled=True)  99.3 us
    reduce_scatter x1, waiting for transfers between devices, per_device(): lax.psum_scatter(grad_cols.reshape(n_ctx * n_exp * part_rows, packed_widt...  54.4 us
    all_to_all x1, waiting for transfers between devices, per_device(): lax.all_to_all(jnp.concatenate([packed, gains], axis=1), 'exp', split_axi...  50.7 us
    reduce_scatter x1, waiting for transfers between devices, per_device(): lax.psum_scatter(branch_part, 'exp', scatter_dimension=0, tiled=True)  49.5 us
  transfers between devices with their start and end apart: 15, of which 13 were waited for; matrix products, arithmetic and copies ran while one was open for 13% of the time, Pallas kernels for 0%

profile of v1, /device:TPU:0, one launch (start us, length us, event | category | flops | bytes accessed | tf_op | source)
XLA Modules:
  0.0 1261.1 jit_solution(13859836603724020803)
XLA Ops:
  8.0 4.2 copy.138
  18.1 2.8 pad_maximum_fusion
  20.9 6.3 copy.142
  27.2 5.2 all-to-all-start
  33.0 50.7 %all-to-all-done = bf16[8,272,768]{2,1,0:T(8,128)(2,1)} async-done(((bf16[8,272,768]{2,1,0:T(8,128)(2,1)}), bf16[8,272,768]{2,1,0:T(8,128)(2,1)}, u32[]{:S(2)}, u32[]{:S(2)}) %all-to-all-start) | async-done | bytes 3342368 | tf_op jit(solution)/shard_map/all_to_all | solution.py:110
  85.6 3.8 slice.116
  89.4 3.2 fusion
  92.8 5.3 fusion.49
  101.2 3.1 slice.117
  104.3 2.9 reshape.288
  107.2 3.1 multiply_reduce_fusion.3
  113.0 2.5 fusion.65
  116.8 29.7 %all-gather.22.cloned.1.call-done = bf16[4096,256]{1,0:T(8,128)(2,1)} async-done(((bf16[1024,256]{1,0:T(8,128)(2,1)}), bf16[4096,256]{1,0:T(8,128)(2,1)}) %all-gather.22.cloned.1.call-update) | async-done | bytes 2097168 | tf_op jit(solution)/shard_map/all_gather | solution.py:170
  148.3 2.4 fusion.4
  150.7 3.7 divide_convert_fusion
  154.4 2.4 copy.146
  156.8 6.3 convolution_convert_fusion.3
  163.8 49.5 %reduce-scatter.8.cloned.1.call-done = bf16[128,2048]{1,0:T(8,128)(2,1)} async-done(((bf16[1024,2048]{1,0:T(8,128)(2,1)}), bf16[128,2048]{1,0:T(8,128)(2,1)}) %reduce-scatter.8.cloned.1.call-update) | async-done | bytes 524304 | tf_op jit(solution)/shard_map/reduce_scatter | solution.py:193
  214.7 2.2 multiply_convert_fusion.7
  217.0 11.9 all_to_all.19
  231.0 99.3 %all-gather.12.cloned.1.call-done = bf16[4096,2048]{1,0:T(8,128)(2,1)} async-done(((bf16[128,2048]{1,0:T(8,128)(2,1)}), bf16[4096,2048]{1,0:T(8,128)(2,1)}) %all-gather.12.cloned.1.call-update) | async-done | bytes 16777232 | tf_op jit(solution)/shard_map/all_gather | solution.py:175
  330.3 13.2 %multiply_convert_fusion.1 = bf16[8,176,2048]{2,1,0:T(8,128)(2,1)} fusion(f32[8,176]{1,0:T(8,128)S(1)} %select_reduce_fusion, bf16[8,512,2048]{2,1,0:T(8,128)(2,1)} %bitcast.203, s32[8,512]{1,0:T(8,128)S(1)} %convolution_convert_fusion.9, pred[8,512]{1,0:T(8,128)(4,1)S(1)} %broadcast_compare_fusion), kind=kOutput, calls=%fused_computation.3 | convolution fusion | flops 2959998976 | bytes 22570496 | tf_op jit(solution)/shard_map/dot_general | solution.py:145
  343.5 102.7 %all-gather.10.cloned.1.call-done = bf16[4096,2048]{1,0:T(8,128)(2,1)} async-done(((bf16[128,2048]{1,0:T(8,128)(2,1)}), bf16[4096,2048]{1,0:T(8,128)(2,1)}) %all-gather.10.cloned.1.call-update) | async-done | bytes 16777232 | tf_op jit(solution)/shard_map/all_gather | solution.py:199
  446.2 8.9 convolution_convert_fusion.2
  455.2 10.2 fusion.18
  465.3 6.2 fusion.22
  471.5 10.2 multiply_convert_fusion.3
  481.7 7.3 fusion.20
  489.1 10.6 add_convert_fusion
  499.7 8.2 convolution_convert_fusion
  507.9 181.2 %reduce-scatter.10.cloned.1.call-done = bf16[128,2048]{1,0:T(8,128)(2,1)} async-done(((bf16[4096,2048]{1,0:T(8,128)(2,1)}), bf16[128,2048]{1,0:T(8,128)(2,1)}) %reduce-scatter.10.cloned.1.call-update) | async-done | bytes 524304 | tf_op jit(solution)/shard_map/reduce_scatter | solution.py:216
  689.1 2.0 fusion.59
  691.2 2.8 fusion.97
  694.2 38.2 %all-gather.14.cloned.1.call-done = bf16[1024,2048]{1,0:T(8,128)(2,1)} async-done(((bf16[128,2048]{1,0:T(8,128)(2,1)}), bf16[1024,2048]{1,0:T(8,128)(2,1)}) %all-gather.14.cloned.1.call-update) | async-done | bytes 4194320 | tf_op jit(solution)/shard_map/all_gather | solution.py:224
  732.4 6.2 convolution_convert_fusion.8
  738.6 2.1 reshape.304
  742.4 1.9 multiply_reduce_fusion.2
  744.3 5.5 fusion.32
  749.8 3.0 multiply_convert_fusion.2
  756.7 5.5 fusion.70
  762.1 3.8 convolution_convert_fusion.6
  766.2 3.0 multiply_bitcast_fusion
  771.5 4.3 multiply_reduce_fusion
  775.9 2.7 multiply_convert_fusion.6
  779.8 20.6 %reduce-scatter.14.cloned.1.call-done = bf16[1024,256]{1,0:T(8,128)(2,1)} async-done(((bf16[4096,256]{1,0:T(8,128)(2,1)}), bf16[1024,256]{1,0:T(8,128)(2,1)}) %reduce-scatter.14.cloned.1.call-update) | async-done | bytes 524304 | tf_op jit(solution)/shard_map/reduce_scatter | solution.py:253
  805.1 4.4 convolution_convert_fusion.5
  809.5 1.9 copy.155
  811.4 34.1 %reduce-scatter.20.cloned.1.call-done = bf16[128,2048]{1,0:T(8,128)(2,1)} async-done(((bf16[512,2048]{1,0:T(8,128)(2,1)}), bf16[128,2048]{1,0:T(8,128)(2,1)}) %reduce-scatter.20.cloned.1.call-update) | async-done | bytes 524304 | tf_op jit(solution)/shard_map/reduce_scatter | solution.py:283
  845.6 7.8 convolution_convert_fusion.4
  853.5 54.4 %reduce-scatter.18.cloned.1.call-done = bf16[512,768]{1,0:T(8,128)(2,1)} async-done(((bf16[2048,768]{1,0:T(8,128)(2,1)}), bf16[512,768]{1,0:T(8,128)(2,1)}) %reduce-scatter.18.cloned.1.call-update) | async-done | bytes 786448 | tf_op jit(solution)/shard_map/reduce_scatter | solution.py:289
  907.9 16.2 %all_to_all.20 = bf16[8,64,768]{2,1,0:T(8,128)(2,1)S(1)} all-to-all(bf16[8,64,768]{2,1,0:T(8,128)(2,1)} %bitcast.251), channel_id=1, replica_groups=mesh['ctx'=4,'exp'=8] {'exp'}, dimensions={0} | all-to-all | bytes 1572864 | tf_op jit(solution)/shard_map/all_to_all | solution.py:293
  925.6 6.5 convolution_convert_fusion.1
  932.1 8.5 multiply_convert_fusion
  940.7 9.7 convolution_bitcast_fusion.1
  950.4 9.7 convolution_bitcast_fusion.2
  960.1 9.8 convolution_bitcast_fusion
  970.0 4.2 convert_element_type.183
  974.2 34.6 %reduce-scatter.16.cloned.1.call-done = bf16[128,2048]{1,0:T(8,128)(2,1)} async-done(((bf16[1024,2048]{1,0:T(8,128)(2,1)}), bf16[128,2048]{1,0:T(8,128)(2,1)}) %reduce-scatter.16.cloned.1.call-update) | async-done | bytes 524304 | tf_op jit(solution)/shard_map/reduce_scatter | solution.py:277
  1010.5 42.7 %psum.7 = f32[4352]{0:T(1024)S(1)} all-reduce(f32[4352]{0:T(1024)S(1)} %pad_maximum_fusion.9), channel_id=1, replica_groups=mesh['ctx'=4,'exp'=8] {'ctx','exp'}, use_global_device_ids=true, to_apply=%region_22.23 | all-reduce | flops 4352 | bytes 34816 | tf_op jit(solution)/shard_map/psum | solution.py:315
  1054.5 12.1 all-gather.16.cloned.1.call-done
  1066.6 4.1 slice.138
  1070.7 2.1 fusion.99
  1072.9 177.7 %reduce-scatter.12.cloned.1.call-done = bf16[128,2048]{1,0:T(8,128)(2,1)} async-done(((bf16[4096,2048]{1,0:T(8,128)(2,1)}), bf16[128,2048]{1,0:T(8,128)(2,1)}) %reduce-scatter.12.cloned.1.call-update) | async-done | bytes 524304 | tf_op jit(solution)/shard_map/reduce_scatter | solution.py:229
  1250.6 3.8 fusion.54
  (214 shorter events, 40.8 us)
Async XLA Ops:
  7.2 464.3 %copy-start = (bf16[1,768,2048]{2,1,0:T(8,128)(2,1)S(1)}, bf16[1,768,2048]{2,1,0:T(8,128)(2,1)}, u32[]{:S(2)}) copy-start(bf16[1,768,2048]{2,1,0:T(8,128)(2,1)} %param.28) | copy-start | bytes 9437188
  7.2 5.0 copy-start.23
  7.2 6.9 copy-start.44
  7.2 6.9 copy-start.42
  7.2 6.9 copy-start.41
  7.2 6.9 copy-start.43
  7.2 82.1 %all-gather.20.cloned.1.call-start = ((), (), s32[]{:S(2)}) async-start(), calls=%async_computation.22 | async-start | bytes 4718592 | tf_op jit(solution)/shard_map/all_gather | solution.py:109
  27.2 56.4 %all-to-all-start = ((bf16[8,272,768]{2,1,0:T(8,128)(2,1)}), bf16[8,272,768]{2,1,0:T(8,128)(2,1)}, u32[]{:S(2)}, u32[]{:S(2)}) async-start(bf16[8,272,768]{2,1,0:T(8,128)(2,1)} %copy.142), calls=%async_computation | async-start | bytes 6684672 | tf_op jit(solution)/shard_map/all_to_all | solution.py:110
  32.4 114.1 %all-gather.22.cloned.1.call-start = ((), (), s32[]{:S(2)}) async-start(), calls=%async_computation.23 | async-start | bytes 2621440 | tf_op jit(solution)/shard_map/all_gather | solution.py:170
  32.9 80.1 %copy-start.13 = (f32[128,128]{1,0:T(8,128)}, f32[128,128]{1,0:T(8,128)S(1)}, u32[]{:S(2)}) copy-start(f32[128,128]{1,0:T(8,128)S(1)} %pad_maximum_fusion.7) | copy-start | bytes 196612
  84.9 7.7 copy-start.28
  85.6 13.3 %copy-start.33 = (f32[128]{0:T(128)}, f32[128]{0:T(128)S(1)}, u32[]{:S(2)}) copy-start(f32[128]{0:T(128)S(1)} %mul.441) | copy-start | bytes 1540
  89.4 3.4 copy-start.11
  92.6 5.6 copy-start.37
  98.5 2.3 copy-start.30
  98.7 2.5 copy-start.32
  100.7 112.5 %reduce-scatter.8.cloned.1.call-start = ((), (), s32[]{:S(2)}) async-start(), calls=%async_computation.10 | async-start | bytes 4718592 | tf_op jit(solution)/shard_map/reduce_scatter | solution.py:193
  101.1 49.6 %copy-start.24 = (pred[512,512]{0,1:T(8,128)(4,1)}, pred[512,512]{0,1:T(8,128)(4,1)S(1)}, u32[]{:S(2)}) copy-start(pred[512,512]{0,1:T(8,128)(4,1)S(1)} %iota_compare_fusion.2) | copy-start | bytes 786436
  101.2 11.8 copy-start.35
  107.2 3.2 copy-start.1
  110.4 2.6 copy-start.4
  148.3 2.4 copy-start.8
  150.7 3.7 copy-start.47
  163.1 53.9 %copy-start.39 = (f32[1,128,8]{1,2,0:T(8,128)S(1)}, f32[1,128,8]{1,2,0:T(8,128)}, u32[]{:S(2)}) copy-start(f32[1,128,8]{1,2,0:T(8,128)} %param.17) | copy-start | bytes 12292
  163.1 53.9 %copy-start.40 = (s32[1,128,8]{1,2,0:T(8,128)S(1)}, s32[1,128,8]{1,2,0:T(8,128)}, u32[]{:S(2)}) copy-start(s32[1,128,8]{1,2,0:T(8,128)} %param.16) | copy-start | bytes 12292
  163.1 167.2 %all-gather.12.cloned.1.call-start = ((), (), s32[]{:S(2)}) async-start(), calls=%async_computation.12 | async-start | bytes 17301504 | tf_op jit(solution)/shard_map/all_gather | solution.py:175
  163.7 282.5 %all-gather.10.cloned.1.call-start = ((), (), s32[]{:S(2)}) async-start(), calls=%async_computation.11 | async-start | bytes 17301504 | tf_op jit(solution)/shard_map/all_gather | solution.py:199
  217.0 472.2 %reduce-scatter.10.cloned.1.call-start = ((), (), s32[]{:S(2)}) async-start(), calls=%async_computation.13 | async-start | bytes 17301504 | tf_op jit(solution)/shard_map/reduce_scatter | solution.py:216
  230.1 113.4 %copy-start.26 = (f32[8,512]{1,0:T(8,128)}, f32[8,512]{1,0:T(8,128)S(1)}, u32[]{:S(2)}) copy-start(f32[8,512]{1,0:T(8,128)S(1)} %reshape.295) | copy-start | bytes 49156
  455.1 10.2 copy-start.6
  455.1 10.2 copy-start.46
  455.2 16.3 %slice-start = ((s8[5767168]{0:T(1024)(128)(4,1)}), s8[4194304]{0:T(1024)(128)(4,1)S(1)}, s32[]{:S(2)}) async-start(s8[5767168]{0:T(1024)(128)(4,1)} %bitcast.214), calls=%async_computation.24 | async-start | bytes 8388608
  465.3 6.2 slice-start.1
  481.7 7.4 copy-start.49
  507.9 224.6 %all-gather.14.cloned.1.call-start = ((), (), s32[]{:S(2)}) async-start(), calls=%async_computation.14 | async-start | bytes 4718592 | tf_op jit(solution)/shard_map/all_gather | solution.py:224
  694.0 106.4 %reduce-scatter.14.cloned.1.call-start = ((), (), s32[]{:S(2)}) async-start(), calls=%async_computation.16 | async-start | bytes 2621440 | tf_op jit(solution)/shard_map/reduce_scatter | solution.py:253
  740.8 3.5 copy-start.25
  740.8 9.0 slice-start.2
  744.3 5.5 copy-start.9
  744.3 5.5 slice-start.3
  749.8 3.0 copy-start.18
  756.6 88.9 %reduce-scatter.20.cloned.1.call-start = ((), (), s32[]{:S(2)}) async-start(), calls=%async_computation.20 | async-start | bytes 2621440 | tf_op jit(solution)/shard_map/reduce_scatter | solution.py:283
  756.6 5.5 copy-start.16
  756.6 5.5 copy-start.45
  765.9 142.0 %reduce-scatter.18.cloned.1.call-start = ((), (), s32[]{:S(2)}) async-start(), calls=%async_computation.18 | async-start | bytes 3932160 | tf_op jit(solution)/shard_map/reduce_scatter | solution.py:289
  769.1 2.2 copy-start.3
  769.2 2.3 copy-start.5
  769.2 2.3 copy-start.14
  769.2 2.3 copy-start.36
  778.6 23.3 %copy-start.31 = (f32[1024]{0:T(1024)S(1)}, f32[1024]{0:T(1024)}, u32[]{:S(2)}) copy-start(f32[1024]{0:T(1024)} %copy-done.30) | copy-start | bytes 12292
  778.6 23.3 %copy-start.34 = (f32[128]{0:T(128)S(1)}, f32[128]{0:T(128)}, u32[]{:S(2)}) copy-start(f32[128]{0:T(128)} %copy-done.33) | copy-start | bytes 1540
  801.5 3.5 copy-start.21
  801.6 3.4 copy-start.12
  801.6 3.4 copy-start.19
  801.6 3.4 copy-start.29
  801.6 3.4 copy-start.38
  805.0 4.4 copy-start.22
  811.3 158.6 %all-gather.18.cloned.1.call-start = ((), (), s32[]{:S(2)}) async-start(), calls=%async_computation.21 | async-start | bytes 2621440 | tf_op jit(solution)/shard_map/all_gather | solution.py:284
  845.6 163.3 %reduce-scatter.16.cloned.1.call-start = ((), (), s32[]{:S(2)}) async-start(), calls=%async_computation.17 | async-start | bytes 4718592 | tf_op jit(solution)/shard_map/reduce_scatter | solution.py:277
  853.5 213.2 %all-gather.16.cloned.1.call-start = ((), (), s32[]{:S(2)}) async-start(), calls=%async_computation.19 | async-start | bytes 3276800 | tf_op jit(solution)/shard_map/all_gather | solution.py:308
  925.1 325.4 %reduce-scatter.12.cloned.1.call-start = ((), (), s32[]{:S(2)}) async-start(), calls=%async_computation.15 | async-start | bytes 17301504 | tf_op jit(solution)/shard_map/reduce_scatter | solution.py:229
  925.6 6.5 copy-start.27
  940.7 9.7 copy-start.50
  950.4 9.8 copy-start.48
  (6 other events, 10.4 us)
Sparse Core Ops, SparseCore 0:
  9.9 59.6 all-gather.19
  100.8 45.5 all-gather.21
  163.3 49.9 reduce-scatter.7
  216.0 114.3 all-gather.11
  333.6 112.5 all-gather.9
  508.0 181.1 reduce-scatter.9
  694.1 38.2 all-gather.13
  756.7 43.6 reduce-scatter.13
  802.7 42.8 reduce-scatter.19
  848.3 59.6 reduce-scatter.17
  909.5 45.5 all-gather.17
  958.9 49.9 reduce-scatter.15
  1011.0 55.6 all-gather.15
  1068.8 181.7 reduce-scatter.11

commit v2 on v1

v2 whole, which is shorter than its diff:
```python
import functools

import jax
import jax.numpy as jnp
from jax import lax
from jax.experimental import pallas as pl
from jax.experimental.pallas import tpu as pltpu
from jax.sharding import PartitionSpec as P


KEY_VALUE_HEADS = 4
HEAD_SIZE = 128
TOPK = 8

EPSILON = 1e-06
THETA = 1000000.0

BF = jnp.bfloat16
F32 = jnp.float32


def rms_scale(tensor):
    return lax.rsqrt(jnp.mean(tensor * tensor, axis=-1, keepdims=True) + EPSILON)


def norm_backward(cotangent, tensor, factor, weight):
    scaled = cotangent * weight
    unit_form = tensor * factor
    return factor * (scaled - unit_form * jnp.mean(scaled * unit_form, axis=-1, keepdims=True))


def rope_tables(positions):
    halfway = HEAD_SIZE // 2
    frequency = THETA ** (-(jnp.arange(halfway, dtype=F32) * (2.0 / HEAD_SIZE)))
    angles = positions.astype(F32)[:, None] * frequency[None, :]
    cosine = jnp.concatenate([jnp.cos(angles), jnp.cos(angles)], axis=-1)
    sine = jnp.concatenate([jnp.sin(angles), jnp.sin(angles)], axis=-1)
    return cosine, sine


def rotate(tensor, cosine, sine):
    halfway = tensor.shape[-1] // 2
    turned = jnp.concatenate([-tensor[..., halfway:], tensor[..., :halfway]], axis=-1)
    return tensor * cosine + turned * sine


def rotation_backward(cotangent, cosine, sine):
    halfway = cotangent.shape[-1] // 2
    sine_part = cotangent * sine
    turned = jnp.concatenate([sine_part[..., halfway:], -sine_part[..., :halfway]], axis=-1)
    return cotangent * cosine + turned


def dot(a, b, dims):
    return lax.dot_general(a, b, (dims, ((), ())), preferred_element_type=F32)


def after(value, *earlier):
    return lax.optimization_barrier((value,) + earlier)[0]


def round_up(number, multiple):
    return -(-number // multiple) * multiple


MESH = pl.DeviceIdType.MESH


def line_sum_steps(n_ctx, chunks, part, finish, line, lag=2):
    (from_left, from_right, to_right, to_left, right_send, right_recv, left_send, left_recv) = line
    ctx, last = lax.axis_index("ctx"), n_ctx - 1

    def copy_right(k):
        return pltpu.make_async_remote_copy(
            src_ref=to_right.at[k], dst_ref=from_left.at[k],
            send_sem=right_send.at[k], recv_sem=right_recv.at[k],
            device_id={"ctx": ctx + 1}, device_id_type=MESH,
        )

    def copy_left(k):
        return pltpu.make_async_remote_copy(
            src_ref=to_left.at[k], dst_ref=from_right.at[k],
            send_sem=left_send.at[k], recv_sem=left_recv.at[k],
            device_id={"ctx": ctx - 1}, device_id_type=MESH,
        )

    def step(time, carry):
        k_right = time - lag * ctx
        k_left = time - lag * (last - ctx)
        k_done = time - lag * jnp.maximum(ctx, last - ctx)

        @pl.when((k_right >= 0) & (k_right < chunks))
        def _():
            @pl.when(ctx == 0)
            def _():
                to_right[k_right] = part(k_right).astype(BF)

            @pl.when(ctx > 0)
            def _():
                copy_right(k_right).wait_recv()
                to_right[k_right] = (part(k_right) + from_left[k_right].astype(F32)).astype(BF)

            @pl.when(ctx < last)
            def _():
                copy_right(k_right).start()

        @pl.when((k_left >= 0) & (k_left < chunks))
        def _():
            @pl.when(ctx == last)
            def _():
                to_left[k_left] = part(k_left).astype(BF)

            @pl.when(ctx < last)
            def _():
                copy_left(k_left).wait_recv()
                to_left[k_left] = (part(k_left) + from_right[k_left].astype(F32)).astype(BF)

            @pl.when(ctx > 0)
            def _():
                copy_left(k_left).start()

        @pl.when((k_done >= 0) & (k_done < chunks))
        def _():
            @pl.when(ctx == last)
            def _():
                finish(k_done, to_right[k_done].astype(F32))

            @pl.when(ctx < last)
            def _():
                finish(k_done, to_right[k_done].astype(F32) + from_right[k_done].astype(F32))

        return carry

    lax.fori_loop(0, chunks + lag * last, step, 0)

    def drain(k, carry):
        @pl.when(ctx < last)
        def _():
            copy_right(k).wait_send()

        @pl.when(ctx > 0)
        def _():
            copy_left(k).wait_send()

        return carry

    lax.fori_loop(0, chunks, drain, 0)


def greet(n_line, others):
    barrier = pltpu.get_barrier_semaphore()
    for other in others:
        pl.semaphore_signal(barrier, inc=1, device_id=other, device_id_type=MESH)
    if n_line == 1:
        pl.semaphore_wait(barrier, len(others))
        return
    ctx, last = lax.axis_index("ctx"), n_line - 1

    @pl.when(ctx > 0)
    def _():
        pl.semaphore_signal(barrier, inc=1, device_id={"ctx": ctx - 1}, device_id_type=MESH)

    @pl.when(ctx < last)
    def _():
        pl.semaphore_signal(barrier, inc=1, device_id={"ctx": ctx + 1}, device_id_type=MESH)

    at_end = (ctx == 0) | (ctx == last)

    @pl.when(at_end)
    def _():
        pl.semaphore_wait(barrier, len(others) + 1)

    @pl.when(jnp.logical_not(at_end))
    def _():
        pl.semaphore_wait(barrier, len(others) + 2)


def line_buffers(chunks, rows, width):
    slots = pltpu.VMEM((chunks, rows, width), BF)
    sems = pltpu.SemaphoreType.DMA((chunks,))
    return [slots] * 4 + [sems] * 4


def line_sum_kernel(n_ctx, chunks, x_ref, out_ref, *line):
    greet(n_ctx, [])

    def finish(k, value):
        out_ref[k] = value

    line_sum_steps(n_ctx, chunks, lambda k: x_ref[k].astype(F32), finish, line)


def line_sum(x, n_ctx, chunks=16):
    total, width = x.shape
    rows = total // chunks
    out = pl.pallas_call(
        functools.partial(line_sum_kernel, n_ctx, chunks),
        out_shape=jax.ShapeDtypeStruct((chunks, rows, width), F32),
        in_specs=[pl.BlockSpec(memory_space=pltpu.VMEM)],
        out_specs=pl.BlockSpec(memory_space=pltpu.VMEM),
        scratch_shapes=line_buffers(chunks, rows, width),
        compiler_params=pltpu.CompilerParams(
            collective_id=2, has_side_effects=True, vmem_limit_bytes=40 * 1024 * 1024
        ),
    )(x.reshape(chunks, rows, width))
    return out.reshape(total, width)


def column_sum_kernel(n_ctx, n_exp, subs, x_ref, out_ref, whole, plane_send, plane_recv, own_sem, *line):
    exp = lax.axis_index("exp")
    chunks = n_exp * subs
    greet(n_ctx, [{"exp": lax.rem(exp + hop, n_exp)} for hop in range(1, n_exp)])

    def copy_plane(k):
        hop, sub = k // subs, lax.rem(k, subs)
        return pltpu.make_async_remote_copy(
            src_ref=whole.at[k], dst_ref=out_ref.at[exp, sub],
            send_sem=plane_send.at[k], recv_sem=plane_recv.at[k],
            device_id={"exp": lax.rem(exp + hop, n_exp)}, device_id_type=MESH,
        )

    def copy_own(k):
        return pltpu.make_async_copy(whole.at[k], out_ref.at[exp, k], own_sem.at[k])

    def part(k):
        owner = lax.rem(exp + k // subs, n_exp)
        return x_ref[owner * subs + lax.rem(k, subs)].astype(F32)

    def finish(k, value):
        whole[k] = value.astype(BF)

        @pl.when(k < subs)
        def _():
            copy_own(k).start()

        @pl.when(k >= subs)
        def _():
            copy_plane(k).start()

    line_sum_steps(n_ctx, chunks, part, finish, line)

    def drain(k, carry):
        @pl.when(k < subs)
        def _():
            copy_own(k).wait()

        @pl.when(k >= subs)
        def _():
            copy_plane(k).wait()

        return carry

    lax.fori_loop(0, chunks, drain, 0)


def column_sum(x, n_ctx, n_exp, subs=2):
    total, width = x.shape
    rows = total // n_exp // subs
    chunks = n_exp * subs
    sems = pltpu.SemaphoreType.DMA((chunks,))
    out = pl.pallas_call(
        functools.partial(column_sum_kernel, n_ctx, n_exp, subs),
        out_shape=jax.ShapeDtypeStruct((n_exp, subs, rows, width), BF),
        in_specs=[pl.BlockSpec(memory_space=pltpu.VMEM)],
        out_specs=pl.BlockSpec(memory_space=pltpu.VMEM),
        scratch_shapes=[
            pltpu.VMEM((chunks, rows, width), BF), sems, sems, pltpu.SemaphoreType.DMA((subs,)),
        ] + line_buffers(chunks, rows, width),
        compiler_params=pltpu.CompilerParams(
            collective_id=1, has_side_effects=True, vmem_limit_bytes=48 * 1024 * 1024
        ),
    )(x.reshape(chunks, rows, width))
    return out.reshape(n_exp, subs * rows, width)


def gather_kernel(n_line, x_ref, out_ref, *sems):
    (z_send, x_send, y_send, d_send, p_send, z_recv, x_recv, y_recv, d_recv, p_recv, own_sem) = sems
    exp = lax.axis_index("exp")
    ctx = lax.axis_index("ctx") if n_line > 1 else 0
    last = n_line - 1

    def flip(bit):
        return exp + bit - 2 * bit * lax.rem(exp // bit, 2)

    over_core, over_x, over_y = flip(1), flip(2), flip(4)
    over_both = over_x + over_y - exp
    greet(n_line, [{"exp": other} for other in (over_core, over_x, over_y)])

    def send(src, place, half, send_sem, recv_sem, device):
        return pltpu.make_async_remote_copy(
            src_ref=src, dst_ref=out_ref.at[place[0], place[1], half],
            send_sem=send_sem, recv_sem=recv_sem, device_id=device, device_id_type=MESH,
        )

    def held(block, line, half):
        return out_ref.at[block, line, half]

    def to_z(src, line, half, way):
        step = 2 * way - 1
        return send(
            src, (exp, line), half, z_send.at[way, line, half], z_recv.at[line, half],
            {"ctx": ctx + step},
        )

    def to_x(src, line, half):
        return send(src, (exp, line), half, x_send.at[line, half], x_recv.at[line, half], {"exp": over_x})

    def to_y(src, line, half):
        return send(src, (exp, line), half, y_send.at[line, half], y_recv.at[line, half], {"exp": over_y})

    def across(line, half):
        block, device = ((over_x, over_y), (over_y, over_x))[half]
        return send(
            held(block, line, half), (block, line), half, d_send.at[line, half],
            d_recv.at[line, half], {"exp": device},
        )

    blocks = (exp, over_x, over_y, over_both)

    def to_core(src, which, line, half):
        return send(
            src, (blocks[which], line), half, p_send.at[which, line, half],
            p_recv.at[which, line, half], {"exp": over_core},
        )

    def when(cond, body):
        if cond is True:
            body()
        else:
            pl.when(cond)(body)

    def own(half):
        return pltpu.make_async_copy(x_ref.at[half], held(exp, ctx, half), own_sem.at[half])

    def place(distance, way):
        line = ctx - (2 * way - 1) * distance
        return line, (True if distance == 0 else (line >= 0) & (line <= last))

    def along(distance, way):
        line, there = place(distance, way)

        def body():
            for half in (0, 1):
                src = x_ref.at[half] if distance == 0 else held(exp, line, half)
                if distance:
                    to_z(src, line, half, way).wait_recv()
                if n_line > 1:
                    for onward in (0, 1) if distance == 0 else (way,):
                        @pl.when((ctx > 0) if onward == 0 else (ctx < last))
                        def _():
                            to_z(src, line, half, onward).start()
            for half in (0, 1):
                src = [x_ref.at[h] if distance == 0 else held(exp, line, h) for h in (0, 1)]
                to_x(src[half], line, half).start()
                to_y(src[1 - half], line, 1 - half).start()
            for half in (0, 1):
                to_core(src[half], 0, line, half).start()

        when(there, body)

    def plane(distance, way):
        line, there = place(distance, way)

        def body():
            to_x(held(over_x, line, 0), line, 0).wait_recv()
            across(line, 0).start()
            to_y(held(over_y, line, 1), line, 1).wait_recv()
            across(line, 1).start()
            to_core(held(over_x, line, 0), 1, line, 0).start()
            to_core(held(over_y, line, 1), 2, line, 1).start()
            to_x(held(over_x, line, 1), line, 1).wait_recv()
            to_core(held(over_x, line, 1), 1, line, 1).start()
            to_y(held(over_y, line, 0), line, 0).wait_recv()
            to_core(held(over_y, line, 0), 2, line, 0).start()

        when(there, body)

    def corner(distance, way):
        line, there = place(distance, way)

        def body():
            for half in (0, 1):
                across(line, half).wait_recv()
                to_core(held(over_both, line, half), 3, line, half).start()

        when(there, body)

    def finish(distance, way):
        line, there = place(distance, way)

        def body():
            for half in (0, 1):
                src = x_ref.at[half] if distance == 0 else held(exp, line, half)
                for which in range(4):
                    from_core = to_core(src, which, line, half)
                    from_core.wait_recv()
                    from_core.wait_send()
                to_x(src, line, half).wait_send()
                to_y(src, line, half).wait_send()
                across(line, half).wait_send()
                if n_line > 1:
                    for onward in (0, 1) if distance == 0 else (way,):
                        @pl.when((ctx > 0) if onward == 0 else (ctx < last))
                        def _():
                            to_z(src, line, half, onward).wait_send()

        when(there, body)

    def everywhere(stage, distance):
        if 0 <= distance < n_line:
            for way in (1,) if distance == 0 else (1, 0):
                stage(distance, way)

    for half in (0, 1):
        own(half).start()
    for time in range(n_line + 2):
        everywhere(along, time)
        everywhere(plane, time - 1)
        everywhere(corner, time - 2)
    for distance in range(n_line):
        everywhere(finish, distance)
    for half in (0, 1):
        own(half).wait()


def gather_rows(x, n_line, n_exp, collective_id):
    rows, width = x.shape
    if n_exp != 8:
        if n_line > 1:
            x = lax.all_gather(x, "ctx", axis=0, tiled=True)
        return lax.all_gather(x, "exp", axis=0, tiled=False)
    dma = pltpu.SemaphoreType.DMA
    pair, four = dma((n_line, 2)), dma((4, n_line, 2))
    out = pl.pallas_call(
        functools.partial(gather_kernel, n_line),
        out_shape=jax.ShapeDtypeStruct((n_exp, n_line, 2, rows // 2, width), x.dtype),
        in_specs=[pl.BlockSpec(memory_space=pltpu.VMEM)],
        out_specs=pl.BlockSpec(memory_space=pl.ANY),
        scratch_shapes=[
            dma((2, n_line, 2)), pair, pair, pair, four, pair, pair, pair, pair, four, dma((2,)),
        ],
        compiler_params=pltpu.CompilerParams(
            collective_id=collective_id, has_side_effects=True
        ),
    )(x.reshape(2, rows // 2, width))
    return out.reshape(n_exp, n_line * rows, width)


def per_device(
    hidden_in,
    expert_ids,
    gate_weights,
    attn_gain,
    w_query,
    key_projection,
    value_projection,
    query_gain,
    key_norm_gain,
    w_output,
    mlp_gain,
    w_gate,
    w_up,
    w_down,
    grad_out,
):
    length, width = hidden_in.shape[1:]
    n_ctx, n_exp = lax.axis_size("ctx"), lax.axis_size("exp")
    n_all = n_ctx * n_exp
    ctx_index = lax.axis_index("ctx")
    rows_own, query_width = w_query.shape
    heads_own = query_width // HEAD_SIZE // n_exp
    own_width = heads_own * HEAD_SIZE
    sharers = n_exp // KEY_VALUE_HEADS
    tokens = n_exp * length
    holds_keys = lax.rem(lax.axis_index("exp"), 2) == 0
    pairs = [(i, i ^ 1) for i in range(n_exp)]
    factor = HEAD_SIZE ** (-0.5)
    w_gate, w_up, w_down = w_gate[0], w_up[0], w_down[0]

    def heads_of(kv):
        return kv.reshape(rows_own, KEY_VALUE_HEADS, 1, HEAD_SIZE)

    halves = jnp.concatenate([heads_of(key_projection), heads_of(value_projection)], axis=2)
    halves = jnp.broadcast_to(
        halves[:, :, None], (rows_own, KEY_VALUE_HEADS, sharers // 2, 2, HEAD_SIZE)
    ).reshape(rows_own, n_exp, HEAD_SIZE)
    packed = jnp.concatenate([w_query.reshape(rows_own, n_exp, own_width), halves], axis=2)
    packed_width = own_width + HEAD_SIZE
    packed = jnp.transpose(packed, (1, 0, 2))
    gains = jnp.concatenate([attn_gain, mlp_gain, query_gain, key_norm_gain])
    gain_rows = round_up(round_up(gains.shape[0], packed_width) // packed_width, 16)
    gains = jnp.pad(gains, (0, gain_rows * packed_width - gains.shape[0]))
    gains = jnp.broadcast_to(gains.reshape(1, gain_rows, packed_width), (n_exp, gain_rows, packed_width))
    hidden_all = lax.all_gather(hidden_in[0], "exp", axis=0, tiled=True)
    heads_in = lax.all_to_all(
        jnp.concatenate([packed, gains], axis=1), "exp", split_axis=0, concat_axis=0, tiled=True
    )
    weight_cols = heads_in[:, :rows_own].reshape(n_exp * rows_own, packed_width)
    gains = heads_in[:, rows_own:].reshape(n_exp, gain_rows * packed_width).astype(F32)
    cut = attn_gain.shape[0]
    small = query_gain.shape[0]
    first_gain = gains[:, :cut].reshape(-1)
    second_gain = gains[:, cut : 2 * cut].reshape(-1)
    q_gain = gains[:, 2 * cut : 2 * cut + small].reshape(-1)
    k_gain = gains[:, 2 * cut + small : 2 * cut + 2 * small].reshape(-1)

    hits = expert_ids[0][:, :, None] == jnp.arange(n_all, dtype=jnp.int32)[None, None, :]
    dense_gates = jnp.sum(jnp.where(hits, gate_weights[0][:, :, None], 0.0), axis=1)
    column_gates = lax.all_gather(dense_gates, "ctx", axis=0, tiled=True)
    span = n_ctx * length
    slots = round_up(n_ctx * max(2, length * TOPK * 4 // (3 * n_all)), 8)
    below = (
        jnp.arange(span, dtype=jnp.int32)[:, None] < jnp.arange(span, dtype=jnp.int32)[None, :]
    ).astype(BF)

    def in_slots(chosen):
        rank = dot(chosen.astype(BF), below, ((1,), (0,))).astype(jnp.int32)
        return chosen[:, None, :] & (
            rank[:, None, :] == jnp.arange(slots, dtype=jnp.int32)[None, :, None]
        )

    plane_gates = jnp.transpose(
        lax.dynamic_slice(column_gates, (0, ctx_index * n_exp), (span, n_exp))
    )
    chosen = plane_gates > 0.0
    is_slot = in_slots(chosen)
    pick = is_slot.astype(BF).reshape(n_exp * slots, span)
    weighted = jnp.where(is_slot, plane_gates[:, None, :], 0.0).reshape(n_exp * slots, span)
    slot_gates = jnp.sum(weighted, axis=1, keepdims=True)
    pick_high = weighted.astype(BF)
    pick_low = (weighted - pick_high.astype(F32)).astype(BF)

    def exchange(rows):
        rows = rows.astype(BF).reshape(n_exp, slots, width)
        rows = lax.all_to_all(rows, "exp", split_axis=0, concat_axis=0, tiled=True)
        return rows.reshape(n_exp * slots, width)

    grad_column = lax.all_gather(grad_out[0], "ctx", axis=0, tiled=True)
    slot_grads = dot(pick, grad_column, ((1,), (0,))) * slot_gates
    pattern = jnp.pad(chosen.astype(BF)[:, None, :], ((0, 0), (0, 7), (0, width - span)))
    sent = jnp.concatenate([slot_grads.astype(BF).reshape(n_exp, slots, width), pattern], axis=1)
    received = lax.all_to_all(sent, "exp", split_axis=0, concat_axis=0, tiled=True)
    slot_grads = received[:, :slots].reshape(n_exp * slots, width)
    take = in_slots(received[:, slots, :span] > 0.5).astype(BF)

    positions = ctx_index * length + jnp.arange(length, dtype=jnp.int32)
    cosine, sine = rope_tables(positions)
    cos_q, sin_q = cosine[None, :, None, :], sine[None, :, None, :]
    cos_k, sin_k = cosine[None], sine[None]
    wide_all = hidden_all.astype(F32)
    normed = (wide_all * rms_scale(wide_all) * first_gain).astype(BF)
    projected = dot(normed, weight_cols, ((1,), (0,)))
    queries = projected[:, :own_width].reshape(n_exp, length, heads_own, HEAD_SIZE)
    own_raw = projected[:, own_width:].reshape(n_exp, length, HEAD_SIZE)
    query_scale, key_scale = rms_scale(queries), rms_scale(own_raw)
    query_rot = rotate(queries * query_scale * q_gain, cos_q, sin_q).astype(BF)
    key_rot = rotate(own_raw * key_scale * k_gain, cos_k, sin_k).astype(BF)
    own_half = jnp.where(holds_keys, key_rot, own_raw.astype(BF)).reshape(tokens, HEAD_SIZE)
    own_half = lax.all_gather(own_half, "ctx", axis=0, tiled=True)
    other_half = lax.ppermute(own_half, "exp", pairs)

    def by_sequence(half):
        half = half.reshape(n_ctx, n_exp, length, HEAD_SIZE)
        return jnp.transpose(half, (1, 0, 2, 3)).reshape(n_exp, n_ctx * length, HEAD_SIZE)

    keys_all = by_sequence(jnp.where(holds_keys, own_half, other_half))
    values_all = by_sequence(jnp.where(holds_keys, other_half, own_half))

    query_rows = jnp.transpose(query_rot, (0, 2, 1, 3)).reshape(n_exp, heads_own * length, HEAD_SIZE)
    key_pos = jnp.arange(n_ctx * length, dtype=jnp.int32)
    causal = key_pos[None, :] <= jnp.tile(positions, heads_own)[:, None]

    def batched(a, b, a_dim, b_dim):
        return lax.dot_general(
            a, b, (((a_dim,), (b_dim,)), ((0,), (0,))), preferred_element_type=F32
        )

    expos = jnp.where(causal, jnp.exp(batched(query_rows, keys_all, 2, 2) * factor), 0.0)
    totals = jnp.sum(expos, axis=-1, keepdims=True)
    attn_heads = (batched(expos.astype(BF), values_all, 2, 1) / totals).astype(BF)
    attn_rows = jnp.transpose(
        attn_heads.reshape(n_exp, heads_own, length, HEAD_SIZE), (0, 2, 1, 3)
    ).reshape(tokens, own_width)
    branch_part = dot(attn_rows, w_output, ((1,), (0,))).astype(BF)
    branch = lax.psum_scatter(branch_part, "exp", scatter_dimension=0, tiled=True)
    wide_in = hidden_in[0].astype(F32)
    mid = wide_in + branch.astype(F32)
    second_scale = rms_scale(mid)
    mlp_in = (mid * second_scale * second_gain).astype(BF)

    mlp_all = gather_rows(after(mlp_in, take), n_ctx, n_exp, 3)
    arrived = lax.dot_general(
        take, mlp_all, (((2,), (1,)), ((0,), (0,))), preferred_element_type=F32
    ).astype(BF).reshape(n_exp * slots, width)
    gate_pre = dot(arrived, w_gate, ((1,), (0,)))
    up_pre = dot(arrived, w_up, ((1,), (0,)))
    sigmoid_gate = jax.nn.sigmoid(gate_pre)
    silu_gate = gate_pre * sigmoid_gate
    inner = (silu_gate * up_pre).astype(BF)
    grad_inner = dot(slot_grads, w_down, ((1,), (1,)))
    grad_gate_pre = (
        grad_inner * up_pre * sigmoid_gate * (1.0 + gate_pre * (1.0 - sigmoid_gate))
    ).astype(BF)
    grad_up_pre = (grad_inner * silu_gate).astype(BF)
    grad_expert_in = dot(grad_gate_pre, w_gate, ((1,), (1,))) + dot(
        grad_up_pre, w_up, ((1,), (1,))
    )
    grad_back = exchange(grad_expert_in)
    grad_mlp = lax.psum_scatter(
        dot(pick, grad_back, ((0,), (0,))).astype(BF), "ctx", scatter_dimension=0, tiled=True
    ).astype(F32)

    gradient_wide = grad_out[0].astype(F32)
    mlp_gain_part = jnp.sum(grad_mlp * mid * second_scale, axis=0)
    grad_mid = gradient_wide + norm_backward(grad_mlp, mid, second_scale, second_gain)
    branch_all = gather_rows(grad_mid.astype(BF), 1, n_exp, 4)
    branch_all = branch_all.reshape(tokens, width)

    expert_out = dot(inner, w_down, ((1,), (0,))).astype(BF)
    out_back = exchange(after(expert_out, branch_all))
    mixed_part = dot(pick_high, out_back, ((0,), (0,))) + dot(pick_low, out_back, ((0,), (0,)))
    mixed = lax.psum_scatter(mixed_part.astype(BF), "ctx", scatter_dimension=0, tiled=True)
    hidden_out = (mid + mixed.astype(F32)).astype(BF)
    grad_down = dot(inner, slot_grads, ((0,), (0,)))
    grad_gate_mat = dot(arrived, grad_gate_pre, ((0,), (0,)))
    grad_up_mat = dot(arrived, grad_up_pre, ((0,), (0,)))

    grad_wout = dot(attn_rows, branch_all, ((0,), (0,))).astype(BF)
    attn_grad = dot(after(branch_all, grad_wout), w_output, ((1,), (1,))).astype(BF)
    grad_heads = jnp.transpose(
        attn_grad.reshape(n_exp, length, heads_own, HEAD_SIZE), (0, 2, 1, 3)
    ).reshape(n_exp, heads_own * length, HEAD_SIZE)
    deltas = jnp.sum(grad_heads.astype(F32) * attn_heads.astype(F32), axis=-1, keepdims=True)
    probs = jnp.where(causal, jnp.exp(batched(query_rows, keys_all, 2, 2) * factor), 0.0) / totals
    grad_scores = (
        probs * (batched(grad_heads, values_all, 2, 2) - deltas) * factor
    ).astype(BF)
    value_part = batched(probs.astype(BF), grad_heads, 1, 1)
    key_part = batched(grad_scores, query_rows, 1, 1)

    def by_position(part):
        part = part.reshape(n_exp, n_ctx, length, HEAD_SIZE)
        return jnp.transpose(part, (1, 0, 2, 3))

    key_part, value_part = by_position(key_part), by_position(value_part)
    partner = jnp.where(holds_keys, value_part, key_part).astype(BF)
    partner = lax.ppermute(partner, "exp", pairs)
    own_part = jnp.where(holds_keys, key_part, value_part) + partner.astype(F32)
    own_part = own_part.astype(BF).reshape(n_ctx, tokens, HEAD_SIZE)
    own_sums = lax.psum_scatter(
        own_part.reshape(n_ctx * tokens, HEAD_SIZE),
        "ctx", scatter_dimension=0, tiled=True,
    ).astype(F32).reshape(n_exp, length, HEAD_SIZE)
    grad_query_rot = batched(grad_scores, keys_all, 2, 1)
    grad_query_unit = rotation_backward(
        jnp.transpose(
            grad_query_rot.reshape(n_exp, heads_own, length, HEAD_SIZE), (0, 2, 1, 3)
        ), cos_q, sin_q,
    )
    q_gain_part = jnp.sum(grad_query_unit * queries * query_scale, axis=(0, 1, 2))
    grad_query_rows = norm_backward(grad_query_unit, queries, query_scale, q_gain).astype(BF)
    grad_query_rows = grad_query_rows.reshape(tokens, own_width)
    grad_key_unit = rotation_backward(own_sums, cos_k, sin_k)
    k_gain_part = jnp.sum(grad_key_unit * own_raw * key_scale, axis=(0, 1))
    k_gain_part = jnp.where(holds_keys, k_gain_part, 0.0)
    grad_own = jnp.where(
        holds_keys, norm_backward(grad_key_unit, own_raw, key_scale, k_gain), own_sums
    ).astype(BF)
    grad_heads_in = jnp.concatenate(
        [grad_query_rows, grad_own.reshape(tokens, HEAD_SIZE)], axis=1
    )
    normed_part = dot(grad_heads_in, weight_cols, ((1,), (1,))).astype(BF)
    grad_normed = lax.psum_scatter(normed_part, "exp", scatter_dimension=0, tiled=True)
    grad_normed = grad_normed.astype(F32)
    first_scale = rms_scale(wide_in)
    grad_in = grad_mid + norm_backward(grad_normed, wide_in, first_scale, first_gain)

    wout_sum = line_sum(grad_wout, n_ctx)
    grad_cols = dot(normed, grad_heads_in, ((0,), (0,))).astype(BF)
    gain_parts = jnp.concatenate(
        [
            mlp_gain_part.reshape(n_exp, cut),
            q_gain_part.reshape(n_exp, small),
            k_gain_part.reshape(n_exp, small),
        ],
        axis=1,
    )
    gain_parts = jnp.pad(gain_parts, ((0, 0), (0, packed_width - cut - 2 * small)))[:, None, :]
    gain_parts = jnp.pad(gain_parts, ((0, 0), (0, 15), (0, 0))).astype(BF)
    grad_cols = jnp.concatenate(
        [grad_cols.reshape(n_exp, rows_own, packed_width), gain_parts], axis=1
    )
    grad_cols = column_sum(grad_cols.reshape(n_exp * (rows_own + 16), packed_width), n_ctx, n_exp)
    own_gains = jnp.sum(grad_cols[:, rows_own].astype(F32), axis=0)
    grad_cols = grad_cols[:, :rows_own]
    to_row = jnp.transpose(grad_cols, (1, 0, 2))
    halves = jnp.sum(
        to_row[:, :, own_width:]
        .reshape(rows_own, KEY_VALUE_HEADS, sharers // 2, 2, HEAD_SIZE)
        .astype(F32),
        axis=2,
    )
    kv_width = KEY_VALUE_HEADS * HEAD_SIZE
    grad_wq = to_row[:, :, :own_width].reshape(rows_own, query_width).astype(F32)
    grad_wk = halves[:, :, 0].reshape(rows_own, kv_width)
    grad_wv = halves[:, :, 1].reshape(rows_own, kv_width)

    attn_gain_sum = (
        jnp.sum(w_query.astype(F32) * grad_wq, axis=1)
        + jnp.sum(key_projection.astype(F32) * grad_wk, axis=1)
        + jnp.sum(value_projection.astype(F32) * grad_wv, axis=1)
    ) / attn_gain.astype(F32)

    return (
        hidden_out[None],
        grad_in[None],
        attn_gain_sum,
        grad_wq,
        grad_wk,
        grad_wv,
        own_gains[cut : cut + small],
        own_gains[cut + small : cut + 2 * small],
        wout_sum,
        own_gains[:cut],
        grad_gate_mat[None],
        grad_up_mat[None],
        grad_down[None],
    )


def solution(mesh):
    rows = P("exp", "ctx", None)
    shard, matrix, expert = P("exp"), P("exp", None), P(("ctx", "exp"), None, None)
    in_specs = (
        rows, rows, rows, shard, matrix, matrix, matrix, shard, shard, matrix, shard,
        expert, expert, expert, rows,
    )
    out_specs = (
        rows, rows, shard, matrix, matrix, matrix, shard, shard, matrix, shard,
        expert, expert, expert,
    )
    return jax.shard_map(
        per_device, mesh=mesh, in_specs=in_specs, out_specs=out_specs, check_vma=False
    )
```

time: 1270 us -> 893 us (0.70)
  waiting for transfers between devices: 886 us -> 221 us
  Pallas kernels: 0 us -> 269 us
  matrix products: 174 us -> 155 us
    reduce_scatter x5 -> x3, waiting for transfers between devices: 468 us -> 48.3 us  [the longest x1 41 us: per_device(): lax.psum_scatter(dot(pick, grad_back, ((0,), (0,))).astype(BF), 'ctx', sc...]
    pallas_call x0 -> x4, Pallas kernels: none -> 269 us  [the longest x2 98 us: gather_rows(): pl.pallas_call(functools.partial(gather_kernel, n_line), out_shape=jax.Sh...]
    all_gather x6 -> x2, waiting for transfers between devices: 282 us -> 18.2 us  [the longest x1 18.2 us: per_device(): grad_column = lax.all_gather(grad_out[0], 'ctx', axis=0, tiled=True)]
    all_to_all x0 -> x2, waiting for transfers between devices: none -> 113 us  [the longest x1 82.7 us: per_device(): lax.all_to_all(sent, 'exp', split_axis=0, concat_axis=0, tiled=True)]
    reduce_scatter x1, waiting for transfers between devices: 49.5 us -> 0.01 us  [per_device(): lax.psum_scatter(branch_part, 'exp', scatter_dimension=0, tiled=True)]
    psum x1 -> x0, blocking collectives: 42.7 us -> none  [per_device(): parts = lax.psum(parts, EVERY)]
    all_to_all x2 -> x1, blocking collectives: 28 us -> 66 us  [exchange(): rows = lax.all_to_all(rows, 'exp', split_axis=0, concat_axis=0, tiled=True)]
    reduce_scatter x1, waiting for transfers between devices: 34.6 us -> 0.01 us  [per_device(): lax.psum_scatter(normed_part, 'exp', scatter_dimension=0, tiled=True)]
  transfers between devices with their start and end apart: 15 -> 13, of which waited for: 13 -> 6; matrix products, arithmetic and copies ran while one was open for 13% -> 19% of each run, Pallas kernels for 0% -> 19%
where the time goes in v2:
time: 893 us; the launch traced here: 884 us
  Pallas kernels  269 us (30%)
  waiting for transfers between devices  221 us (25%)
  matrix products  155 us (17%)
  blocking collectives  79.9 us (9%)
  other arithmetic  68.9 us (8%)
  local copies, waits for them, and re-layouts  59.3 us (7%)
  starting transfers between devices  15.7 us (2%)
  between operations  15.5 us (2%)
    dot_general x21, matrix products, dot(): return lax.dot_general(a, b, (dims, ((), ())), preferred_element_type=F32)  126 us
    pallas_call x2, Pallas kernels, gather_rows(): pl.pallas_call(functools.partial(gather_kernel, n_line), out_shape=jax.Sh...  98 us
    pallas_call x1, Pallas kernels, line_sum(): pl.pallas_call(functools.partial(line_sum_kernel, n_ctx, chunks), out_sha...  88.8 us
    all_to_all x1, waiting for transfers between devices, per_device(): lax.all_to_all(sent, 'exp', split_axis=0, concat_axis=0, tiled=True)  82.7 us
    pallas_call x1, Pallas kernels, column_sum(): pl.pallas_call(functools.partial(column_sum_kernel, n_ctx, n_exp, subs),...  82.2 us
    all_to_all x1, blocking collectives, exchange(): rows = lax.all_to_all(rows, 'exp', split_axis=0, concat_axis=0, tiled=True)  66 us
    reduce_scatter x1, waiting for transfers between devices, per_device(): lax.psum_scatter(dot(pick, grad_back, ((0,), (0,))).astype(BF), 'ctx', sc...  41 us
    all_to_all x1, waiting for transfers between devices, per_device(): lax.all_to_all(jnp.concatenate([packed, gains], axis=1), 'exp', split_axi...  39.7 us
  transfers between devices with their start and end apart: 13, of which 6 were waited for; matrix products, arithmetic and copies ran while one was open for 19% of the time, Pallas kernels for 19%

profile of v2, /device:TPU:0, one launch (start us, length us, event | category | flops | bytes accessed | tf_op | source)
XLA Modules:
  0.0 884.2 jit_solution(8661690245642735996)
XLA Ops:
  14.4 2.0 copy.147
  16.5 2.0 copy.148
  18.5 4.1 copy.144
  24.8 2.5 pad_maximum_fusion.1
  27.3 5.7 copy.150
  33.0 5.2 all-to-all-start
  38.7 39.7 %all-to-all-done = bf16[8,272,640]{2,1,0:T(8,128)(2,1)} async-done(((bf16[8,272,640]{2,1,0:T(8,128)(2,1)}), bf16[8,272,640]{2,1,0:T(8,128)(2,1)}, u32[]{:S(2)}, u32[]{:S(2)}) %all-to-all-start) | async-done | bytes 2785312 | tf_op jit(solution)/shard_map/all_to_all | solution.py:495
  80.3 3.5 slice.110
  83.8 3.2 fusion
  87.2 5.2 fusion.57
  96.8 13.9 %all_gather.14 = f32[512,32]{0,1:T(8,128)S(1)} all-gather(f32[128,32]{0,1:T(8,128)S(1)} %select_reduce_fusion.1), channel_id=1, replica_groups=mesh['ctx'=4,'exp'=8] {'ctx'}, dimensions={0}, use_global_device_ids=true | all-gather | bytes 81920 | tf_op jit(solution)/shard_map/all_gather | solution.py:509
  113.6 2.1 fusion.32
  117.8 3.1 slice.111
  120.9 2.9 reshape.318
  123.8 2.8 multiply_reduce_fusion.4
  127.5 2.5 multiply_multiply_fusion
  131.9 2.5 fusion.72
  136.0 2.2 fusion.5
  138.2 3.7 divide_convert_fusion
  141.9 2.8 copy.155
  144.7 6.3 convolution_convert_fusion.3
  151.1 18.2 %all-gather.10.cloned.1.call-done = bf16[1,512,2048]{2,1,0:T(8,128)(2,1)} async-done(((bf16[1,128,2048]{2,1,0:T(8,128)(2,1)}), bf16[1,512,2048]{2,1,0:T(8,128)(2,1)}) %all-gather.10.cloned.1.call-update) | async-done | bytes 2097168 | tf_op jit(solution)/shard_map/all_gather | solution.py:538
  169.3 4.8 multiply_convert_fusion
  174.1 3.1 pad_maximum_fusion
  177.2 4.9 all-to-all-start.1
  182.2 82.7 %all-to-all-done.1 = bf16[8,176,2048]{2,1,0:T(8,128)(2,1)} async-done(((bf16[8,176,2048]{2,1,0:T(8,128)(2,1)}), bf16[8,176,2048]{2,1,0:T(8,128)(2,1)}, u32[]{:S(2)}, u32[]{:S(2)}) %all-to-all-start.1) | async-done | bytes 5767200 | tf_op jit(solution)/shard_map/all_to_all | solution.py:542
  265.7 5.9 slice.121
  273.3 2.2 multiply_convert_fusion.6
  275.5 74.9 %shard_map.246 = bf16[8,4,2,64,2048]{4,3,2,1,0:T(8,128)(2,1)} custom-call(bf16[2,64,2048]{2,1,0:T(8,128)(2,1)} %bitcast.285), custom_call_target="tpu_custom_call" | custom-call | tf_op jit(solution)/shard_map/pallas_call | solution.py:434
  350.4 8.9 %convolution_convert_fusion.1 = bf16[8,168,2048]{2,1,0:T(8,128)(2,1)S(1)} fusion(bf16[8,512,2048]{2,1,0:T(8,128)(2,1)} %bitcast.245, s32[8,512]{1,0:T(8,128)S(1)} %convolution_convert_fusion.7, pred[8,512]{1,0:T(8,128)(4,1)S(1)} %compare_bitcast_fusion), kind=kOutput, calls=%fused_computation.19 | convolution fusion | flops 2822701056 | bytes 22302720 | tf_op jit(solution)/shard_map/dot_general | solution.py:592
  359.4 6.1 fusion.24
  365.6 5.9 fusion.20
  371.5 9.6 %multiply_convert_fusion.2 = (bf16[1344,768]{1,0:T(8,128)(2,1)}, bf16[1344,768]{1,0:T(8,128)(2,1)S(1)}, bf16[1344,768]{1,0:T(8,128)(2,1)}) fusion(f32[1344,768]{1,0:T(8,128)} %fusion.24, f32[1344,768]{1,0:T(8,128)} %fusion.20, bf16[1344,2048]{1,0:T(8,128)(2,1)S(1)} %bitcast.254, bf16[1,768,2048]{2,1,0:T(8,128)(2,1)S(1)} %copy-done), kind=kOutput, calls=%fused_computation.31 | convolution fusion | flops 4243341312 | bytes 23101440 | tf_op jit(solution)/shard_map/dot_general | solution.py:55
  381.1 7.1 fusion.22
  388.2 7.9 add_convert_fusion
  396.1 66.0 %all_to_all.20 = bf16[8,168,2048]{2,1,0:T(8,128)(2,1)S(1)} all-to-all(bf16[8,168,2048]{2,1,0:T(8,128)(2,1)S(1)} %bitcast.264), channel_id=1, replica_groups=mesh['ctx'=4,'exp'=8] {'exp'}, dimensions={0} | all-to-all | bytes 11010048 | tf_op jit(solution)/shard_map/all_to_all | solution.py:535
  462.1 4.7 bitcast_convert_fusion
  466.9 41.0 %reduce-scatter.8.cloned.1.call-done = bf16[128,2048]{1,0:T(8,128)(2,1)} async-done(((bf16[512,2048]{1,0:T(8,128)(2,1)}), bf16[128,2048]{1,0:T(8,128)(2,1)}) %reduce-scatter.8.cloned.1.call-update) | async-done | bytes 524304 | tf_op jit(solution)/shard_map/reduce_scatter | solution.py:609
  507.9 2.0 fusion.68
  509.9 2.8 fusion.107
  512.7 23.2 %shard_map.247 = bf16[8,1,2,64,2048]{4,3,2,1,0:T(8,128)(2,1)} custom-call(bf16[2,64,2048]{2,1,0:T(8,128)(2,1)} %bitcast.284), custom_call_target="tpu_custom_call" | custom-call | tf_op jit(solution)/shard_map/pallas_call | solution.py:434
  535.9 6.3 convolution_convert_fusion.5
  542.2 3.3 convolution_convert_fusion.6
  545.5 2.5 reshape.335
  551.4 4.7 fusion.10
  556.2 5.3 multiply_convert_fusion.1
  564.3 6.3 convolution_convert_fusion
  570.6 2.8 fusion.114
  574.8 3.0 multiply_bitcast_fusion
  580.2 4.5 multiply_reduce_fusion.1
  584.8 2.7 multiply_convert_fusion.5
  588.7 4.8 all-to-all-start.3
  593.6 7.3 reduce-scatter.12.cloned.1.call-done
  605.4 5.0 convolution_convert_fusion.2
  610.5 9.6 %convolution_bitcast_fusion.2 = f32[1,2048,768]{2,1,0:T(8,128)} fusion(bf16[1344,2048]{1,0:T(8,128)(2,1)} %bitcast.260, bf16[1344,768]{1,0:T(8,128)(2,1)} %copy-done.57), kind=kOutput, calls=%fused_computation.39 | convolution fusion | flops 4227858432 | bytes 13860864 | tf_op jit(solution)/shard_map/dot_general | solution.py:55
  620.1 10.1 %convolution_bitcast_fusion.1 = f32[1,2048,768]{2,1,0:T(8,128)} fusion(bf16[1344,2048]{1,0:T(8,128)(2,1)} %bitcast.261, bf16[1344,768]{1,0:T(8,128)(2,1)S(1)} %copy-done.60), kind=kOutput, calls=%fused_computation.38 | convolution fusion | flops 4227858432 | bytes 13860864 | tf_op jit(solution)/shard_map/dot_general | solution.py:55
  630.2 7.1 convolution_bitcast_fusion
  637.2 30.6 %all-to-all-done.3 = bf16[8,168,2048]{2,1,0:T(8,128)(2,1)} async-done(((bf16[8,168,2048]{2,1,0:T(8,128)(2,1)}), bf16[8,168,2048]{2,1,0:T(8,128)(2,1)}, u32[]{:S(2)}, u32[]{:S(2)}) %all-to-all-start.3) | async-done | bytes 5505056 | tf_op jit(solution)/shard_map/all_to_all | solution.py:535
  667.9 5.8 fusion.38
  673.7 7.4 fusion.9
  682.9 88.8 %shard_map.249 = f32[16,32,2048]{2,1,0:T(8,128)S(1)} custom-call(bf16[16,32,2048]{2,1,0:T(8,128)(2,1)S(1)} %bitcast.244), custom_call_target="tpu_custom_call" | custom-call | tf_op jit(solution)/shard_map/pallas_call | solution.py:196
  773.8 6.3 convolution_convert_fusion.4
  780.4 82.2 %shard_map.248 = bf16[8,2,136,640]{3,2,1,0:T(8,128)(2,1)S(1)} custom-call(bf16[16,136,640]{2,1,0:T(8,128)(2,1)S(1)} %bitcast.241), custom_call_target="tpu_custom_call" | custom-call | tf_op jit(solution)/shard_map/pallas_call | solution.py:261
  871.2 4.0 fusion.63
  (246 shorter events, 58.3 us)
Async XLA Ops:
  7.2 364.3 %copy-start = (bf16[1,768,2048]{2,1,0:T(8,128)(2,1)S(1)}, bf16[1,768,2048]{2,1,0:T(8,128)(2,1)}, u32[]{:S(2)}) copy-start(bf16[1,768,2048]{2,1,0:T(8,128)(2,1)} %param.28) | copy-start | bytes 9437188
  7.2 76.6 %all-gather.8.cloned.1.call-start = ((), (), s32[]{:S(2)}) async-start(), calls=%async_computation.15 | async-start | bytes 4718592 | tf_op jit(solution)/shard_map/all_gather | solution.py:494
  33.0 45.5 %all-to-all-start = ((bf16[8,272,640]{2,1,0:T(8,128)(2,1)}), bf16[8,272,640]{2,1,0:T(8,128)(2,1)}, u32[]{:S(2)}, u32[]{:S(2)}) async-start(bf16[8,272,640]{2,1,0:T(8,128)(2,1)} %copy.150), calls=%async_computation | async-start | bytes 5570560 | tf_op jit(solution)/shard_map/all_to_all | solution.py:495
  38.1 89.3 %all-gather.6.cloned.1.call-start = ((), (), s32[]{:S(2)}) async-start(), calls=%async_computation.9 | async-start | bytes 1310720 | tf_op jit(solution)/shard_map/all_gather | solution.py:559
  38.6 92.7 %copy-start.23 = (f32[128,128]{1,0:T(8,128)}, f32[128,128]{1,0:T(8,128)S(1)}, u32[]{:S(2)}) copy-start(f32[128,128]{1,0:T(8,128)S(1)} %pad_maximum_fusion.7) | copy-start | bytes 196612
  38.7 92.6 %copy-start.21 = (f32[128,128]{1,0:T(8,128)}, f32[128,128]{1,0:T(8,128)S(1)}, u32[]{:S(2)}) copy-start(f32[128,128]{1,0:T(8,128)S(1)} %pad_maximum_fusion.6) | copy-start | bytes 196612
  80.1 6.9 copy-start.34
  80.3 12.9 %copy-start.41 = (f32[128]{0:T(128)}, f32[128]{0:T(128)S(1)}, u32[]{:S(2)}) copy-start(f32[128]{0:T(128)S(1)} %mul.430) | copy-start | bytes 1540
  83.8 3.4 copy-start.15
  87.0 5.5 copy-start.46
  92.7 4.0 copy-start.48
  92.7 4.0 copy-start.49
  95.1 74.2 %all-gather.10.cloned.1.call-start = ((), (), s32[]{:S(2)}) async-start(), calls=%async_computation.16 | async-start | bytes 2621440 | tf_op jit(solution)/shard_map/all_gather | solution.py:538
  95.8 176.1 %reduce-scatter.6.cloned.1.call-start = ((), (), s32[]{:S(2)}) async-start(), calls=%async_computation.10 | async-start | bytes 4718592 | tf_op jit(solution)/shard_map/reduce_scatter | solution.py:585
  117.8 13.5 %copy-start.43 = (f32[128]{0:T(128)}, f32[128]{0:T(128)S(1)}, u32[]{:S(2)}) copy-start(f32[128]{0:T(128)S(1)} %mul.415) | copy-start | bytes 1540
  127.5 7.2 collective-permute-start
  131.9 2.8 copy-start.25
  134.9 3.3 copy-start.13
  135.0 3.2 copy-start.26
  138.2 3.7 copy-start.54
  138.2 3.7 copy-start.58
  151.0 18.3 %copy-start.45 = (f32[1344]{0:T(1024)S(1)}, f32[1344]{0:T(1024)}, u32[]{:S(2)}) copy-start(f32[1344]{0:T(1024)} %mul.445) | copy-start | bytes 16132
  177.2 5.0 copy-start.40
  177.2 87.7 %all-to-all-start.1 = ((bf16[8,176,2048]{2,1,0:T(8,128)(2,1)}), bf16[8,176,2048]{2,1,0:T(8,128)(2,1)}, u32[]{:S(2)}, u32[]{:S(2)}) async-start(bf16[8,176,2048]{2,1,0:T(8,128)(2,1)} %pad_maximum_fusion), calls=%async_computation.2 | async-start | bytes 11534336 | tf_op jit(solution)/shard_map/all_to_all | solution.py:542
  182.1 325.8 %reduce-scatter.8.cloned.1.call-start = ((), (), s32[]{:S(2)}) async-start(), calls=%async_computation.11 | async-start | bytes 2621440 | tf_op jit(solution)/shard_map/reduce_scatter | solution.py:609
  350.4 9.0 %copy-start.51 = (bf16[1,2048,768]{2,1,0:T(8,128)(2,1)S(1)}, bf16[1,2048,768]{2,1,0:T(8,128)(2,1)}, u32[]{:S(2)}) copy-start(bf16[1,2048,768]{2,1,0:T(8,128)(2,1)} %param.26) | copy-start | bytes 9437188
  359.4 6.2 copy-start.12
  359.4 6.1 copy-start.52
  359.4 12.1 %slice-start = ((s8[5505024]{0:T(1024)(128)(4,1)}), s8[4194304]{0:T(1024)(128)(4,1)S(1)}, s32[]{:S(2)}) async-start(s8[5505024]{0:T(1024)(128)(4,1)} %bitcast.252), calls=%async_computation.17 | async-start | bytes 8388608
  365.6 5.9 slice-start.1
  381.1 7.1 copy-start.57
  396.1 66.0 %copy-start.38 = (s32[8,512]{1,0:T(8,128)S(1)}, s32[8,512]{1,0:T(8,128)}, u32[]{:S(2)}) copy-start(s32[8,512]{1,0:T(8,128)} %convolution_convert_fusion.8) | copy-start | bytes 49156
  466.9 134.0 %reduce-scatter.12.cloned.1.call-start = ((), (), s32[]{:S(2)}) async-start(), calls=%async_computation.13 | async-start | bytes 1310720 | tf_op jit(solution)/shard_map/reduce_scatter | solution.py:650
  535.9 6.3 copy-start.16
  535.9 6.3 copy-start.53
  545.5 5.9 copy-start.33
  545.5 5.9 copy-start.59
  551.4 4.8 copy-start.27
  556.2 5.3 copy-start.18
  563.1 10.3 %collective-permute-start.1 = (bf16[4,8,128,128]{3,2,1,0:T(8,128)(2,1)S(1)}, bf16[4,8,128,128]{3,2,1,0:T(8,128)(2,1)S(1)}, u32[]{:S(2)}, u32[]{:S(2)}) collective-permute-start(bf16[4,8,128,128]{3,2,1,0:T(8,128)(2,1)S(1)} %bitcast.300), channel_id=1, source_target_pairs={{0,1},{1,0},{2,3},{3,2},{4,5},{5,4},{6,7},{7,6},{8,9},{9,8},{10,11... | collective-permute-start | bytes 3145736 | tf_op jit(solution)/shard_map/ppermute | solution.py:647
  564.3 6.3 copy-start.14
  577.8 2.4 copy-start.6
  577.8 2.5 copy-start.9
  577.8 2.5 copy-start.22
  577.8 2.4 copy-start.44
  588.7 13.5 %copy-start.37 = (f32[1024]{0:T(1024)S(1)}, f32[1024]{0:T(1024)}, u32[]{:S(2)}) copy-start(f32[1024]{0:T(1024)} %copy-done.36) | copy-start | bytes 12292
  588.7 13.5 %copy-start.42 = (f32[128]{0:T(128)S(1)}, f32[128]{0:T(128)}, u32[]{:S(2)}) copy-start(f32[128]{0:T(128)} %copy-done.41) | copy-start | bytes 1540
  588.7 79.2 %all-to-all-start.3 = ((bf16[8,168,2048]{2,1,0:T(8,128)(2,1)}), bf16[8,168,2048]{2,1,0:T(8,128)(2,1)}, u32[]{:S(2)}, u32[]{:S(2)}) async-start(bf16[8,168,2048]{2,1,0:T(8,128)(2,1)} %bitcast.262), calls=%async_computation.5 | async-start | bytes 11010048 | tf_op jit(solution)/shard_map/all_to_all | solution.py:535
  593.5 276.1 %reduce-scatter.14.cloned.1.call-start = ((), (), s32[]{:S(2)}) async-start(), calls=%async_computation.14 | async-start | bytes 4718592 | tf_op jit(solution)/shard_map/reduce_scatter | solution.py:673
  600.8 3.1 copy-start.20
  601.9 3.4 copy-start.19
  601.9 3.4 copy-start.28
  610.4 260.8 %reduce-scatter.10.cloned.1.call-start = ((), (), s32[]{:S(2)}) async-start(), calls=%async_computation.12 | async-start | bytes 2621440 | tf_op jit(solution)/shard_map/reduce_scatter | solution.py:622
  610.4 9.6 %copy-start.60 = (bf16[1344,768]{1,0:T(8,128)(2,1)S(1)}, bf16[1344,768]{1,0:T(8,128)(2,1)}, u32[]{:S(2)}) copy-start(bf16[1344,768]{1,0:T(8,128)(2,1)} %get-tuple-element.32) | copy-start | bytes 6193156
  610.5 19.7 %slice-start.2 = ((s8[5505024]{0:T(1024)(128)(4,1)}), s8[4194304]{0:T(1024)(128)(4,1)S(1)}, s32[]{:S(2)}) async-start(s8[5505024]{0:T(1024)(128)(4,1)} %bitcast.255), calls=%async_computation.19 | async-start | bytes 8388608
  620.1 10.1 %slice-start.3 = ((s8[5505024]{0:T(1024)(128)(4,1)}), s8[1310720]{0:T(1024)(128)(4,1)S(1)}, s32[]{:S(2)}) async-start(s8[5505024]{0:T(1024)(128)(4,1)} %bitcast.255), calls=%async_computation.20 | async-start | bytes 2621440
  620.1 10.1 %copy-start.56 = (bf16[1344,768]{1,0:T(8,128)(2,1)S(1)}, bf16[1344,768]{1,0:T(8,128)(2,1)}, u32[]{:S(2)}) copy-start(bf16[1344,768]{1,0:T(8,128)(2,1)} %get-tuple-element.34) | copy-start | bytes 6193156
  630.2 37.7 %copy-start.39 = (f32[8,512]{1,0:T(8,128)S(1)}, f32[8,512]{1,0:T(8,128)}, u32[]{:S(2)}) copy-start(f32[8,512]{1,0:T(8,128)} %get-tuple-element.31) | copy-start | bytes 49156
  682.9 90.9 %copy-start.35 = (f32[1,2,8,128]{3,1,2,0:T(2,128)S(1)}, f32[1,2,8,128]{3,1,2,0:T(2,128)}, u32[]{:S(2)}) copy-start(f32[1,2,8,128]{3,1,2,0:T(2,128)} %copy-done.34) | copy-start | bytes 24580
  682.9 90.9 %copy-start.47 = (f32[1024]{0:T(1024)S(1)}, f32[1024]{0:T(1024)}, u32[]{:S(2)}) copy-start(f32[1024]{0:T(1024)} %copy-done.46) | copy-start | bytes 12292
  864.0 2.5 copy-start.30
  864.6 3.7 copy-start.7
  864.6 3.2 copy-start.10
  871.2 4.0 copy-start.2
  (14 other events, 20.9 us)
Sparse Core Ops, SparseCore 0:
  9.9 45.5 all-gather.7
  95.2 27.2 all-gather.5
  124.1 45.1 all-gather.9
  173.1 81.5 reduce-scatter.5
  467.0 40.8 reduce-scatter.7
  574.9 25.9 reduce-scatter.11
  610.5 67.0 reduce-scatter.13
  681.3 74.2 reduce-scatter.9

commit v3 on v2

--- a/solution.py
+++ b/solution.py
@@ -444,6 +444,144 @@
         ),
     )(x.reshape(2, rows // 2, width))
     return out.reshape(n_exp, n_line * rows, width)
+
+
+def reduce_kernel(x_ref, out_ref, from_core, sums, arrived, c_send, c_recv, q_send, q_recv):
+    exp = lax.axis_index("exp")
+
+    def flip(device, bit):
+        return device + bit - 2 * bit * lax.rem(device // bit, 2)
+
+    over_core, over_x, over_y = flip(exp, 1), flip(exp, 2), flip(exp, 4)
+    owners = (flip(over_x, 4), over_x, over_y, exp)
+    greet(1, [{"exp": other} for other in (over_core,) + owners[:3]])
+    rows = 16
+
+    def to_core(t):
+        return pltpu.make_async_remote_copy(
+            src_ref=x_ref.at[flip(owners[t], 1)], dst_ref=from_core.at[t],
+            send_sem=c_send.at[t], recv_sem=c_recv.at[t],
+            device_id={"exp": over_core}, device_id_type=MESH,
+        )
+
+    def to_owner(t):
+        return pltpu.make_async_remote_copy(
+            src_ref=sums.at[t], dst_ref=arrived.at[t],
+            send_sem=q_send.at[t], recv_sem=q_recv.at[t],
+            device_id={"exp": owners[t]}, device_id_type=MESH,
+        )
+
+    def by_rows(body):
+        def step(i, carry):
+            body(pl.ds(pl.multiple_of(i * rows, rows), rows))
+            return carry
+
+        lax.fori_loop(0, out_ref.shape[0] // rows, step, 0)
+
+    for t in range(4):
+        to_core(t).start()
+    for t in range(4):
+        to_core(t).wait_recv()
+
+        def add(at, t=t):
+            value = x_ref[owners[t], at, :].astype(F32) + from_core[t, at, :].astype(F32)
+            if t < 3:
+                sums[t, at, :] = value.astype(BF)
+            else:
+                out_ref[at, :] = value
+
+        by_rows(add)
+        if t < 3:
+            to_owner(t).start()
+    for t in (1, 2, 0):
+        to_owner(t).wait_recv()
+
+        def gather(at, t=t):
+            out_ref[at, :] = out_ref[at, :] + arrived[t, at, :].astype(F32)
+
+        by_rows(gather)
+    for t in range(4):
+        to_core(t).wait_send()
+        if t < 3:
+            to_owner(t).wait_send()
+
+
+def reduce_rows(x, n_exp, collective_id):
+    rows, width = x.shape[0] // n_exp, x.shape[1]
+    if n_exp != 8:
+        return lax.psum_scatter(x, "exp", scatter_dimension=0, tiled=True).astype(F32)
+    dma = pltpu.SemaphoreType.DMA
+    return pl.pallas_call(
+        reduce_kernel,
+        out_shape=jax.ShapeDtypeStruct((rows, width), F32),
+        in_specs=[pl.BlockSpec(memory_space=pltpu.VMEM)],
+        out_specs=pl.BlockSpec(memory_space=pltpu.VMEM),
+        scratch_shapes=[
+            pltpu.VMEM((4, rows, width), BF), pltpu.VMEM((3, rows, width), BF),
+            pltpu.VMEM((3, rows, width), BF), dma((4,)), dma((4,)), dma((3,)), dma((3,)),
+        ],
+        compiler_params=pltpu.CompilerParams(
+            collective_id=collective_id, has_side_effects=True, vmem_limit_bytes=32 * 1024 * 1024
+        ),
+    )(x.reshape(n_exp, rows, width))
+
+
+def spread_kernel(
+    n_exp, sharers, query_ref, halves_ref, gains_ref, out_ref, gains_out_ref,
+    q_send, q_recv, h_send, h_recv, g_send, g_recv, own_sems,
+):
+    exp = lax.axis_index("exp")
+    own_width = query_ref.shape[1] // n_exp
+    greet(1, [{"exp": lax.rem(exp + hop, n_exp)} for hop in range(1, n_exp)])
+
+    def pieces(owner):
+        columns = pl.ds(pl.multiple_of(owner * own_width, own_width), own_width)
+        return (
+            (query_ref.at[:, columns], out_ref.at[exp, :, pl.ds(0, own_width)]),
+            (
+                halves_ref.at[owner // sharers, lax.rem(owner, 2)],
+                out_ref.at[exp, :, pl.ds(own_width, HEAD_SIZE)],
+            ),
+            (gains_ref, gains_out_ref.at[exp]),
+        )
+
+    copies = []
+    for hop in range(1, n_exp):
+        owner = lax.rem(exp + hop, n_exp)
+        for (src, dst), send, recv in zip(
+            pieces(owner), (q_send, h_send, g_send), (q_recv, h_recv, g_recv)
+        ):
+            copies.append(
+                pltpu.make_async_remote_copy(
+                    src_ref=src, dst_ref=dst, send_sem=send.at[hop], recv_sem=recv.at[hop],
+                    device_id={"exp": owner}, device_id_type=MESH,
+                )
+            )
+    for i, (src, dst) in enumerate(pieces(exp)):
+        copies.append(pltpu.make_async_copy(src, dst, own_sems.at[i]))
+    for copy in copies:
+        copy.start()
+    for copy in copies:
+        copy.wait()
+
+
+def spread_columns(query, halves, gains, n_exp, sharers):
+    rows, width = query.shape
+    dma = pltpu.SemaphoreType.DMA((n_exp,))
+    vmem = pl.BlockSpec(memory_space=pltpu.VMEM)
+    return pl.pallas_call(
+        functools.partial(spread_kernel, n_exp, sharers),
+        out_shape=(
+            jax.ShapeDtypeStruct((n_exp, rows, width // n_exp + HEAD_SIZE), BF),
+            jax.ShapeDtypeStruct((n_exp,) + gains.shape, BF),
+        ),
+        in_specs=[vmem] * 3,
+        out_specs=(vmem, vmem),
+        scratch_shapes=[dma] * 6 + [pltpu.SemaphoreType.DMA((3,))],
+        compiler_params=pltpu.CompilerParams(
+            collective_id=6, has_side_effects=True, vmem_limit_bytes=24 * 1024 * 1024
+        ),
+    )(query, halves, gains)
 
 
 def per_device(
@@ -481,22 +619,19 @@
         return kv.reshape(rows_own, KEY_VALUE_HEADS, 1, HEAD_SIZE)
 
     halves = jnp.concatenate([heads_of(key_projection), heads_of(value_projection)], axis=2)
-    halves = jnp.broadcast_to(
-        halves[:, :, None], (rows_own, KEY_VALUE_HEADS, sharers // 2, 2, HEAD_SIZE)
-    ).reshape(rows_own, n_exp, HEAD_SIZE)
-    packed = jnp.concatenate([w_query.reshape(rows_own, n_exp, own_width), halves], axis=2)
+    halves = jnp.transpose(halves, (1, 2, 0, 3))
     packed_width = own_width + HEAD_SIZE
-    packed = jnp.transpose(packed, (1, 0, 2))
     gains = jnp.concatenate([attn_gain, mlp_gain, query_gain, key_norm_gain])
-    gain_rows = round_up(round_up(gains.shape[0], packed_width) // packed_width, 16)
-    gains = jnp.pad(gains, (0, gain_rows * packed_width - gains.shape[0]))
-    gains = jnp.broadcast_to(gains.reshape(1, gain_rows, packed_width), (n_exp, gain_rows, packed_width))
-    hidden_all = lax.all_gather(hidden_in[0], "exp", axis=0, tiled=True)
-    heads_in = lax.all_to_all(
-        jnp.concatenate([packed, gains], axis=1), "exp", split_axis=0, concat_axis=0, tiled=True
-    )
-    weight_cols = heads_in[:, :rows_own].reshape(n_exp * rows_own, packed_width)
-    gains = heads_in[:, rows_own:].reshape(n_exp, gain_rows * packed_width).astype(F32)
+    gain_rows = round_up(gains.shape[0], 16 * HEAD_SIZE) // HEAD_SIZE
+    gains = jnp.pad(gains, (0, gain_rows * HEAD_SIZE - gains.shape[0]))
+    hidden_all = gather_rows(hidden_in[0], 1, n_exp, 7)
+    hidden_all = hidden_all.reshape(tokens, width)
+    weight_cols, gains = spread_columns(
+        after(w_query, hidden_all), halves, gains.reshape(gain_rows, HEAD_SIZE),
+        n_exp, sharers,
+    )
+    weight_cols = weight_cols.reshape(n_exp * rows_own, packed_width)
+    gains = gains.reshape(n_exp, gain_rows * HEAD_SIZE).astype(F32)
     cut = attn_gain.shape[0]
     small = query_gain.shape[0]
     first_gain = gains[:, :cut].reshape(-1)
@@ -506,7 +641,18 @@
 
     hits = expert_ids[0][:, :, None] == jnp.arange(n_all, dtype=jnp.int32)[None, None, :]
     dense_gates = jnp.sum(jnp.where(hits, gate_weights[0][:, :, None], 0.0), axis=1)
-    column_gates = lax.all_gather(dense_gates, "ctx", axis=0, tiled=True)
+    high = lax.reduce_precision(dense_gates, 8, 7)
+    middle = lax.reduce_precision(dense_gates - high, 8, 7)
+    gate_parts = jnp.concatenate([high, middle, dense_gates - high - middle], axis=1).astype(BF)
+    gate_parts = jnp.pad(gate_parts, ((0, 0), (0, round_up(3 * n_all, HEAD_SIZE) - 3 * n_all)))
+    grad_column = lax.all_gather(
+        jnp.concatenate([grad_out[0], gate_parts], axis=1), "ctx",
+        axis=0, tiled=True,
+    )
+    gate_parts = grad_column[:, width : width + 3 * n_all].astype(F32)
+    column_gates = (
+        gate_parts[:, :n_all] + gate_parts[:, n_all : 2 * n_all] + gate_parts[:, 2 * n_all :]
+    )
     span = n_ctx * length
     slots = round_up(n_ctx * max(2, length * TOPK * 4 // (3 * n_all)), 8)
     below = (
@@ -527,16 +673,15 @@
     pick = is_slot.astype(BF).reshape(n_exp * slots, span)
     weighted = jnp.where(is_slot, plane_gates[:, None, :], 0.0).reshape(n_exp * slots, span)
     slot_gates = jnp.sum(weighted, axis=1, keepdims=True)
-    pick_high = weighted.astype(BF)
-    pick_low = (weighted - pick_high.astype(F32)).astype(BF)
+    high = lax.reduce_precision(weighted, 8, 7)
+    pick_high, pick_low = high.astype(BF), (weighted - high).astype(BF)
 
     def exchange(rows):
         rows = rows.astype(BF).reshape(n_exp, slots, width)
         rows = lax.all_to_all(rows, "exp", split_axis=0, concat_axis=0, tiled=True)
         return rows.reshape(n_exp * slots, width)
 
-    grad_column = lax.all_gather(grad_out[0], "ctx", axis=0, tiled=True)
-    slot_grads = dot(pick, grad_column, ((1,), (0,))) * slot_gates
+    slot_grads = dot(pick, grad_column[:, :width], ((1,), (0,))) * slot_gates
     pattern = jnp.pad(chosen.astype(BF)[:, None, :], ((0, 0), (0, 7), (0, width - span)))
     sent = jnp.concatenate([slot_grads.astype(BF).reshape(n_exp, slots, width), pattern], axis=1)
     received = lax.all_to_all(sent, "exp", split_axis=0, concat_axis=0, tiled=True)
@@ -582,9 +727,9 @@
         attn_heads.reshape(n_exp, heads_own, length, HEAD_SIZE), (0, 2, 1, 3)
     ).reshape(tokens, own_width)
     branch_part = dot(attn_rows, w_output, ((1,), (0,))).astype(BF)
-    branch = lax.psum_scatter(branch_part, "exp", scatter_dimension=0, tiled=True)
+    branch = reduce_rows(branch_part, n_exp, 5)
     wide_in = hidden_in[0].astype(F32)
-    mid = wide_in + branch.astype(F32)
+    mid = wide_in + branch
     second_scale = rms_scale(mid)
     mlp_in = (mid * second_scale * second_gain).astype(BF)
 
@@ -602,13 +747,20 @@
         grad_inner * up_pre * sigmoid_gate * (1.0 + gate_pre * (1.0 - sigmoid_gate))
     ).astype(BF)
     grad_up_pre = (grad_inner * silu_gate).astype(BF)
-    grad_expert_in = dot(grad_gate_pre, w_gate, ((1,), (1,))) + dot(
-        grad_up_pre, w_up, ((1,), (1,))
-    )
-    grad_back = exchange(grad_expert_in)
-    grad_mlp = lax.psum_scatter(
-        dot(pick, grad_back, ((0,), (0,))).astype(BF), "ctx", scatter_dimension=0, tiled=True
-    ).astype(F32)
+    split = width // 2
+
+    def give_back(at):
+        rows = dot(grad_gate_pre, w_gate[at], ((1,), (1,))) + dot(grad_up_pre, w_up[at], ((1,), (1,)))
+        return rows.astype(BF).reshape(n_exp, slots, split)
+
+    def back_sum(rows):
+        part = dot(pick, rows.reshape(n_exp * slots, split), ((0,), (0,))).astype(BF)
+        return lax.psum_scatter(part, "ctx", scatter_dimension=0, tiled=True)
+
+    first = lax.all_to_all(give_back(slice(0, split)), "exp", split_axis=0, concat_axis=0, tiled=True)
+    second = after(give_back(slice(split, width)), first)
+    second = lax.all_to_all(second, "exp", split_axis=0, concat_axis=0, tiled=True)
+    grad_mlp = jnp.concatenate([back_sum(first), back_sum(second)], axis=1).astype(F32)
 
     gradient_wide = grad_out[0].astype(F32)
     mlp_gain_part = jnp.sum(grad_mlp * mid * second_scale, axis=0)
@@ -619,16 +771,18 @@
     expert_out = dot(inner, w_down, ((1,), (0,))).astype(BF)
     out_back = exchange(after(expert_out, branch_all))
     mixed_part = dot(pick_high, out_back, ((0,), (0,))) + dot(pick_low, out_back, ((0,), (0,)))
-    mixed = lax.psum_scatter(mixed_part.astype(BF), "ctx", scatter_dimension=0, tiled=True)
+    mixed_part = mixed_part.astype(BF)
+    mixed = lax.psum_scatter(mixed_part, "ctx", scatter_dimension=0, tiled=True)
     hidden_out = (mid + mixed.astype(F32)).astype(BF)
     grad_down = dot(inner, slot_grads, ((0,), (0,)))
     grad_gate_mat = dot(arrived, grad_gate_pre, ((0,), (0,)))
     grad_up_mat = dot(arrived, grad_up_pre, ((0,), (0,)))
 
     grad_wout = dot(attn_rows, branch_all, ((0,), (0,))).astype(BF)
-    attn_grad = dot(after(branch_all, grad_wout), w_output, ((1,), (1,))).astype(BF)
+    wout_sum = line_sum(grad_wout, n_ctx)
+    attn_grad = dot(after(branch_all, wout_sum), w_output, ((1,), (1,))).astype(BF)
     grad_heads = jnp.transpose(
-        attn_grad.reshape(n_exp, length, heads_own, HEAD_SIZE), (0, 2, 1, 3)
+        after(attn_grad, mixed_part).reshape(n_exp, length, heads_own, HEAD_SIZE), (0, 2, 1, 3)
     ).reshape(n_exp, heads_own * length, HEAD_SIZE)
     deltas = jnp.sum(grad_heads.astype(F32) * attn_heads.astype(F32), axis=-1, keepdims=True)
     probs = jnp.where(causal, jnp.exp(batched(query_rows, keys_all, 2, 2) * factor), 0.0) / totals
@@ -675,7 +829,6 @@
     first_scale = rms_scale(wide_in)
     grad_in = grad_mid + norm_backward(grad_normed, wide_in, first_scale, first_gain)
 
-    wout_sum = line_sum(grad_wout, n_ctx)
     grad_cols = dot(normed, grad_heads_in, ((0,), (0,))).astype(BF)
     gain_parts = jnp.concatenate(
         [

time: 893 us -> 855 us (0.957)
  Pallas kernels: 269 us -> 394 us
  blocking collectives: 79.9 us -> 0 us
  waiting for transfers between devices: 221 us -> 149 us
  local copies, waits for them, and re-layouts: 59.3 us -> 45 us
    pallas_call x0 -> x2, Pallas kernels: none -> 97 us  [the longest x1 66.1 us: reduce_rows(): pl.pallas_call(reduce_kernel, out_shape=jax.ShapeDtypeStruct((rows, width...]
    all_to_all x1, waiting for transfers between devices: 82.7 us -> 0.01 us  [per_device(): lax.all_to_all(sent, 'exp', split_axis=0, concat_axis=0, tiled=True)]
    all_to_all x1 -> x0, blocking collectives: 66 us -> none  [exchange(): rows = lax.all_to_all(rows, 'exp', split_axis=0, concat_axis=0, tiled=True)]
    pallas_call x1, Pallas kernels: 82.2 us -> 114 us  [column_sum(): pl.pallas_call(functools.partial(column_sum_kernel, n_ctx, n_exp, subs),...]
    all_gather x2 -> x1, waiting for transfers between devices: 18.2 us -> 49.4 us  [per_device(): lax.all_gather(jnp.concatenate([grad_out[0], gate_parts], axis=1), 'ctx',...]
    all_to_all x1, waiting for transfers between devices: 30.6 us -> 0.01 us  [exchange(): rows = lax.all_to_all(rows, 'exp', split_axis=0, concat_axis=0, tiled=True)]
    pallas_call x1, Pallas kernels: 88.8 us -> 58.2 us  [line_sum(): pl.pallas_call(functools.partial(line_sum_kernel, n_ctx, chunks), out_sha...]
    pallas_call x2 -> x3, Pallas kernels: 98 us -> 124 us  [gather_rows(): pl.pallas_call(functools.partial(gather_kernel, n_line), out_shape=jax.Sh...]
  transfers between devices with their start and end apart: 13 -> 13, of which waited for: 6 -> 7; matrix products, arithmetic and copies ran while one was open for 19% -> 17% of each run, Pallas kernels for 19% -> 37%
where the time goes in v3:
time: 855 us; the launch traced here: 847 us
  Pallas kernels  394 us (46%)
  matrix products  157 us (18%)
  waiting for transfers between devices  149 us (17%)
  other arithmetic  66.8 us (8%)
  local copies, waits for them, and re-layouts  45 us (5%)
  starting transfers between devices  19.6 us (2%)
  between operations  15.9 us (2%)
    dot_general x24, matrix products, dot(): return lax.dot_general(a, b, (dims, ((), ())), preferred_element_type=F32)  129 us
    pallas_call x3, Pallas kernels, gather_rows(): pl.pallas_call(functools.partial(gather_kernel, n_line), out_shape=jax.Sh...  124 us
    pallas_call x1, Pallas kernels, column_sum(): pl.pallas_call(functools.partial(column_sum_kernel, n_ctx, n_exp, subs),...  114 us
    pallas_call x1, Pallas kernels, reduce_rows(): pl.pallas_call(reduce_kernel, out_shape=jax.ShapeDtypeStruct((rows, width...  66.1 us
    pallas_call x1, Pallas kernels, line_sum(): pl.pallas_call(functools.partial(line_sum_kernel, n_ctx, chunks), out_sha...  58.2 us
    all_gather x1, waiting for transfers between devices, per_device(): lax.all_gather(jnp.concatenate([grad_out[0], gate_parts], axis=1), 'ctx',...  49.4 us
    pallas_call x1, Pallas kernels, spread_columns(): pl.pallas_call(functools.partial(spread_kernel, n_exp, sharers), out_shap...  30.9 us
    all_to_all x1, waiting for transfers between devices, per_device(): lax.all_to_all(second, 'exp', split_axis=0, concat_axis=0, tiled=True)  28.9 us
  transfers between devices with their start and end apart: 13, of which 7 were waited for; matrix products, arithmetic and copies ran while one was open for 17% of the time, Pallas kernels for 37%

profile of v3, /device:TPU:0, one launch (start us, length us, event | category | flops | bytes accessed | tf_op | source)
XLA Modules:
  0.0 847.0 jit_solution(7870597386609843197)
XLA Ops:
  11.3 25.1 %shard_map.246 = bf16[8,1,2,64,2048]{4,3,2,1,0:T(8,128)(2,1)} custom-call(bf16[2,64,2048]{2,1,0:T(8,128)(2,1)} %bitcast.257), custom_call_target="tpu_custom_call" | custom-call | tf_op jit(solution)/shard_map/pallas_call | solution.py:434
  36.5 3.2 fusion
  39.9 30.9 %shard_map.247 = (bf16[8,256,640]{2,1,0:T(8,128)(2,1)S(1)}, bf16[8,16,128]{2,1,0:T(8,128)(2,1)S(1)}) custom-call(bf16[256,4096]{1,0:T(8,128)(2,1)S(1)} %copy-done.4, bf16[4,2,256,128]{3,2,1,0:T(8,128)(2,1)S(1)} %maximum_bitcast_fusion.halves_ref, bf16[16,128]{1,0:T(8,128)(2,1)S(1)} %fusion.122.gains_ref), custom_call_target="tpu_custom_call" | custom-call | tf_op jit(solution)/shard_map/pallas_call | solution.py:572
  74.2 3.4 fusion.2
  77.6 3.4 fusion.143
  86.1 3.1 slice.153
  90.0 2.9 reshape.353
  92.9 3.0 multiply_reduce_fusion.4
  96.7 2.2 multiply_multiply_fusion
  98.9 14.4 %all-gather.3.cloned.1.call-done = bf16[4096,128]{1,0:T(8,128)(2,1)} async-done(((bf16[1024,128]{1,0:T(8,128)(2,1)}), bf16[4096,128]{1,0:T(8,128)(2,1)}) %all-gather.3.cloned.1.call-update) | async-done | bytes 1048592 | tf_op jit(solution)/shard_map/all_gather | solution.py:704
  113.4 49.4 %all-gather.5.cloned.1.call-done = bf16[512,2176]{1,0:T(8,128)(2,1)} async-done(((bf16[128,2176]{1,0:T(8,128)(2,1)}), bf16[512,2176]{1,0:T(8,128)(2,1)}) %all-gather.5.cloned.1.call-update) | async-done | bytes 2228240 | tf_op jit(solution)/shard_map/all_gather | solution.py:648
  167.8 2.1 fusion.37
  169.9 3.4 pad_convert_fusion
  173.3 3.5 copy.166
  176.9 4.7 multiply_convert_fusion
  181.6 3.1 pad_maximum_fusion
  184.7 4.9 all-to-all-start
  189.7 3.6 slice_negate_fusion.1
  193.4 2.5 fusion.91
  198.8 2.2 fusion.5
  201.1 3.7 divide_convert_fusion
  204.7 2.4 copy.160
  207.1 4.3 convolution_convert_fusion.3
  211.5 66.1 %shard_map.248 = f32[128,2048]{1,0:T(8,128)S(1)} custom-call(bf16[8,128,2048]{2,1,0:T(8,128)(2,1)S(1)} %bitcast.247), custom_call_target="tpu_custom_call" | custom-call | tf_op jit(solution)/shard_map/pallas_call | solution.py:514
  280.3 75.6 %shard_map.249 = bf16[8,4,2,64,2048]{4,3,2,1,0:T(8,128)(2,1)} custom-call(bf16[2,64,2048]{2,1,0:T(8,128)(2,1)} %bitcast.289), custom_call_target="tpu_custom_call" | custom-call | tf_op jit(solution)/shard_map/pallas_call | solution.py:434
  357.0 9.0 %convolution_convert_fusion.1 = bf16[8,168,2048]{2,1,0:T(8,128)(2,1)S(1)} fusion(bf16[8,512,2048]{2,1,0:T(8,128)(2,1)} %bitcast.251, s32[8,512]{1,0:T(8,128)S(1)} %convolution_convert_fusion.6, pred[8,512]{1,0:T(8,128)(4,1)S(1)} %compare_bitcast_fusion), kind=kOutput, calls=%fused_computation.22 | convolution fusion | flops 2822701056 | bytes 22302720 | tf_op jit(solution)/shard_map/dot_general | solution.py:737
  366.0 6.3 fusion.24
  372.3 5.9 fusion.26
  378.2 3.0 slice.168
  381.3 11.1 %multiply_convert_fusion.4 = (bf16[1344,768]{1,0:T(8,128)(2,1)S(1)}, bf16[1344,768]{1,0:T(8,128)(2,1)S(1)}, bf16[1344,768]{1,0:T(8,128)(2,1)}) fusion(f32[1344,768]{1,0:T(8,128)} %fusion.26, f32[1344,768]{1,0:T(8,128)} %fusion.24, bf16[1344,2048]{1,0:T(8,128)(2,1)S(1)} %bitcast.263, bf16[1,768,2048]{2,1,0:T(8,128)(2,1)S(1)} %copy-done), kind=kOutput, calls=%fused_computation.36 | convolution fusion | flops 4243341312 | bytes 23101440 | tf_op jit(solution)/shard_map/dot_general | solution.py:55
  392.4 2.3 fusion.51
  394.8 4.0 add_convert_fusion.1
  398.8 4.6 all-to-all-start.1
  403.4 4.5 fusion.48
  408.0 4.0 add_convert_fusion
  412.0 25.1 %all-to-all-done.1 = bf16[8,168,1024]{2,1,0:T(8,128)(2,1)} async-done(((bf16[8,168,1024]{2,1,0:T(8,128)(2,1)}), bf16[8,168,1024]{2,1,0:T(8,128)(2,1)}, u32[]{:S(2)}, u32[]{:S(2)}) %all-to-all-start.1) | async-done | bytes 2752544 | tf_op jit(solution)/shard_map/all_to_all | solution.py:760
  437.0 4.6 all-to-all-start.2
  441.7 4.6 bitcast_convert_fusion.1
  446.3 28.9 %all-to-all-done.2 = bf16[8,168,1024]{2,1,0:T(8,128)(2,1)} async-done(((bf16[8,168,1024]{2,1,0:T(8,128)(2,1)}), bf16[8,168,1024]{2,1,0:T(8,128)(2,1)}, u32[]{:S(2)}, u32[]{:S(2)}) %all-to-all-start.2) | async-done | bytes 2752544 | tf_op jit(solution)/shard_map/all_to_all | solution.py:762
  475.3 4.6 bitcast_convert_fusion
  479.9 7.8 convolution_convert_fusion
  487.6 17.4 %reduce-scatter.8.cloned.1.call-done = bf16[128,1024]{1,0:T(8,128)(2,1)} async-done(((bf16[512,1024]{1,0:T(8,128)(2,1)}), bf16[128,1024]{1,0:T(8,128)(2,1)}) %reduce-scatter.8.cloned.1.call-update) | async-done | bytes 262160 | tf_op jit(solution)/shard_map/reduce_scatter | solution.py:758
  506.8 2.7 fusion.134
  509.5 23.2 %shard_map.250 = bf16[8,1,2,64,2048]{4,3,2,1,0:T(8,128)(2,1)} custom-call(bf16[2,64,2048]{2,1,0:T(8,128)(2,1)} %bitcast.288), custom_call_target="tpu_custom_call" | custom-call | tf_op jit(solution)/shard_map/pallas_call | solution.py:434
  532.7 4.8 all-to-all-start.3
  537.8 4.5 convolution_convert_fusion.4
  542.3 58.2 %shard_map.251 = f32[16,32,2048]{2,1,0:T(8,128)S(1)} custom-call(bf16[16,32,2048]{2,1,0:T(8,128)(2,1)S(1)} %bitcast.248), custom_call_target="tpu_custom_call" | custom-call | tf_op jit(solution)/shard_map/pallas_call | solution.py:196
  600.5 2.0 copy-done.2
  602.5 2.4 convolution_convert_fusion.5
  604.9 5.5 fusion.58
  610.4 7.3 fusion.10
  619.6 4.7 fusion.13
  624.3 5.6 multiply_convert_fusion.2
  639.5 4.4 multiply_reduce_fusion.1
  643.9 2.7 multiply_convert_fusion.9
  647.8 13.7 %reduce-scatter.12.cloned.1.call-done = bf16[1024,128]{1,0:T(8,128)(2,1)} async-done(((bf16[4096,128]{1,0:T(8,128)(2,1)}), bf16[1024,128]{1,0:T(8,128)(2,1)}) %reduce-scatter.12.cloned.1.call-update) | async-done | bytes 262160 | tf_op jit(solution)/shard_map/reduce_scatter | solution.py:804
  665.9 5.0 convolution_convert_fusion.2
  672.5 10.2 %convolution_bitcast_fusion = f32[1,768,2048]{2,1,0:T(8,128)} fusion(bf16[1344,768]{1,0:T(8,128)(2,1)S(1)} %copy-done.76, bf16[1344,2048]{1,0:T(8,128)(2,1)} %bitcast.264), kind=kOutput, calls=%fused_computation.42 | convolution fusion | flops 4227858432 | bytes 13860864 | tf_op jit(solution)/shard_map/dot_general | solution.py:55
  682.8 9.8 %convolution_bitcast_fusion.1 = f32[1,2048,768]{2,1,0:T(8,128)} fusion(bf16[1344,2048]{1,0:T(8,128)(2,1)} %bitcast.261, bf16[1344,768]{1,0:T(8,128)(2,1)S(1)} %copy-done.79), kind=kOutput, calls=%fused_computation.43 | convolution fusion | flops 4227858432 | bytes 13860864 | tf_op jit(solution)/shard_map/dot_general | solution.py:55
  692.6 9.5 %convolution_bitcast_fusion.2 = f32[1,2048,768]{2,1,0:T(8,128)} fusion(bf16[1344,2048]{1,0:T(8,128)(2,1)} %bitcast.262, bf16[1344,768]{1,0:T(8,128)(2,1)S(1)} %copy-done.75), kind=kOutput, calls=%fused_computation.44 | convolution fusion | flops 4227858432 | bytes 13860864 | tf_op jit(solution)/shard_map/dot_general | solution.py:55
  702.4 6.4 fusion.20
  709.1 114.5 %shard_map.252 = bf16[8,2,136,640]{3,2,1,0:T(8,128)(2,1)S(1)} custom-call(bf16[16,136,640]{2,1,0:T(8,128)(2,1)S(1)} %bitcast.244), custom_call_target="tpu_custom_call" | custom-call | tf_op jit(solution)/shard_map/pallas_call | solution.py:261
  833.1 3.4 fusion.82
  836.6 2.1 copy.223
  (281 shorter events, 57.6 us)
Async XLA Ops:
  7.2 374.1 %copy-start = (bf16[1,768,2048]{2,1,0:T(8,128)(2,1)S(1)}, bf16[1,768,2048]{2,1,0:T(8,128)(2,1)}, u32[]{:S(2)}) copy-start(bf16[1,768,2048]{2,1,0:T(8,128)(2,1)} %param.28) | copy-start | bytes 9437188
  7.2 106.2 %all-gather.3.cloned.1.call-start = ((), (), s32[]{:S(2)}) async-start(), calls=%async_computation.9 | async-start | bytes 1310720 | tf_op jit(solution)/shard_map/all_gather | solution.py:704
  36.4 3.3 copy-start.43
  36.4 3.3 copy-start.44
  36.4 3.4 copy-start.62
  36.4 3.4 copy-start.65
  36.4 3.4 copy-start.66
  36.4 3.4 copy-start.67
  36.4 3.4 copy-start.4
  73.9 119.4 %copy-start.32 = (f32[128,128]{1,0:T(8,128)}, f32[128,128]{1,0:T(8,128)S(1)}, u32[]{:S(2)}) copy-start(f32[128,128]{1,0:T(8,128)S(1)} %pad_maximum_fusion.6) | copy-start | bytes 196612
  74.0 119.3 %copy-start.34 = (f32[128,128]{1,0:T(8,128)}, f32[128,128]{1,0:T(8,128)S(1)}, u32[]{:S(2)}) copy-start(f32[128,128]{1,0:T(8,128)S(1)} %pad_maximum_fusion.7) | copy-start | bytes 196612
  74.0 3.5 copy-start.48
  74.1 7.5 copy-start.55
  74.1 3.4 copy-start.46
  74.1 3.4 copy-start.7
  81.2 2.6 copy-start.60
  81.2 2.6 copy-start.61
  83.6 79.1 %all-gather.5.cloned.1.call-start = ((), (), s32[]{:S(2)}) async-start(), calls=%async_computation.10 | async-start | bytes 2785280 | tf_op jit(solution)/shard_map/all_gather | solution.py:648
  90.0 6.0 copy-start.57
  92.9 3.9 copy-start.9
  113.4 83.0 %collective-permute-start = (bf16[4096,128]{1,0:T(8,128)(2,1)}, bf16[4096,128]{1,0:T(8,128)(2,1)}, u32[]{:S(2)}, u32[]{:S(2)}) collective-permute-start(bf16[4096,128]{1,0:T(8,128)(2,1)} %all-gather.3.cloned.1.call-done), channel_id=1, source_target_pairs={{0,1},{1,0},{2,3},{3,2},{4,5},{5,4},{6,7},{7,6},{8,9},{9,8},{10,11... | collective-permute-start | bytes 3145736 | tf_op jit(solution)/shard_map/ppermute | solution.py:705
  184.7 171.2 %all-to-all-start = ((bf16[8,176,2048]{2,1,0:T(8,128)(2,1)}), bf16[8,176,2048]{2,1,0:T(8,128)(2,1)}, u32[]{:S(2)}, u32[]{:S(2)}) async-start(bf16[8,176,2048]{2,1,0:T(8,128)(2,1)} %pad_maximum_fusion), calls=%async_computation | async-start | bytes 11534336 | tf_op jit(solution)/shard_map/all_to_all | solution.py:687
  189.6 3.7 copy-start.54
  189.6 3.7 copy-start.10
  189.6 3.7 copy-start.18
  189.6 3.7 copy-start.58
  193.4 2.8 copy-start.68
  196.2 2.6 copy-start.28
  201.0 3.7 copy-start.73
  211.4 66.1 %copy-start.20 = (bf16[1,128,2048]{2,1,0:T(8,128)(2,1)S(1)}, bf16[1,128,2048]{2,1,0:T(8,128)(2,1)}, u32[]{:S(2)}) copy-start(bf16[1,128,2048]{2,1,0:T(8,128)(2,1)} %param.15) | copy-start | bytes 1572868
  357.0 9.0 %copy-start.70 = (bf16[1,2048,768]{2,1,0:T(8,128)(2,1)S(1)}, bf16[1,2048,768]{2,1,0:T(8,128)(2,1)}, u32[]{:S(2)}) copy-start(bf16[1,2048,768]{2,1,0:T(8,128)(2,1)} %param.27) | copy-start | bytes 9437188
  365.9 6.4 copy-start.22
  365.9 6.4 copy-start.69
  381.3 11.2 %copy-start.23 = (bf16[8,168,2048]{2,1,0:T(8,128)(2,1)}, bf16[8,168,2048]{2,1,0:T(8,128)(2,1)S(1)}, u32[]{:S(2)}) copy-start(bf16[8,168,2048]{2,1,0:T(8,128)(2,1)S(1)} %slice.168) | copy-start | bytes 16515076
  398.8 38.3 %all-to-all-start.1 = ((bf16[8,168,1024]{2,1,0:T(8,128)(2,1)}), bf16[8,168,1024]{2,1,0:T(8,128)(2,1)}, u32[]{:S(2)}, u32[]{:S(2)}) async-start(bf16[8,168,1024]{2,1,0:T(8,128)(2,1)} %bitcast.285), calls=%async_computation.1 | async-start | bytes 5505024 | tf_op jit(solution)/shard_map/all_to_all | solution.py:760
  403.4 4.6 copy-start.71
  403.4 4.6 copy-start.78
  437.0 4.6 copy-start.53
  437.0 38.2 %all-to-all-start.2 = ((bf16[8,168,1024]{2,1,0:T(8,128)(2,1)}), bf16[8,168,1024]{2,1,0:T(8,128)(2,1)}, u32[]{:S(2)}, u32[]{:S(2)}) async-start(bf16[8,168,1024]{2,1,0:T(8,128)(2,1)} %bitcast.284), calls=%async_computation.3 | async-start | bytes 5505024 | tf_op jit(solution)/shard_map/all_to_all | solution.py:762
  441.6 46.0 %reduce-scatter.6.cloned.1.call-start = ((), (), s32[]{:S(2)}) async-start(), calls=%async_computation.11 | async-start | bytes 1310720 | tf_op jit(solution)/shard_map/reduce_scatter | solution.py:758
  446.3 58.8 %reduce-scatter.8.cloned.1.call-start = ((), (), s32[]{:S(2)}) async-start(), calls=%async_computation.12 | async-start | bytes 1310720 | tf_op jit(solution)/shard_map/reduce_scatter | solution.py:758
  532.6 5.1 copy-start.39
  532.7 72.2 %all-to-all-start.3 = ((bf16[8,168,2048]{2,1,0:T(8,128)(2,1)}), bf16[8,168,2048]{2,1,0:T(8,128)(2,1)}, u32[]{:S(2)}, u32[]{:S(2)}) async-start(bf16[8,168,2048]{2,1,0:T(8,128)(2,1)} %bitcast.265), calls=%async_computation.5 | async-start | bytes 11010048 | tf_op jit(solution)/shard_map/all_to_all | solution.py:681
  537.5 124.0 %reduce-scatter.12.cloned.1.call-start = ((), (), s32[]{:S(2)}) async-start(), calls=%async_computation.14 | async-start | bytes 1310720 | tf_op jit(solution)/shard_map/reduce_scatter | solution.py:804
  542.3 60.2 %copy-start.26 = (bf16[8,1,2,64,2048]{4,3,2,1,0:T(8,128)(2,1)S(1)}, bf16[8,1,2,64,2048]{4,3,2,1,0:T(8,128)(2,1)}, u32[]{:S(2)}) copy-start(bf16[8,1,2,64,2048]{4,3,2,1,0:T(8,128)(2,1)} %shard_map.250) | copy-start | bytes 12582916
  542.3 60.2 %copy-start.72 = (bf16[512,2048]{1,0:T(8,128)(2,1)S(1)}, bf16[512,2048]{1,0:T(8,128)(2,1)}, u32[]{:S(2)}) copy-start(bf16[512,2048]{1,0:T(8,128)(2,1)} %param.24) | copy-start | bytes 6291460
  619.6 4.7 copy-start.38
  624.3 5.7 copy-start.29
  631.6 2.7 collective-permute-start.1
  635.7 195.8 %reduce-scatter.14.cloned.1.call-start = ((), (), s32[]{:S(2)}) async-start(), calls=%async_computation.15 | async-start | bytes 4718592 | tf_op jit(solution)/shard_map/reduce_scatter | solution.py:827
  646.6 16.2 %copy-start.51 = (f32[1024]{0:T(1024)S(1)}, f32[1024]{0:T(1024)}, u32[]{:S(2)}) copy-start(f32[1024]{0:T(1024)} %copy-done.50) | copy-start | bytes 12292
  646.6 16.2 %copy-start.56 = (f32[128]{0:T(128)S(1)}, f32[128]{0:T(128)}, u32[]{:S(2)}) copy-start(f32[128]{0:T(128)} %copy-done.55) | copy-start | bytes 1540
  662.5 3.4 copy-start.8
  662.5 3.4 copy-start.40
  670.9 162.1 %reduce-scatter.10.cloned.1.call-start = ((), (), s32[]{:S(2)}) async-start(), calls=%async_computation.13 | async-start | bytes 2621440 | tf_op jit(solution)/shard_map/reduce_scatter | solution.py:775
  672.5 10.2 %copy-start.79 = (bf16[1344,768]{1,0:T(8,128)(2,1)S(1)}, bf16[1344,768]{1,0:T(8,128)(2,1)}, u32[]{:S(2)}) copy-start(bf16[1344,768]{1,0:T(8,128)(2,1)} %copy-done.77) | copy-start | bytes 6193156
  682.8 9.8 %copy-start.75 = (bf16[1344,768]{1,0:T(8,128)(2,1)S(1)}, bf16[1344,768]{1,0:T(8,128)(2,1)}, u32[]{:S(2)}) copy-start(bf16[1344,768]{1,0:T(8,128)(2,1)} %copy-done.74) | copy-start | bytes 6193156
  692.6 9.8 %copy-start.47 = (f32[1,2,8,128]{3,1,2,0:T(2,128)S(1)}, f32[1,2,8,128]{3,1,2,0:T(2,128)}, u32[]{:S(2)}) copy-start(f32[1,2,8,128]{3,1,2,0:T(2,128)} %copy-done.46) | copy-start | bytes 24580
  826.5 3.7 copy-start.16
  826.5 3.2 copy-start.5
  829.7 3.4 copy-start.13
  829.7 3.4 copy-start.30
  833.1 3.4 copy-start.3
  836.5 3.4 copy-start.1
  (29 other events, 46.2 us)
Sparse Core Ops, SparseCore 0:
  83.7 29.5 all-gather.2
  115.5 47.1 all-gather.4
  446.4 27.2 reduce-scatter.5
  480.0 25.0 reduce-scatter.7
  635.8 25.5 reduce-scatter.11
  671.1 49.6 reduce-scatter.13
  723.1 75.6 reduce-scatter.9

commit v4 on v3

--- a/solution.py
+++ b/solution.py
@@ -253,7 +253,7 @@
     lax.fori_loop(0, chunks, drain, 0)
 
 
-def column_sum(x, n_ctx, n_exp, subs=2):
+def column_sum(x, n_ctx, n_exp, subs=4):
     total, width = x.shape
     rows = total // n_exp // subs
     chunks = n_exp * subs
@@ -649,10 +649,11 @@
         jnp.concatenate([grad_out[0], gate_parts], axis=1), "ctx",
         axis=0, tiled=True,
     )
-    gate_parts = grad_column[:, width : width + 3 * n_all].astype(F32)
-    column_gates = (
-        gate_parts[:, :n_all] + gate_parts[:, n_all : 2 * n_all] + gate_parts[:, 2 * n_all :]
-    )
+    gate_parts = grad_column[:, width : width + 3 * n_all].reshape(n_ctx * length, 3, n_all)
+    gate_parts = lax.dynamic_slice(
+        gate_parts, (0, 0, ctx_index * n_exp), (n_ctx * length, 3, n_exp)
+    )
+    gate_parts = jnp.transpose(gate_parts, (2, 1, 0))
     span = n_ctx * length
     slots = round_up(n_ctx * max(2, length * TOPK * 4 // (3 * n_all)), 8)
     below = (
@@ -665,28 +666,26 @@
             rank[:, None, :] == jnp.arange(slots, dtype=jnp.int32)[None, :, None]
         )
 
-    plane_gates = jnp.transpose(
-        lax.dynamic_slice(column_gates, (0, ctx_index * n_exp), (span, n_exp))
-    )
-    chosen = plane_gates > 0.0
-    is_slot = in_slots(chosen)
-    pick = is_slot.astype(BF).reshape(n_exp * slots, span)
-    weighted = jnp.where(is_slot, plane_gates[:, None, :], 0.0).reshape(n_exp * slots, span)
-    slot_gates = jnp.sum(weighted, axis=1, keepdims=True)
-    high = lax.reduce_precision(weighted, 8, 7)
-    pick_high, pick_low = high.astype(BF), (weighted - high).astype(BF)
+    pick = in_slots(gate_parts[:, 0] > 0.0).astype(BF).reshape(n_exp * slots, span)
 
     def exchange(rows):
         rows = rows.astype(BF).reshape(n_exp, slots, width)
         rows = lax.all_to_all(rows, "exp", split_axis=0, concat_axis=0, tiled=True)
         return rows.reshape(n_exp * slots, width)
 
-    slot_grads = dot(pick, grad_column[:, :width], ((1,), (0,))) * slot_gates
-    pattern = jnp.pad(chosen.astype(BF)[:, None, :], ((0, 0), (0, 7), (0, width - span)))
-    sent = jnp.concatenate([slot_grads.astype(BF).reshape(n_exp, slots, width), pattern], axis=1)
+    packed_rows = dot(pick, grad_column[:, :width], ((1,), (0,))).astype(BF)
+    gate_parts = jnp.pad(gate_parts, ((0, 0), (0, 5), (0, width - span)))
+    sent = jnp.concatenate(
+        [packed_rows.reshape(n_exp, slots, width), gate_parts], axis=1,
+    )
     received = lax.all_to_all(sent, "exp", split_axis=0, concat_axis=0, tiled=True)
-    slot_grads = received[:, :slots].reshape(n_exp * slots, width)
-    take = in_slots(received[:, slots, :span] > 0.5).astype(BF)
+    own_gates = jnp.sum(received[:, slots : slots + 3, :span].astype(F32), axis=1)
+    taken = in_slots(own_gates > 0.0)
+    take = taken.astype(BF)
+    slot_gates = jnp.sum(jnp.where(taken, own_gates[:, None, :], 0.0), axis=2)
+    slot_grads = slot_gates[:, :, None] * received[:, :slots].astype(F32)
+    slot_grads = slot_grads.astype(BF).reshape(n_exp * slots, width)
+    slot_gates = slot_gates.reshape(n_exp * slots, 1)
 
     positions = ctx_index * length + jnp.arange(length, dtype=jnp.int32)
     cosine, sine = rope_tables(positions)
@@ -695,7 +694,7 @@
     wide_all = hidden_all.astype(F32)
     normed = (wide_all * rms_scale(wide_all) * first_gain).astype(BF)
     projected = dot(normed, weight_cols, ((1,), (0,)))
-    queries = projected[:, :own_width].reshape(n_exp, length, heads_own, HEAD_SIZE)
+    queries = after(projected[:, :own_width], sent).reshape(n_exp, length, heads_own, HEAD_SIZE)
     own_raw = projected[:, own_width:].reshape(n_exp, length, HEAD_SIZE)
     query_scale, key_scale = rms_scale(queries), rms_scale(own_raw)
     query_rot = rotate(queries * query_scale * q_gain, cos_q, sin_q).astype(BF)
@@ -768,10 +767,9 @@
     branch_all = gather_rows(grad_mid.astype(BF), 1, n_exp, 4)
     branch_all = branch_all.reshape(tokens, width)
 
-    expert_out = dot(inner, w_down, ((1,), (0,))).astype(BF)
-    out_back = exchange(after(expert_out, branch_all))
-    mixed_part = dot(pick_high, out_back, ((0,), (0,))) + dot(pick_low, out_back, ((0,), (0,)))
-    mixed_part = mixed_part.astype(BF)
+    expert_out = slot_gates * dot(inner, w_down, ((1,), (0,)))
+    out_back = exchange(after(expert_out.astype(BF), branch_all))
+    mixed_part = dot(pick, out_back, ((0,), (0,))).astype(BF)
     mixed = lax.psum_scatter(mixed_part, "ctx", scatter_dimension=0, tiled=True)
     hidden_out = (mid + mixed.astype(F32)).astype(BF)
     grad_down = dot(inner, slot_grads, ((0,), (0,)))
@@ -801,10 +799,8 @@
     partner = lax.ppermute(partner, "exp", pairs)
     own_part = jnp.where(holds_keys, key_part, value_part) + partner.astype(F32)
     own_part = own_part.astype(BF).reshape(n_ctx, tokens, HEAD_SIZE)
-    own_sums = lax.psum_scatter(
-        own_part.reshape(n_ctx * tokens, HEAD_SIZE),
-        "ctx", scatter_dimension=0, tiled=True,
-    ).astype(F32).reshape(n_exp, length, HEAD_SIZE)
+    own_part = lax.all_to_all(own_part, "ctx", split_axis=0, concat_axis=0, tiled=True)
+    own_sums = jnp.sum(own_part.astype(F32), axis=0).reshape(n_exp, length, HEAD_SIZE)
     grad_query_rot = batched(grad_scores, keys_all, 2, 1)
     grad_query_unit = rotation_backward(
         jnp.transpose(
@@ -839,11 +835,11 @@
         axis=1,
     )
     gain_parts = jnp.pad(gain_parts, ((0, 0), (0, packed_width - cut - 2 * small)))[:, None, :]
-    gain_parts = jnp.pad(gain_parts, ((0, 0), (0, 15), (0, 0))).astype(BF)
+    gain_parts = jnp.pad(gain_parts, ((0, 0), (0, 31), (0, 0))).astype(BF)
     grad_cols = jnp.concatenate(
         [grad_cols.reshape(n_exp, rows_own, packed_width), gain_parts], axis=1
     )
-    grad_cols = column_sum(grad_cols.reshape(n_exp * (rows_own + 16), packed_width), n_ctx, n_exp)
+    grad_cols = column_sum(grad_cols.reshape(n_exp * (rows_own + 32), packed_width), n_ctx, n_exp)
     own_gains = jnp.sum(grad_cols[:, rows_own].astype(F32), axis=0)
     grad_cols = grad_cols[:, :rows_own]
     to_row = jnp.transpose(grad_cols, (1, 0, 2))

time: 855 us -> 857 us (level)
  local copies, waits for them, and re-layouts: 45 us -> 35 us
  waiting for transfers between devices: 149 us -> 158 us
    reduce_scatter x1 -> x0, waiting for transfers between devices: 13.7 us -> none  [per_device(): lax.psum_scatter(own_part.reshape(n_ctx * tokens, HEAD_SIZE), 'ctx', scat...]
    all_to_all x0 -> x1, waiting for transfers between devices: none -> 13.5 us  [per_device(): lax.all_to_all(own_part, 'ctx', split_axis=0, concat_axis=0, tiled=True)]
    pallas_call x3, Pallas kernels: 124 us -> 134 us  [gather_rows(): pl.pallas_call(functools.partial(gather_kernel, n_line), out_shape=jax.Sh...]
    all_gather x1, waiting for transfers between devices: 14.4 us -> 23.3 us  [per_device(): own_half = lax.all_gather(own_half, 'ctx', axis=0, tiled=True)]
    dot_general x24 -> x23, matrix products: 129 us -> 123 us  [dot(): return lax.dot_general(a, b, (dims, ((), ())), preferred_element_type=F32)]
    unnamed x171 -> x166, local copies, waits for them, and re-layouts: 20.7 us -> 17.9 us
  transfers between devices with their start and end apart: 13 -> 13, of which waited for: 7 -> 6; matrix products, arithmetic and copies ran while one was open for 17% -> 16% of each run, Pallas kernels for 37% -> 38%
where the time goes in v4:
time: 857 us; the launch traced here: 848 us
  Pallas kernels  399 us (47%)
  waiting for transfers between devices  158 us (18%)
  matrix products  150 us (18%)
  other arithmetic  65.7 us (8%)
  local copies, waits for them, and re-layouts  35 us (4%)
  starting transfers between devices  23.8 us (3%)
  between operations  16.1 us (2%)
    pallas_call x3, Pallas kernels, gather_rows(): pl.pallas_call(functools.partial(gather_kernel, n_line), out_shape=jax.Sh...  134 us
    dot_general x23, matrix products, dot(): return lax.dot_general(a, b, (dims, ((), ())), preferred_element_type=F32)  123 us
    pallas_call x1, Pallas kernels, column_sum(): pl.pallas_call(functools.partial(column_sum_kernel, n_ctx, n_exp, subs),...  115 us
    pallas_call x1, Pallas kernels, reduce_rows(): pl.pallas_call(reduce_kernel, out_shape=jax.ShapeDtypeStruct((rows, width...  60.1 us
    pallas_call x1, Pallas kernels, line_sum(): pl.pallas_call(functools.partial(line_sum_kernel, n_ctx, chunks), out_sha...  58.4 us
    all_gather x1, waiting for transfers between devices, per_device(): lax.all_gather(jnp.concatenate([grad_out[0], gate_parts], axis=1), 'ctx',...  49.4 us
    pallas_call x1, Pallas kernels, spread_columns(): pl.pallas_call(functools.partial(spread_kernel, n_exp, sharers), out_shap...  30.9 us
    all_to_all x1, waiting for transfers between devices, per_device(): lax.all_to_all(second, 'exp', split_axis=0, concat_axis=0, tiled=True)  28.9 us
  transfers between devices with their start and end apart: 13, of which 6 were waited for; matrix products, arithmetic and copies ran while one was open for 16% of the time, Pallas kernels for 38%

profile of v4, /device:TPU:0, one launch (start us, length us, event | category | flops | bytes accessed | tf_op | source)
XLA Modules:
  0.0 847.5 jit_solution(4128219331464293851)
XLA Ops:
  11.3 25.1 %shard_map.246 = bf16[8,1,2,64,2048]{4,3,2,1,0:T(8,128)(2,1)} custom-call(bf16[2,64,2048]{2,1,0:T(8,128)(2,1)} %bitcast.250), custom_call_target="tpu_custom_call" | custom-call | tf_op jit(solution)/shard_map/pallas_call | solution.py:434
  36.5 3.2 fusion.1
  39.9 30.9 %shard_map.247 = (bf16[8,256,640]{2,1,0:T(8,128)(2,1)S(1)}, bf16[8,16,128]{2,1,0:T(8,128)(2,1)S(1)}) custom-call(bf16[256,4096]{1,0:T(8,128)(2,1)S(1)} %copy-done.4, bf16[4,2,256,128]{3,2,1,0:T(8,128)(2,1)S(1)} %maximum_bitcast_fusion.halves_ref, bf16[16,128]{1,0:T(8,128)(2,1)S(1)} %fusion.112.gains_ref), custom_call_target="tpu_custom_call" | custom-call | tf_op jit(solution)/shard_map/pallas_call | solution.py:572
  73.1 3.4 fusion.3
  76.5 3.4 fusion.129
  83.0 1.9 pad_maximum_fusion.3
  84.9 3.1 slice.145
  89.0 23.3 %all-gather.5.cloned.1.call-done = bf16[4096,128]{1,0:T(8,128)(2,1)} async-done(((bf16[1024,128]{1,0:T(8,128)(2,1)}), bf16[4096,128]{1,0:T(8,128)(2,1)}) %all-gather.5.cloned.1.call-update) | async-done | bytes 1048592 | tf_op jit(solution)/shard_map/all_gather | solution.py:703
  112.3 49.4 %all-gather.3.cloned.1.call-done = bf16[512,2176]{1,0:T(8,128)(2,1)} async-done(((bf16[128,2176]{1,0:T(8,128)(2,1)}), bf16[512,2176]{1,0:T(8,128)(2,1)}) %all-gather.3.cloned.1.call-update) | async-done | bytes 2228240 | tf_op jit(solution)/shard_map/all_gather | solution.py:648
  163.5 4.8 convolution_convert_fusion
  168.3 3.1 fusion.5
  171.4 4.9 all-to-all-start
  180.1 2.9 reshape.341
  183.0 2.9 multiply_reduce_fusion.4
  188.7 2.5 fusion.82
  191.5 2.2 fusion.7
  193.8 3.6 divide_convert_fusion
  197.4 2.4 copy.105
  199.8 4.3 convolution_convert_fusion.3
  204.1 60.1 %shard_map.248 = f32[128,2048]{1,0:T(8,128)S(1)} custom-call(bf16[8,128,2048]{2,1,0:T(8,128)(2,1)S(1)} %bitcast.240), custom_call_target="tpu_custom_call" | custom-call | tf_op jit(solution)/shard_map/pallas_call | solution.py:514
  267.0 86.1 %shard_map.249 = bf16[8,4,2,64,2048]{4,3,2,1,0:T(8,128)(2,1)} custom-call(bf16[2,64,2048]{2,1,0:T(8,128)(2,1)} %bitcast.281), custom_call_target="tpu_custom_call" | custom-call | tf_op jit(solution)/shard_map/pallas_call | solution.py:434
  354.9 8.9 %convolution_convert_fusion.1 = bf16[8,168,2048]{2,1,0:T(8,128)(2,1)S(1)} fusion(bf16[8,512,2048]{2,1,0:T(8,128)(2,1)} %bitcast.244, s32[8,512]{1,0:T(8,128)S(1)} %convolution_convert_fusion.6, pred[8,512]{1,0:T(8,128)(4,1)S(1)} %broadcast_compare_fusion), kind=kOutput, calls=%fused_computation.21 | convolution fusion | flops 2822701056 | bytes 22302720 | tf_op jit(solution)/shard_map/dot_general | solution.py:736
  363.9 5.9 fusion.24
  369.8 5.9 fusion.26
  375.8 3.5 multiply_convert_fusion
  379.3 11.1 %multiply_convert_fusion.5 = (bf16[1344,768]{1,0:T(8,128)(2,1)S(1)}, bf16[1344,768]{1,0:T(8,128)(2,1)S(1)}, bf16[1344,768]{1,0:T(8,128)(2,1)}) fusion(f32[1344,768]{1,0:T(8,128)} %fusion.26, f32[1344,768]{1,0:T(8,128)} %fusion.24, bf16[1344,2048]{1,0:T(8,128)(2,1)S(1)} %bitcast.257, bf16[1,768,2048]{2,1,0:T(8,128)(2,1)S(1)} %copy-done), kind=kOutput, calls=%fused_computation.34 | convolution fusion | flops 4243341312 | bytes 23101440 | tf_op jit(solution)/shard_map/dot_general | solution.py:55
  390.4 2.3 fusion.51
  392.8 4.0 add_convert_fusion.1
  396.8 4.6 all-to-all-start.1
  401.5 4.5 fusion.48
  406.0 4.0 add_convert_fusion
  410.0 25.1 %all-to-all-done.1 = bf16[8,168,1024]{2,1,0:T(8,128)(2,1)} async-done(((bf16[8,168,1024]{2,1,0:T(8,128)(2,1)}), bf16[8,168,1024]{2,1,0:T(8,128)(2,1)}, u32[]{:S(2)}, u32[]{:S(2)}) %all-to-all-start.1) | async-done | bytes 2752544 | tf_op jit(solution)/shard_map/all_to_all | solution.py:759
  435.1 4.4 all-to-all-start.2
  439.6 4.6 bitcast_convert_fusion.2
  444.3 28.9 %all-to-all-done.2 = bf16[8,168,1024]{2,1,0:T(8,128)(2,1)} async-done(((bf16[8,168,1024]{2,1,0:T(8,128)(2,1)}), bf16[8,168,1024]{2,1,0:T(8,128)(2,1)}, u32[]{:S(2)}, u32[]{:S(2)}) %all-to-all-start.2) | async-done | bytes 2752544 | tf_op jit(solution)/shard_map/all_to_all | solution.py:761
  473.2 4.6 bitcast_convert_fusion.1
  477.9 7.8 multiply_convert_fusion.1
  485.7 17.3 %reduce-scatter.7.cloned.1.call-done = bf16[128,1024]{1,0:T(8,128)(2,1)} async-done(((bf16[512,1024]{1,0:T(8,128)(2,1)}), bf16[128,1024]{1,0:T(8,128)(2,1)}) %reduce-scatter.7.cloned.1.call-update) | async-done | bytes 262160 | tf_op jit(solution)/shard_map/reduce_scatter | solution.py:757
  503.0 1.7 fusion.78
  504.7 2.7 fusion.122
  507.4 23.2 %shard_map.250 = bf16[8,1,2,64,2048]{4,3,2,1,0:T(8,128)(2,1)} custom-call(bf16[2,64,2048]{2,1,0:T(8,128)(2,1)} %bitcast.280), custom_call_target="tpu_custom_call" | custom-call | tf_op jit(solution)/shard_map/pallas_call | solution.py:434
  530.6 5.2 all-to-all-start.3
  535.8 4.5 convolution_convert_fusion.4
  540.4 58.4 %shard_map.251 = f32[16,32,2048]{2,1,0:T(8,128)S(1)} custom-call(bf16[16,32,2048]{2,1,0:T(8,128)(2,1)S(1)} %bitcast.241), custom_call_target="tpu_custom_call" | custom-call | tf_op jit(solution)/shard_map/pallas_call | solution.py:196
  598.8 2.0 copy-done.2
  600.8 2.4 convolution_convert_fusion.5
  603.2 7.2 bitcast_convert_fusion
  612.3 4.7 fusion.14
  617.0 5.4 multiply_convert_fusion.3
  626.5 2.7 multiply_bitcast_fusion
  630.5 4.2 all-to-all-start.4
  634.8 4.0 fusion.124
  638.8 4.4 multiply_reduce_fusion.1
  643.3 2.7 multiply_convert_fusion.10
  647.1 13.5 %all-to-all-done.4 = bf16[4,1024,128]{2,1,0:T(8,128)(2,1)} async-done(((bf16[4,1024,128]{2,1,0:T(8,128)(2,1)}), bf16[4,1024,128]{2,1,0:T(8,128)(2,1)}, u32[]{:S(2)}, u32[]{:S(2)}) %all-to-all-start.4) | async-done | bytes 1048608 | tf_op jit(solution)/shard_map/all_to_all | solution.py:802
  662.4 1.7 multiply_reduce_fusion.8
  665.5 5.0 convolution_convert_fusion.2
  672.2 9.9 %convolution_bitcast_fusion = f32[1,768,2048]{2,1,0:T(8,128)} fusion(bf16[1344,768]{1,0:T(8,128)(2,1)S(1)} %copy-done.73, bf16[1344,2048]{1,0:T(8,128)(2,1)} %bitcast.258), kind=kOutput, calls=%fused_computation.39 | convolution fusion | flops 4227858432 | bytes 13860864 | tf_op jit(solution)/shard_map/dot_general | solution.py:55
  682.1 9.9 %convolution_bitcast_fusion.1 = f32[1,2048,768]{2,1,0:T(8,128)} fusion(bf16[1344,2048]{1,0:T(8,128)(2,1)} %bitcast.255, bf16[1344,768]{1,0:T(8,128)(2,1)S(1)} %copy-done.76), kind=kOutput, calls=%fused_computation.40 | convolution fusion | flops 4227858432 | bytes 13860864 | tf_op jit(solution)/shard_map/dot_general | solution.py:55
  692.0 9.6 %convolution_bitcast_fusion.2 = f32[1,2048,768]{2,1,0:T(8,128)} fusion(bf16[1344,2048]{1,0:T(8,128)(2,1)} %bitcast.256, bf16[1344,768]{1,0:T(8,128)(2,1)S(1)} %copy-done.72), kind=kOutput, calls=%fused_computation.41 | convolution fusion | flops 4227858432 | bytes 13860864 | tf_op jit(solution)/shard_map/dot_general | solution.py:55
  701.9 6.3 fusion.20
  708.5 115.3 %shard_map.252 = bf16[8,4,72,640]{3,2,1,0:T(8,128)(2,1)S(1)} custom-call(bf16[32,72,640]{2,1,0:T(8,128)(2,1)S(1)} %bitcast.237), custom_call_target="tpu_custom_call" | custom-call | tf_op jit(solution)/shard_map/pallas_call | solution.py:261
  833.4 3.4 fusion.73
  836.8 2.1 copy.157
  (272 shorter events, 48.0 us)
Async XLA Ops:
  7.2 372.1 %copy-start = (bf16[1,768,2048]{2,1,0:T(8,128)(2,1)S(1)}, bf16[1,768,2048]{2,1,0:T(8,128)(2,1)}, u32[]{:S(2)}) copy-start(bf16[1,768,2048]{2,1,0:T(8,128)(2,1)} %param.28) | copy-start | bytes 9437188
  7.2 105.1 %all-gather.5.cloned.1.call-start = ((), (), s32[]{:S(2)}) async-start(), calls=%async_computation.10 | async-start | bytes 1310720 | tf_op jit(solution)/shard_map/all_gather | solution.py:703
  36.4 3.3 copy-start.39
  36.4 3.4 copy-start.60
  36.4 3.4 copy-start.63
  36.4 3.4 copy-start.64
  36.4 3.4 copy-start.65
  36.4 3.4 copy-start.4
  72.8 115.9 %copy-start.29 = (f32[128,128]{1,0:T(8,128)}, f32[128,128]{1,0:T(8,128)S(1)}, u32[]{:S(2)}) copy-start(f32[128,128]{1,0:T(8,128)S(1)} %pad_maximum_fusion.5) | copy-start | bytes 196612
  72.9 115.8 %copy-start.31 = (f32[128,128]{1,0:T(8,128)}, f32[128,128]{1,0:T(8,128)S(1)}, u32[]{:S(2)}) copy-start(f32[128,128]{1,0:T(8,128)S(1)} %pad_maximum_fusion.6) | copy-start | bytes 196612
  72.9 3.5 copy-start.44
  73.0 7.5 copy-start.50
  73.0 3.4 copy-start.42
  73.0 3.4 copy-start.7
  82.5 79.1 %all-gather.3.cloned.1.call-start = ((), (), s32[]{:S(2)}) async-start(), calls=%async_computation.9 | async-start | bytes 2785280 | tf_op jit(solution)/shard_map/all_gather | solution.py:648
  88.2 100.5 %copy-start.52 = (f32[128]{0:T(128)}, f32[128]{0:T(128)S(1)}, u32[]{:S(2)}) copy-start(f32[128]{0:T(128)S(1)} %mul.435) | copy-start | bytes 1540
  112.3 64.0 %collective-permute-start = (bf16[4096,128]{1,0:T(8,128)(2,1)}, bf16[4096,128]{1,0:T(8,128)(2,1)}, u32[]{:S(2)}, u32[]{:S(2)}) collective-permute-start(bf16[4096,128]{1,0:T(8,128)(2,1)} %all-gather.5.cloned.1.call-done), channel_id=1, source_target_pairs={{0,1},{1,0},{2,3},{3,2},{4,5},{5,4},{6,7},{7,6},{8,9},{9,8},{10,11... | collective-permute-start | bytes 3145736 | tf_op jit(solution)/shard_map/ppermute | solution.py:704
  162.9 5.4 copy-start.48
  171.4 181.8 %all-to-all-start = ((bf16[8,176,2048]{2,1,0:T(8,128)(2,1)}), bf16[8,176,2048]{2,1,0:T(8,128)(2,1)}, u32[]{:S(2)}, u32[]{:S(2)}) async-start(bf16[8,176,2048]{2,1,0:T(8,128)(2,1)} %fusion.5), calls=%async_computation | async-start | bytes 11534336 | tf_op jit(solution)/shard_map/all_to_all | solution.py:681
  193.8 3.6 copy-start.70
  204.1 60.2 %copy-start.18 = (bf16[1,128,2048]{2,1,0:T(8,128)(2,1)S(1)}, bf16[1,128,2048]{2,1,0:T(8,128)(2,1)}, u32[]{:S(2)}) copy-start(bf16[1,128,2048]{2,1,0:T(8,128)(2,1)} %param.15) | copy-start | bytes 1572868
  265.1 239.6 %copy-start.54 = (f32[128]{0:T(128)}, f32[128]{0:T(128)S(1)}, u32[]{:S(2)}) copy-start(f32[128]{0:T(128)S(1)} %add_rsqrt_fusion.4) | copy-start | bytes 1540
  354.9 9.0 %copy-start.67 = (bf16[1,2048,768]{2,1,0:T(8,128)(2,1)S(1)}, bf16[1,2048,768]{2,1,0:T(8,128)(2,1)}, u32[]{:S(2)}) copy-start(bf16[1,2048,768]{2,1,0:T(8,128)(2,1)} %param.27) | copy-start | bytes 9437188
  363.9 6.0 copy-start.20
  363.9 6.0 copy-start.66
  379.3 11.2 %copy-start.21 = (bf16[8,168,2048]{2,1,0:T(8,128)(2,1)}, bf16[8,168,2048]{2,1,0:T(8,128)(2,1)S(1)}, u32[]{:S(2)}) copy-start(bf16[8,168,2048]{2,1,0:T(8,128)(2,1)S(1)} %multiply_convert_fusion) | copy-start | bytes 16515076
  396.8 38.3 %all-to-all-start.1 = ((bf16[8,168,1024]{2,1,0:T(8,128)(2,1)}), bf16[8,168,1024]{2,1,0:T(8,128)(2,1)}, u32[]{:S(2)}, u32[]{:S(2)}) async-start(bf16[8,168,1024]{2,1,0:T(8,128)(2,1)} %bitcast.278), calls=%async_computation.1 | async-start | bytes 5505024 | tf_op jit(solution)/shard_map/all_to_all | solution.py:759
  401.4 4.6 copy-start.68
  401.5 4.6 copy-start.75
  410.0 29.6 %copy-start.49 = (s32[8,512]{1,0:T(8,128)S(1)}, s32[8,512]{1,0:T(8,128)}, u32[]{:S(2)}) copy-start(s32[8,512]{1,0:T(8,128)} %copy-done.48) | copy-start | bytes 49156
  435.1 38.1 %all-to-all-start.2 = ((bf16[8,168,1024]{2,1,0:T(8,128)(2,1)}), bf16[8,168,1024]{2,1,0:T(8,128)(2,1)}, u32[]{:S(2)}, u32[]{:S(2)}) async-start(bf16[8,168,1024]{2,1,0:T(8,128)(2,1)} %bitcast.277), calls=%async_computation.3 | async-start | bytes 5505024 | tf_op jit(solution)/shard_map/all_to_all | solution.py:761
  439.5 46.1 %reduce-scatter.5.cloned.1.call-start = ((), (), s32[]{:S(2)}) async-start(), calls=%async_computation.11 | async-start | bytes 1310720 | tf_op jit(solution)/shard_map/reduce_scatter | solution.py:757
  444.2 58.8 %reduce-scatter.7.cloned.1.call-start = ((), (), s32[]{:S(2)}) async-start(), calls=%async_computation.12 | async-start | bytes 1310720 | tf_op jit(solution)/shard_map/reduce_scatter | solution.py:757
  504.7 25.8 %copy-start.58 = (f32[128]{0:T(128)}, f32[128]{0:T(128)S(1)}, u32[]{:S(2)}) copy-start(f32[128]{0:T(128)S(1)} %broadcast_multiply_fusion.4) | copy-start | bytes 1540
  530.6 5.2 copy-start.35
  530.6 72.6 %all-to-all-start.3 = ((bf16[8,168,2048]{2,1,0:T(8,128)(2,1)}), bf16[8,168,2048]{2,1,0:T(8,128)(2,1)}, u32[]{:S(2)}, u32[]{:S(2)}) async-start(bf16[8,168,2048]{2,1,0:T(8,128)(2,1)} %bitcast.259), calls=%async_computation.5 | async-start | bytes 11010048 | tf_op jit(solution)/shard_map/all_to_all | solution.py:673
  540.4 60.4 %copy-start.24 = (bf16[8,1,2,64,2048]{4,3,2,1,0:T(8,128)(2,1)S(1)}, bf16[8,1,2,64,2048]{4,3,2,1,0:T(8,128)(2,1)}, u32[]{:S(2)}) copy-start(bf16[8,1,2,64,2048]{4,3,2,1,0:T(8,128)(2,1)} %shard_map.250) | copy-start | bytes 12582916
  540.4 60.4 %copy-start.69 = (bf16[512,2048]{1,0:T(8,128)(2,1)S(1)}, bf16[512,2048]{1,0:T(8,128)(2,1)}, u32[]{:S(2)}) copy-start(bf16[512,2048]{1,0:T(8,128)(2,1)} %param.24) | copy-start | bytes 6291460
  612.3 4.7 copy-start.34
  617.0 5.4 copy-start.27
  624.1 5.1 collective-permute-start.1
  626.5 4.0 copy-start.13
  630.5 30.2 %all-to-all-start.4 = ((bf16[4,1024,128]{2,1,0:T(8,128)(2,1)}), bf16[4,1024,128]{2,1,0:T(8,128)(2,1)}, u32[]{:S(2)}, u32[]{:S(2)}) async-start(bf16[4,1024,128]{2,1,0:T(8,128)(2,1)} %bitcast.69), calls=%async_computation.7 | async-start | bytes 2097152 | tf_op jit(solution)/shard_map/all_to_all | solution.py:802
  634.7 4.1 copy-start.10
  634.7 4.1 copy-start.17
  634.7 4.1 copy-start.30
  634.7 4.1 copy-start.53
  634.8 197.0 %reduce-scatter.11.cloned.1.call-start = ((), (), s32[]{:S(2)}) async-start(), calls=%async_computation.14 | async-start | bytes 4718592 | tf_op jit(solution)/shard_map/reduce_scatter | solution.py:823
  634.8 4.0 copy-start.14
  646.0 16.4 %copy-start.47 = (f32[1024]{0:T(1024)S(1)}, f32[1024]{0:T(1024)}, u32[]{:S(2)}) copy-start(f32[1024]{0:T(1024)} %copy-done.46) | copy-start | bytes 12292
  646.0 16.4 %copy-start.51 = (f32[128]{0:T(128)S(1)}, f32[128]{0:T(128)}, u32[]{:S(2)}) copy-start(f32[128]{0:T(128)} %copy-done.50) | copy-start | bytes 1540
  662.1 3.4 copy-start.8
  662.2 3.4 copy-start.36
  670.6 162.8 %reduce-scatter.9.cloned.1.call-start = ((), (), s32[]{:S(2)}) async-start(), calls=%async_computation.13 | async-start | bytes 2621440 | tf_op jit(solution)/shard_map/reduce_scatter | solution.py:773
  672.2 9.9 %copy-start.76 = (bf16[1344,768]{1,0:T(8,128)(2,1)S(1)}, bf16[1344,768]{1,0:T(8,128)(2,1)}, u32[]{:S(2)}) copy-start(bf16[1344,768]{1,0:T(8,128)(2,1)} %copy-done.74) | copy-start | bytes 6193156
  682.1 9.9 %copy-start.72 = (bf16[1344,768]{1,0:T(8,128)(2,1)S(1)}, bf16[1344,768]{1,0:T(8,128)(2,1)}, u32[]{:S(2)}) copy-start(bf16[1344,768]{1,0:T(8,128)(2,1)} %copy-done.71) | copy-start | bytes 6193156
  691.9 10.0 %copy-start.43 = (f32[1,2,8,128]{3,1,2,0:T(2,128)S(1)}, f32[1,2,8,128]{3,1,2,0:T(2,128)}, u32[]{:S(2)}) copy-start(f32[1,2,8,128]{3,1,2,0:T(2,128)} %copy-done.42) | copy-start | bytes 24580
  826.8 3.7 copy-start.15
  830.0 3.4 copy-start.12
  830.0 3.4 copy-start.28
  830.0 3.4 copy-start.55
  830.0 3.4 copy-start.59
  833.4 3.4 copy-start.3
  836.8 3.4 copy-start.1
  (26 other events, 50.7 us)
Sparse Core Ops, SparseCore 0:
  82.7 29.5 all-gather.4
  114.4 47.1 all-gather.2
  444.3 27.1 reduce-scatter.4
  477.9 25.0 reduce-scatter.6
  670.7 50.2 reduce-scatter.10
  723.2 65.2 reduce-scatter.8

commit v5 on v4

--- a/solution.py
+++ b/solution.py
@@ -674,17 +674,26 @@
         return rows.reshape(n_exp * slots, width)
 
     packed_rows = dot(pick, grad_column[:, :width], ((1,), (0,))).astype(BF)
-    gate_parts = jnp.pad(gate_parts, ((0, 0), (0, 5), (0, width - span)))
-    sent = jnp.concatenate(
-        [packed_rows.reshape(n_exp, slots, width), gate_parts], axis=1,
-    )
+    split = width // 2
+    packed_rows = packed_rows.reshape(n_exp, slots, width)
+    gate_parts = jnp.pad(gate_parts, ((0, 0), (0, 5), (0, split - span)))
+    sent = jnp.concatenate([packed_rows[:, :, :split], gate_parts], axis=1)
     received = lax.all_to_all(sent, "exp", split_axis=0, concat_axis=0, tiled=True)
+    received_rest = lax.all_to_all(
+        packed_rows[:, :, split:], "exp",
+        split_axis=0, concat_axis=0, tiled=True,
+    )
     own_gates = jnp.sum(received[:, slots : slots + 3, :span].astype(F32), axis=1)
     taken = in_slots(own_gates > 0.0)
     take = taken.astype(BF)
     slot_gates = jnp.sum(jnp.where(taken, own_gates[:, None, :], 0.0), axis=2)
-    slot_grads = slot_gates[:, :, None] * received[:, :slots].astype(F32)
-    slot_grads = slot_grads.astype(BF).reshape(n_exp * slots, width)
+
+    def weigh(rows):
+        rows = slot_gates[:, :, None] * rows.astype(F32)
+        return rows.astype(BF).reshape(n_exp * slots, split)
+
+    slot_grads = weigh(received[:, :slots])
+    slot_grads_rest = weigh(received_rest)
     slot_gates = slot_gates.reshape(n_exp * slots, 1)
 
     positions = ctx_index * length + jnp.arange(length, dtype=jnp.int32)
@@ -741,12 +750,13 @@
     sigmoid_gate = jax.nn.sigmoid(gate_pre)
     silu_gate = gate_pre * sigmoid_gate
     inner = (silu_gate * up_pre).astype(BF)
-    grad_inner = dot(slot_grads, w_down, ((1,), (1,)))
+    grad_inner = dot(slot_grads, w_down[:, :split], ((1,), (1,))) + dot(
+        slot_grads_rest, w_down[:, split:], ((1,), (1,))
+    )
     grad_gate_pre = (
         grad_inner * up_pre * sigmoid_gate * (1.0 + gate_pre * (1.0 - sigmoid_gate))
     ).astype(BF)
     grad_up_pre = (grad_inner * silu_gate).astype(BF)
-    split = width // 2
 
     def give_back(at):
         rows = dot(grad_gate_pre, w_gate[at], ((1,), (1,))) + dot(grad_up_pre, w_up[at], ((1,), (1,)))
@@ -772,7 +782,7 @@
     mixed_part = dot(pick, out_back, ((0,), (0,))).astype(BF)
     mixed = lax.psum_scatter(mixed_part, "ctx", scatter_dimension=0, tiled=True)
     hidden_out = (mid + mixed.astype(F32)).astype(BF)
-    grad_down = dot(inner, slot_grads, ((0,), (0,)))
+    grad_down = dot(inner, jnp.concatenate([slot_grads, slot_grads_rest], axis=1), ((0,), (0,)))
     grad_gate_mat = dot(arrived, grad_gate_pre, ((0,), (0,)))
     grad_up_mat = dot(arrived, grad_up_pre, ((0,), (0,)))
 

time: 857 us -> 829 us (0.967)
  Pallas kernels: 399 us -> 363 us
    pallas_call x1, Pallas kernels: 60.1 us -> 35.7 us  [reduce_rows(): pl.pallas_call(reduce_kernel, out_shape=jax.ShapeDtypeStruct((rows, width...]
    all_to_all x0 -> x1, waiting for transfers between devices: none -> 11.1 us  [per_device(): lax.all_to_all(packed_rows[:, :, split:], 'exp', split_axis=0, concat_axi...]
    pallas_call x3, Pallas kernels: 134 us -> 123 us  [gather_rows(): pl.pallas_call(functools.partial(gather_kernel, n_line), out_shape=jax.Sh...]
    dot_general x23 -> x24, matrix products: 123 us -> 121 us  [dot(): return lax.dot_general(a, b, (dims, ((), ())), preferred_element_type=F32)]
    unnamed x166 -> x168, local copies, waits for them, and re-layouts: 17.9 us -> 18.1 us
  transfers between devices with their start and end apart: 13 -> 14, of which waited for: 6 -> 7; matrix products, arithmetic and copies ran while one was open for 16% -> 18% of each run, Pallas kernels for 38% -> 35%
where the time goes in v5:
time: 829 us; the launch traced here: 819 us
  Pallas kernels  363 us (44%)
  waiting for transfers between devices  165 us (20%)
  matrix products  148 us (18%)
  other arithmetic  61.9 us (7%)
  local copies, waits for them, and re-layouts  36.8 us (4%)
  starting transfers between devices  27.6 us (3%)
  between operations  15.9 us (2%)
    pallas_call x3, Pallas kernels, gather_rows(): pl.pallas_call(functools.partial(gather_kernel, n_line), out_shape=jax.Sh...  123 us
    dot_general x24, matrix products, dot(): return lax.dot_general(a, b, (dims, ((), ())), preferred_element_type=F32)  121 us
    pallas_call x1, Pallas kernels, column_sum(): pl.pallas_call(functools.partial(column_sum_kernel, n_ctx, n_exp, subs),...  115 us
    pallas_call x1, Pallas kernels, line_sum(): pl.pallas_call(functools.partial(line_sum_kernel, n_ctx, chunks), out_sha...  58.5 us
    all_gather x1, waiting for transfers between devices, per_device(): lax.all_gather(jnp.concatenate([grad_out[0], gate_parts], axis=1), 'ctx',...  41.6 us
    pallas_call x1, Pallas kernels, reduce_rows(): pl.pallas_call(reduce_kernel, out_shape=jax.ShapeDtypeStruct((rows, width...  35.7 us
    pallas_call x1, Pallas kernels, spread_columns(): pl.pallas_call(functools.partial(spread_kernel, n_exp, sharers), out_shap...  30.9 us
    all_to_all x1, waiting for transfers between devices, per_device(): lax.all_to_all(second, 'exp', split_axis=0, concat_axis=0, tiled=True)  28.7 us
  transfers between devices with their start and end apart: 14, of which 7 were waited for; matrix products, arithmetic and copies ran while one was open for 18% of the time, Pallas kernels for 35%

profile of v5, /device:TPU:0, one launch (start us, length us, event | category | flops | bytes accessed | tf_op | source)
XLA Modules:
  0.0 818.8 jit_solution(10785670009360180943)
XLA Ops:
  9.9 25.1 %shard_map.246 = bf16[8,1,2,64,2048]{4,3,2,1,0:T(8,128)(2,1)} custom-call(bf16[2,64,2048]{2,1,0:T(8,128)(2,1)} %bitcast.247), custom_call_target="tpu_custom_call" | custom-call | tf_op jit(solution)/shard_map/pallas_call | solution.py:434
  35.1 3.2 fusion
  38.5 30.9 %shard_map.247 = (bf16[8,256,640]{2,1,0:T(8,128)(2,1)S(1)}, bf16[8,16,128]{2,1,0:T(8,128)(2,1)S(1)}) custom-call(bf16[256,4096]{1,0:T(8,128)(2,1)S(1)} %copy-done.4, bf16[4,2,256,128]{3,2,1,0:T(8,128)(2,1)S(1)} %maximum_bitcast_fusion.halves_ref, bf16[16,128]{1,0:T(8,128)(2,1)S(1)} %fusion.119.gains_ref), custom_call_target="tpu_custom_call" | custom-call | tf_op jit(solution)/shard_map/pallas_call | solution.py:572
  71.7 3.4 fusion.2
  75.1 3.4 fusion.139
  82.4 28.5 %all-gather.5.cloned.1.call-done = bf16[4096,128]{1,0:T(8,128)(2,1)} async-done(((bf16[1024,128]{1,0:T(8,128)(2,1)}), bf16[4096,128]{1,0:T(8,128)(2,1)}) %all-gather.5.cloned.1.call-update) | async-done | bytes 1048592 | tf_op jit(solution)/shard_map/all_gather | solution.py:712
  110.8 3.1 slice.161
  118.6 41.6 %all-gather.3.cloned.1.call-done = bf16[512,2176]{1,0:T(8,128)(2,1)} async-done(((bf16[128,2176]{1,0:T(8,128)(2,1)}), bf16[512,2176]{1,0:T(8,128)(2,1)}) %all-gather.3.cloned.1.call-update) | async-done | bytes 2228240 | tf_op jit(solution)/shard_map/all_gather | solution.py:648
  162.0 4.8 convolution_convert_fusion
  166.8 2.2 fusion.133
  169.0 1.9 fusion.32
  170.9 4.6 all-to-all-start
  175.5 2.9 reshape.344
  178.4 2.9 multiply_reduce_fusion.4
  184.1 2.5 fusion.89
  186.9 2.2 fusion.10
  189.2 2.8 divide_convert_fusion
  193.9 3.6 convolution_convert_fusion.3
  197.6 35.7 %shard_map.248 = f32[128,2048]{1,0:T(8,128)S(1)} custom-call(bf16[8,128,2048]{2,1,0:T(8,128)(2,1)S(1)} %bitcast.237), custom_call_target="tpu_custom_call" | custom-call | tf_op jit(solution)/shard_map/pallas_call | solution.py:514
  235.1 75.2 %shard_map.249 = bf16[8,4,2,64,2048]{4,3,2,1,0:T(8,128)(2,1)} custom-call(bf16[2,64,2048]{2,1,0:T(8,128)(2,1)} %bitcast.281), custom_call_target="tpu_custom_call" | custom-call | tf_op jit(solution)/shard_map/pallas_call | solution.py:434
  310.2 4.6 all-to-all-start.1
  316.0 9.0 %convolution_convert_fusion.1 = bf16[8,168,2048]{2,1,0:T(8,128)(2,1)S(1)} fusion(bf16[8,512,2048]{2,1,0:T(8,128)(2,1)} %bitcast.241, s32[8,512]{1,0:T(8,128)S(1)} %convolution_convert_fusion.6, pred[8,512]{1,0:T(8,128)(4,1)S(1)} %broadcast_compare_fusion), kind=kOutput, calls=%fused_computation.25 | convolution fusion | flops 2822701056 | bytes 22302720 | tf_op jit(solution)/shard_map/dot_general | solution.py:745
  325.6 5.9 fusion.27
  331.6 5.9 fusion.29
  337.5 11.1 %all-to-all-done.1 = bf16[8,168,1024]{2,1,0:T(8,128)(2,1)} async-done(((bf16[8,168,1024]{2,1,0:T(8,128)(2,1)}), bf16[8,168,1024]{2,1,0:T(8,128)(2,1)}, u32[]{:S(2)}, u32[]{:S(2)}) %all-to-all-start.1) | async-done | bytes 2752544 | tf_op jit(solution)/shard_map/all_to_all | solution.py:682
  348.6 3.3 multiply_convert_fusion.3
  352.1 2.4 fusion.52
  356.0 8.1 multiply_convert_fusion.6
  364.1 2.4 fusion.58
  367.5 4.0 add_convert_fusion.1
  371.5 4.4 all-to-all-start.2
  375.9 4.5 fusion.55
  380.5 4.0 add_convert_fusion
  384.5 25.1 %all-to-all-done.2 = bf16[8,168,1024]{2,1,0:T(8,128)(2,1)} async-done(((bf16[8,168,1024]{2,1,0:T(8,128)(2,1)}), bf16[8,168,1024]{2,1,0:T(8,128)(2,1)}, u32[]{:S(2)}, u32[]{:S(2)}) %all-to-all-start.2) | async-done | bytes 2752544 | tf_op jit(solution)/shard_map/all_to_all | solution.py:769
  409.5 4.5 all-to-all-start.3
  414.2 4.6 bitcast_convert_fusion.2
  419.0 28.7 %all-to-all-done.3 = bf16[8,168,1024]{2,1,0:T(8,128)(2,1)} async-done(((bf16[8,168,1024]{2,1,0:T(8,128)(2,1)}), bf16[8,168,1024]{2,1,0:T(8,128)(2,1)}, u32[]{:S(2)}, u32[]{:S(2)}) %all-to-all-start.3) | async-done | bytes 2752544 | tf_op jit(solution)/shard_map/all_to_all | solution.py:771
  447.7 4.6 bitcast_convert_fusion.1
  452.4 9.4 %multiply_convert_fusion = bf16[1344,2048]{1,0:T(8,128)(2,1)} fusion(bf16[1344,768]{1,0:T(8,128)(2,1)} %get-tuple-element.45, f32[1344]{0:T(1024)S(1)} %mul.470, bf16[1,768,2048]{2,1,0:T(8,128)(2,1)} %param.28), kind=kOutput, calls=%fused_computation | convolution fusion | flops 4233363456 | bytes 10720512 | tf_op jit(solution)/shard_map/dot_general | solution.py:55
  461.8 16.0 %reduce-scatter.7.cloned.1.call-done = bf16[128,1024]{1,0:T(8,128)(2,1)} async-done(((bf16[512,1024]{1,0:T(8,128)(2,1)}), bf16[128,1024]{1,0:T(8,128)(2,1)}) %reduce-scatter.7.cloned.1.call-update) | async-done | bytes 262160 | tf_op jit(solution)/shard_map/reduce_scatter | solution.py:767
  479.3 2.3 fusion.131
  481.7 23.2 %shard_map.250 = bf16[8,1,2,64,2048]{4,3,2,1,0:T(8,128)(2,1)} custom-call(bf16[2,64,2048]{2,1,0:T(8,128)(2,1)} %bitcast.280), custom_call_target="tpu_custom_call" | custom-call | tf_op jit(solution)/shard_map/pallas_call | solution.py:434
  504.9 4.7 all-to-all-start.4
  509.6 4.8 convolution_convert_fusion.4
  514.4 58.5 %shard_map.251 = f32[16,32,2048]{2,1,0:T(8,128)S(1)} custom-call(bf16[16,32,2048]{2,1,0:T(8,128)(2,1)S(1)} %bitcast.238), custom_call_target="tpu_custom_call" | custom-call | tf_op jit(solution)/shard_map/pallas_call | solution.py:196
  572.9 2.0 copy-done.2
  574.9 3.3 convolution_convert_fusion.5
  578.2 7.2 bitcast_convert_fusion
  587.8 4.7 fusion.17
  592.6 5.5 multiply_convert_fusion.2
  602.2 2.7 multiply_bitcast_fusion
  606.1 4.2 all-to-all-start.5
  610.5 4.0 fusion.134
  614.5 4.3 multiply_reduce_fusion.1
  618.9 2.7 multiply_convert_fusion.11
  622.8 13.6 %all-to-all-done.5 = bf16[4,1024,128]{2,1,0:T(8,128)(2,1)} async-done(((bf16[4,1024,128]{2,1,0:T(8,128)(2,1)}), bf16[4,1024,128]{2,1,0:T(8,128)(2,1)}, u32[]{:S(2)}, u32[]{:S(2)}) %all-to-all-start.5) | async-done | bytes 1048608 | tf_op jit(solution)/shard_map/all_to_all | solution.py:812
  641.2 5.0 convolution_convert_fusion.2
  647.0 10.2 %convolution_bitcast_fusion = f32[1,2048,768]{2,1,0:T(8,128)} fusion(bf16[1344,2048]{1,0:T(8,128)(2,1)} %bitcast.252, bf16[1344,768]{1,0:T(8,128)(2,1)} %copy-done.74), kind=kOutput, calls=%fused_computation.45 | convolution fusion | flops 4227858432 | bytes 13860864 | tf_op jit(solution)/shard_map/dot_general | solution.py:55
  657.2 7.3 fusion.23
  664.5 9.7 %convolution_bitcast_fusion.1 = f32[1,2048,768]{2,1,0:T(8,128)} fusion(bf16[1344,2048]{1,0:T(8,128)(2,1)} %bitcast.253, bf16[1344,768]{1,0:T(8,128)(2,1)} %copy-done.73), kind=kOutput, calls=%fused_computation.46 | convolution fusion | flops 4227858432 | bytes 13860864 | tf_op jit(solution)/shard_map/dot_general | solution.py:55
  674.5 6.0 fusion.26
  680.8 114.9 %shard_map.252 = bf16[8,4,72,640]{3,2,1,0:T(8,128)(2,1)S(1)} custom-call(bf16[32,72,640]{2,1,0:T(8,128)(2,1)S(1)} %bitcast.234), custom_call_target="tpu_custom_call" | custom-call | tf_op jit(solution)/shard_map/pallas_call | solution.py:261
  805.2 3.4 fusion.80
  808.7 2.1 copy.157
  (278 shorter events, 53.5 us)
Async XLA Ops:
  7.2 186.7 %copy-start = (bf16[512,2048]{1,0:T(8,128)(2,1)S(1)}, bf16[512,2048]{1,0:T(8,128)(2,1)}, u32[]{:S(2)}) copy-start(bf16[512,2048]{1,0:T(8,128)(2,1)} %param.24) | copy-start | bytes 6291460
  7.2 103.6 %all-gather.5.cloned.1.call-start = ((), (), s32[]{:S(2)}) async-start(), calls=%async_computation.11 | async-start | bytes 1310720 | tf_op jit(solution)/shard_map/all_gather | solution.py:712
  35.0 3.3 copy-start.60
  35.1 3.3 copy-start.63
  35.1 3.3 copy-start.64
  35.1 3.3 copy-start.65
  35.1 3.4 copy-start.4
  71.4 112.6 %copy-start.32 = (f32[128,128]{1,0:T(8,128)}, f32[128,128]{1,0:T(8,128)S(1)}, u32[]{:S(2)}) copy-start(f32[128,128]{1,0:T(8,128)S(1)} %pad_maximum_fusion.5) | copy-start | bytes 196612
  71.5 112.6 %copy-start.34 = (f32[128,128]{1,0:T(8,128)}, f32[128,128]{1,0:T(8,128)S(1)}, u32[]{:S(2)}) copy-start(f32[128,128]{1,0:T(8,128)S(1)} %pad_maximum_fusion.6) | copy-start | bytes 196612
  71.6 3.5 copy-start.44
  71.6 7.5 copy-start.52
  71.7 3.4 copy-start.42
  71.7 3.4 copy-start.7
  81.1 79.1 %all-gather.3.cloned.1.call-start = ((), (), s32[]{:S(2)}) async-start(), calls=%async_computation.10 | async-start | bytes 2785280 | tf_op jit(solution)/shard_map/all_gather | solution.py:648
  110.8 4.0 collective-permute-start
  161.2 5.6 copy-start.48
  161.5 5.4 copy-start.50
  170.9 139.3 %all-to-all-start = ((bf16[8,176,1024]{2,1,0:T(8,128)(2,1)}), bf16[8,176,1024]{2,1,0:T(8,128)(2,1)}, u32[]{:S(2)}, u32[]{:S(2)}) async-start(bf16[8,176,1024]{2,1,0:T(8,128)(2,1)} %fusion.32), calls=%async_computation | async-start | bytes 5767168 | tf_op jit(solution)/shard_map/all_to_all | solution.py:681
  189.2 3.3 copy-start.72
  192.5 5.1 copy-start.23
  197.6 35.7 %copy-start.16 = (bf16[1,128,2048]{2,1,0:T(8,128)(2,1)S(1)}, bf16[1,128,2048]{2,1,0:T(8,128)(2,1)}, u32[]{:S(2)}) copy-start(bf16[1,128,2048]{2,1,0:T(8,128)(2,1)} %param.15) | copy-start | bytes 1572868
  310.2 38.3 %all-to-all-start.1 = ((bf16[8,168,1024]{2,1,0:T(8,128)(2,1)}), bf16[8,168,1024]{2,1,0:T(8,128)(2,1)}, u32[]{:S(2)}, u32[]{:S(2)}) async-start(bf16[8,168,1024]{2,1,0:T(8,128)(2,1)} %get-tuple-element.46), calls=%async_computation.1 | async-start | bytes 5505024 | tf_op jit(solution)/shard_map/all_to_all | solution.py:682
  316.0 9.6 %copy-start.68 = (bf16[1,2048,768]{2,1,0:T(8,128)(2,1)S(1)}, bf16[1,2048,768]{2,1,0:T(8,128)(2,1)}, u32[]{:S(2)}) copy-start(bf16[1,2048,768]{2,1,0:T(8,128)(2,1)} %param.27) | copy-start | bytes 9437188
  324.9 6.6 copy-start.18
  325.6 6.0 copy-start.66
  348.6 3.5 copy-start.71
  352.1 3.9 copy-start.76
  356.0 8.1 copy-start.67
  364.1 3.4 copy-start.69
  371.5 38.1 %all-to-all-start.2 = ((bf16[8,168,1024]{2,1,0:T(8,128)(2,1)}), bf16[8,168,1024]{2,1,0:T(8,128)(2,1)}, u32[]{:S(2)}, u32[]{:S(2)}) async-start(bf16[8,168,1024]{2,1,0:T(8,128)(2,1)} %bitcast.278), calls=%async_computation.2 | async-start | bytes 5505024 | tf_op jit(solution)/shard_map/all_to_all | solution.py:769
  375.9 4.6 copy-start.70
  375.9 4.6 copy-start.75
  409.5 4.6 copy-start.49
  409.5 4.6 copy-start.51
  409.5 38.2 %all-to-all-start.3 = ((bf16[8,168,1024]{2,1,0:T(8,128)(2,1)}), bf16[8,168,1024]{2,1,0:T(8,128)(2,1)}, u32[]{:S(2)}, u32[]{:S(2)}) async-start(bf16[8,168,1024]{2,1,0:T(8,128)(2,1)} %bitcast.277), calls=%async_computation.4 | async-start | bytes 5505024 | tf_op jit(solution)/shard_map/all_to_all | solution.py:771
  414.1 47.8 %reduce-scatter.5.cloned.1.call-start = ((), (), s32[]{:S(2)}) async-start(), calls=%async_computation.12 | async-start | bytes 1310720 | tf_op jit(solution)/shard_map/reduce_scatter | solution.py:767
  418.8 59.1 %reduce-scatter.7.cloned.1.call-start = ((), (), s32[]{:S(2)}) async-start(), calls=%async_computation.13 | async-start | bytes 1310720 | tf_op jit(solution)/shard_map/reduce_scatter | solution.py:767
  479.3 25.5 %copy-start.58 = (f32[128]{0:T(128)}, f32[128]{0:T(128)S(1)}, u32[]{:S(2)}) copy-start(f32[128]{0:T(128)S(1)} %broadcast_multiply_fusion.4) | copy-start | bytes 1540
  504.9 73.4 %all-to-all-start.4 = ((bf16[8,168,2048]{2,1,0:T(8,128)(2,1)}), bf16[8,168,2048]{2,1,0:T(8,128)(2,1)}, u32[]{:S(2)}, u32[]{:S(2)}) async-start(bf16[8,168,2048]{2,1,0:T(8,128)(2,1)} %bitcast.254), calls=%async_computation.6 | async-start | bytes 11010048 | tf_op jit(solution)/shard_map/all_to_all | solution.py:673
  514.4 60.5 %copy-start.22 = (bf16[8,1,2,64,2048]{4,3,2,1,0:T(8,128)(2,1)S(1)}, bf16[8,1,2,64,2048]{4,3,2,1,0:T(8,128)(2,1)}, u32[]{:S(2)}) copy-start(bf16[8,1,2,64,2048]{4,3,2,1,0:T(8,128)(2,1)} %shard_map.250) | copy-start | bytes 12582916
  587.8 4.8 copy-start.37
  592.6 5.5 copy-start.26
  599.8 5.1 collective-permute-start.1
  602.1 4.0 copy-start.11
  606.1 30.2 %all-to-all-start.5 = ((bf16[4,1024,128]{2,1,0:T(8,128)(2,1)}), bf16[4,1024,128]{2,1,0:T(8,128)(2,1)}, u32[]{:S(2)}, u32[]{:S(2)}) async-start(bf16[4,1024,128]{2,1,0:T(8,128)(2,1)} %bitcast.270), calls=%async_computation.8 | async-start | bytes 2097152 | tf_op jit(solution)/shard_map/all_to_all | solution.py:812
  610.4 4.1 copy-start.10
  610.4 4.1 copy-start.33
  610.4 4.1 copy-start.55
  610.4 193.2 %reduce-scatter.11.cloned.1.call-start = ((), (), s32[]{:S(2)}) async-start(), calls=%async_computation.15 | async-start | bytes 4718592 | tf_op jit(solution)/shard_map/reduce_scatter | solution.py:833
  610.5 4.0 copy-start.12
  610.5 4.0 copy-start.15
  622.8 15.3 %copy-start.47 = (f32[1024]{0:T(1024)S(1)}, f32[1024]{0:T(1024)}, u32[]{:S(2)}) copy-start(f32[1024]{0:T(1024)} %copy-done.46) | copy-start | bytes 12292
  622.8 15.3 %copy-start.53 = (f32[128]{0:T(128)S(1)}, f32[128]{0:T(128)}, u32[]{:S(2)}) copy-start(f32[128]{0:T(128)} %copy-done.52) | copy-start | bytes 1540
  646.2 159.0 %reduce-scatter.9.cloned.1.call-start = ((), (), s32[]{:S(2)}) async-start(), calls=%async_computation.14 | async-start | bytes 2621440 | tf_op jit(solution)/shard_map/reduce_scatter | solution.py:783
  647.0 10.2 %copy-start.28 = (bf16[8,168,1024]{2,1,0:T(8,128)(2,1)S(1)}, bf16[8,168,1024]{2,1,0:T(8,128)(2,1)}, u32[]{:S(2)}) copy-start(bf16[8,168,1024]{2,1,0:T(8,128)(2,1)} %copy-done.27) | copy-start | bytes 8257540
  647.0 10.2 %copy-start.30 = (bf16[8,168,1024]{2,1,0:T(8,128)(2,1)S(1)}, bf16[8,168,1024]{2,1,0:T(8,128)(2,1)}, u32[]{:S(2)}) copy-start(bf16[8,168,1024]{2,1,0:T(8,128)(2,1)} %copy-done.29) | copy-start | bytes 8257540
  647.0 10.2 %copy-start.77 = (bf16[1344,768]{1,0:T(8,128)(2,1)S(1)}, bf16[1344,768]{1,0:T(8,128)(2,1)}, u32[]{:S(2)}) copy-start(bf16[1344,768]{1,0:T(8,128)(2,1)} %get-tuple-element.45) | copy-start | bytes 6193156
  664.5 10.0 %copy-start.39 = (bf16[128,8,4,128]{3,1,2,0:T(8,128)(2,1)S(1)}, bf16[128,8,4,128]{3,1,2,0:T(8,128)(2,1)}, u32[]{:S(2)}) copy-start(bf16[128,8,4,128]{3,1,2,0:T(8,128)(2,1)} %copy.151) | copy-start | bytes 3145732
  664.5 10.0 %copy-start.43 = (f32[1,2,8,128]{3,1,2,0:T(2,128)S(1)}, f32[1,2,8,128]{3,1,2,0:T(2,128)}, u32[]{:S(2)}) copy-start(f32[1,2,8,128]{3,1,2,0:T(2,128)} %copy-done.42) | copy-start | bytes 24580
  798.6 3.7 copy-start.13
  798.7 3.2 copy-start.5
  801.8 3.4 copy-start.31
  801.8 3.4 copy-start.59
  805.2 3.4 copy-start.3
  (28 other events, 59.4 us)
Sparse Core Ops, SparseCore 0:
  81.2 29.5 all-gather.4
  113.0 47.1 all-gather.2
  418.9 27.5 reduce-scatter.4
  452.5 25.3 reduce-scatter.6
  646.3 50.3 reduce-scatter.10
  698.9 65.4 reduce-scatter.8

commit v6 on v5

--- a/solution.py
+++ b/solution.py
@@ -74,14 +74,14 @@
         return pltpu.make_async_remote_copy(
             src_ref=to_right.at[k], dst_ref=from_left.at[k],
             send_sem=right_send.at[k], recv_sem=right_recv.at[k],
-            device_id={"ctx": ctx + 1}, device_id_type=MESH,
+            device_id={"ctx": jnp.minimum(ctx + 1, last)}, device_id_type=MESH,
         )
 
     def copy_left(k):
         return pltpu.make_async_remote_copy(
             src_ref=to_left.at[k], dst_ref=from_right.at[k],
             send_sem=left_send.at[k], recv_sem=left_recv.at[k],
-            device_id={"ctx": ctx - 1}, device_id_type=MESH,
+            device_id={"ctx": jnp.maximum(ctx - 1, 0)}, device_id_type=MESH,
         )
 
     def step(time, carry):
@@ -299,7 +299,7 @@
         step = 2 * way - 1
         return send(
             src, (exp, line), half, z_send.at[way, line, half], z_recv.at[line, half],
-            {"ctx": ctx + step},
+            {"ctx": jnp.clip(ctx + step, 0, last)},
         )
 
     def to_x(src, line, half):

time: 829 us -> 829 us (level)
  no operation moved by 1% of the time
where the time goes in v6:
time: 829 us; the launch traced here: 819 us
  Pallas kernels  363 us (44%)
  waiting for transfers between devices  165 us (20%)
  matrix products  148 us (18%)
  other arithmetic  61.9 us (7%)
  local copies, waits for them, and re-layouts  36.8 us (4%)
  starting transfers between devices  27.6 us (3%)
  between operations  15.9 us (2%)
    pallas_call x3, Pallas kernels, gather_rows(): pl.pallas_call(functools.partial(gather_kernel, n_line), out_shape=jax.Sh...  123 us
    dot_general x24, matrix products, dot(): return lax.dot_general(a, b, (dims, ((), ())), preferred_element_type=F32)  121 us
    pallas_call x1, Pallas kernels, column_sum(): pl.pallas_call(functools.partial(column_sum_kernel, n_ctx, n_exp, subs),...  115 us
    pallas_call x1, Pallas kernels, line_sum(): pl.pallas_call(functools.partial(line_sum_kernel, n_ctx, chunks), out_sha...  58.5 us
    all_gather x1, waiting for transfers between devices, per_device(): lax.all_gather(jnp.concatenate([grad_out[0], gate_parts], axis=1), 'ctx',...  41.6 us
    pallas_call x1, Pallas kernels, reduce_rows(): pl.pallas_call(reduce_kernel, out_shape=jax.ShapeDtypeStruct((rows, width...  35.7 us
    pallas_call x1, Pallas kernels, spread_columns(): pl.pallas_call(functools.partial(spread_kernel, n_exp, sharers), out_shap...  30.9 us
    all_to_all x1, waiting for transfers between devices, per_device(): lax.all_to_all(second, 'exp', split_axis=0, concat_axis=0, tiled=True)  28.7 us
  transfers between devices with their start and end apart: 14, of which 7 were waited for; matrix products, arithmetic and copies ran while one was open for 18% of the time, Pallas kernels for 35%

profile of v6, /device:TPU:0, one launch (start us, length us, event | category | flops | bytes accessed | tf_op | source)
XLA Modules:
  0.0 818.8 jit_solution(7101491136626344571)
XLA Ops:
  9.9 25.1 %shard_map.246 = bf16[8,1,2,64,2048]{4,3,2,1,0:T(8,128)(2,1)} custom-call(bf16[2,64,2048]{2,1,0:T(8,128)(2,1)} %bitcast.247), custom_call_target="tpu_custom_call" | custom-call | tf_op jit(solution)/shard_map/pallas_call | solution.py:434
  35.1 3.2 fusion
  38.5 30.9 %shard_map.247 = (bf16[8,256,640]{2,1,0:T(8,128)(2,1)S(1)}, bf16[8,16,128]{2,1,0:T(8,128)(2,1)S(1)}) custom-call(bf16[256,4096]{1,0:T(8,128)(2,1)S(1)} %copy-done.4, bf16[4,2,256,128]{3,2,1,0:T(8,128)(2,1)S(1)} %maximum_bitcast_fusion.halves_ref, bf16[16,128]{1,0:T(8,128)(2,1)S(1)} %fusion.119.gains_ref), custom_call_target="tpu_custom_call" | custom-call | tf_op jit(solution)/shard_map/pallas_call | solution.py:572
  71.7 3.4 fusion.2
  75.1 3.4 fusion.139
  82.4 28.5 %all-gather.5.cloned.1.call-done = bf16[4096,128]{1,0:T(8,128)(2,1)} async-done(((bf16[1024,128]{1,0:T(8,128)(2,1)}), bf16[4096,128]{1,0:T(8,128)(2,1)}) %all-gather.5.cloned.1.call-update) | async-done | bytes 1048592 | tf_op jit(solution)/shard_map/all_gather | solution.py:712
  110.8 3.1 slice.161
  118.6 41.6 %all-gather.3.cloned.1.call-done = bf16[512,2176]{1,0:T(8,128)(2,1)} async-done(((bf16[128,2176]{1,0:T(8,128)(2,1)}), bf16[512,2176]{1,0:T(8,128)(2,1)}) %all-gather.3.cloned.1.call-update) | async-done | bytes 2228240 | tf_op jit(solution)/shard_map/all_gather | solution.py:648
  162.0 4.8 convolution_convert_fusion
  166.8 2.2 fusion.133
  169.0 1.9 fusion.32
  170.9 4.6 all-to-all-start
  175.5 2.9 reshape.344
  178.4 2.9 multiply_reduce_fusion.4
  184.1 2.5 fusion.89
  186.9 2.2 fusion.10
  189.2 2.8 divide_convert_fusion
  193.9 3.6 convolution_convert_fusion.3
  197.6 35.7 %shard_map.248 = f32[128,2048]{1,0:T(8,128)S(1)} custom-call(bf16[8,128,2048]{2,1,0:T(8,128)(2,1)S(1)} %bitcast.237), custom_call_target="tpu_custom_call" | custom-call | tf_op jit(solution)/shard_map/pallas_call | solution.py:514
  235.1 75.2 %shard_map.249 = bf16[8,4,2,64,2048]{4,3,2,1,0:T(8,128)(2,1)} custom-call(bf16[2,64,2048]{2,1,0:T(8,128)(2,1)} %bitcast.281), custom_call_target="tpu_custom_call" | custom-call | tf_op jit(solution)/shard_map/pallas_call | solution.py:434
  310.2 4.6 all-to-all-start.1
  316.0 9.0 %convolution_convert_fusion.1 = bf16[8,168,2048]{2,1,0:T(8,128)(2,1)S(1)} fusion(bf16[8,512,2048]{2,1,0:T(8,128)(2,1)} %bitcast.241, s32[8,512]{1,0:T(8,128)S(1)} %convolution_convert_fusion.6, pred[8,512]{1,0:T(8,128)(4,1)S(1)} %broadcast_compare_fusion), kind=kOutput, calls=%fused_computation.25 | convolution fusion | flops 2822701056 | bytes 22302720 | tf_op jit(solution)/shard_map/dot_general | solution.py:745
  325.6 5.9 fusion.27
  331.6 5.9 fusion.29
  337.5 11.1 %all-to-all-done.1 = bf16[8,168,1024]{2,1,0:T(8,128)(2,1)} async-done(((bf16[8,168,1024]{2,1,0:T(8,128)(2,1)}), bf16[8,168,1024]{2,1,0:T(8,128)(2,1)}, u32[]{:S(2)}, u32[]{:S(2)}) %all-to-all-start.1) | async-done | bytes 2752544 | tf_op jit(solution)/shard_map/all_to_all | solution.py:682
  348.6 3.3 multiply_convert_fusion.3
  352.1 2.4 fusion.52
  356.0 8.1 multiply_convert_fusion.6
  364.1 2.4 fusion.58
  367.5 4.0 add_convert_fusion.1
  371.5 4.4 all-to-all-start.2
  375.9 4.5 fusion.55
  380.5 4.0 add_convert_fusion
  384.5 25.1 %all-to-all-done.2 = bf16[8,168,1024]{2,1,0:T(8,128)(2,1)} async-done(((bf16[8,168,1024]{2,1,0:T(8,128)(2,1)}), bf16[8,168,1024]{2,1,0:T(8,128)(2,1)}, u32[]{:S(2)}, u32[]{:S(2)}) %all-to-all-start.2) | async-done | bytes 2752544 | tf_op jit(solution)/shard_map/all_to_all | solution.py:769
  409.5 4.5 all-to-all-start.3
  414.2 4.6 bitcast_convert_fusion.2
  419.0 28.7 %all-to-all-done.3 = bf16[8,168,1024]{2,1,0:T(8,128)(2,1)} async-done(((bf16[8,168,1024]{2,1,0:T(8,128)(2,1)}), bf16[8,168,1024]{2,1,0:T(8,128)(2,1)}, u32[]{:S(2)}, u32[]{:S(2)}) %all-to-all-start.3) | async-done | bytes 2752544 | tf_op jit(solution)/shard_map/all_to_all | solution.py:771
  447.7 4.6 bitcast_convert_fusion.1
  452.4 9.4 %multiply_convert_fusion = bf16[1344,2048]{1,0:T(8,128)(2,1)} fusion(bf16[1344,768]{1,0:T(8,128)(2,1)} %get-tuple-element.45, f32[1344]{0:T(1024)S(1)} %mul.470, bf16[1,768,2048]{2,1,0:T(8,128)(2,1)} %param.28), kind=kOutput, calls=%fused_computation | convolution fusion | flops 4233363456 | bytes 10720512 | tf_op jit(solution)/shard_map/dot_general | solution.py:55
  461.8 16.0 %reduce-scatter.7.cloned.1.call-done = bf16[128,1024]{1,0:T(8,128)(2,1)} async-done(((bf16[512,1024]{1,0:T(8,128)(2,1)}), bf16[128,1024]{1,0:T(8,128)(2,1)}) %reduce-scatter.7.cloned.1.call-update) | async-done | bytes 262160 | tf_op jit(solution)/shard_map/reduce_scatter | solution.py:767
  479.3 2.3 fusion.131
  481.7 23.2 %shard_map.250 = bf16[8,1,2,64,2048]{4,3,2,1,0:T(8,128)(2,1)} custom-call(bf16[2,64,2048]{2,1,0:T(8,128)(2,1)} %bitcast.280), custom_call_target="tpu_custom_call" | custom-call | tf_op jit(solution)/shard_map/pallas_call | solution.py:434
  504.9 4.7 all-to-all-start.4
  509.6 4.8 convolution_convert_fusion.4
  514.4 58.5 %shard_map.251 = f32[16,32,2048]{2,1,0:T(8,128)S(1)} custom-call(bf16[16,32,2048]{2,1,0:T(8,128)(2,1)S(1)} %bitcast.238), custom_call_target="tpu_custom_call" | custom-call | tf_op jit(solution)/shard_map/pallas_call | solution.py:196
  572.9 2.0 copy-done.2
  574.9 3.3 convolution_convert_fusion.5
  578.2 7.2 bitcast_convert_fusion
  587.8 4.7 fusion.17
  592.6 5.5 multiply_convert_fusion.2
  602.2 2.7 multiply_bitcast_fusion
  606.1 4.2 all-to-all-start.5
  610.5 4.0 fusion.134
  614.5 4.3 multiply_reduce_fusion.1
  618.9 2.7 multiply_convert_fusion.11
  622.8 13.6 %all-to-all-done.5 = bf16[4,1024,128]{2,1,0:T(8,128)(2,1)} async-done(((bf16[4,1024,128]{2,1,0:T(8,128)(2,1)}), bf16[4,1024,128]{2,1,0:T(8,128)(2,1)}, u32[]{:S(2)}, u32[]{:S(2)}) %all-to-all-start.5) | async-done | bytes 1048608 | tf_op jit(solution)/shard_map/all_to_all | solution.py:812
  641.2 5.0 convolution_convert_fusion.2
  647.0 10.2 %convolution_bitcast_fusion = f32[1,2048,768]{2,1,0:T(8,128)} fusion(bf16[1344,2048]{1,0:T(8,128)(2,1)} %bitcast.252, bf16[1344,768]{1,0:T(8,128)(2,1)} %copy-done.74), kind=kOutput, calls=%fused_computation.45 | convolution fusion | flops 4227858432 | bytes 13860864 | tf_op jit(solution)/shard_map/dot_general | solution.py:55
  657.2 7.3 fusion.23
  664.5 9.7 %convolution_bitcast_fusion.1 = f32[1,2048,768]{2,1,0:T(8,128)} fusion(bf16[1344,2048]{1,0:T(8,128)(2,1)} %bitcast.253, bf16[1344,768]{1,0:T(8,128)(2,1)} %copy-done.73), kind=kOutput, calls=%fused_computation.46 | convolution fusion | flops 4227858432 | bytes 13860864 | tf_op jit(solution)/shard_map/dot_general | solution.py:55
  674.5 6.0 fusion.26
  680.8 114.9 %shard_map.252 = bf16[8,4,72,640]{3,2,1,0:T(8,128)(2,1)S(1)} custom-call(bf16[32,72,640]{2,1,0:T(8,128)(2,1)S(1)} %bitcast.234), custom_call_target="tpu_custom_call" | custom-call | tf_op jit(solution)/shard_map/pallas_call | solution.py:261
  805.2 3.4 fusion.80
  808.6 2.1 copy.157
  (278 shorter events, 53.5 us)
Async XLA Ops:
  7.2 186.7 %copy-start = (bf16[512,2048]{1,0:T(8,128)(2,1)S(1)}, bf16[512,2048]{1,0:T(8,128)(2,1)}, u32[]{:S(2)}) copy-start(bf16[512,2048]{1,0:T(8,128)(2,1)} %param.24) | copy-start | bytes 6291460
  7.2 103.6 %all-gather.5.cloned.1.call-start = ((), (), s32[]{:S(2)}) async-start(), calls=%async_computation.11 | async-start | bytes 1310720 | tf_op jit(solution)/shard_map/all_gather | solution.py:712
  35.0 3.3 copy-start.60
  35.1 3.3 copy-start.63
  35.1 3.3 copy-start.64
  35.1 3.3 copy-start.65
  35.1 3.4 copy-start.4
  71.4 112.6 %copy-start.32 = (f32[128,128]{1,0:T(8,128)}, f32[128,128]{1,0:T(8,128)S(1)}, u32[]{:S(2)}) copy-start(f32[128,128]{1,0:T(8,128)S(1)} %pad_maximum_fusion.5) | copy-start | bytes 196612
  71.5 112.6 %copy-start.34 = (f32[128,128]{1,0:T(8,128)}, f32[128,128]{1,0:T(8,128)S(1)}, u32[]{:S(2)}) copy-start(f32[128,128]{1,0:T(8,128)S(1)} %pad_maximum_fusion.6) | copy-start | bytes 196612
  71.6 3.5 copy-start.44
  71.6 7.5 copy-start.52
  71.7 3.4 copy-start.42
  71.7 3.4 copy-start.7
  81.1 79.1 %all-gather.3.cloned.1.call-start = ((), (), s32[]{:S(2)}) async-start(), calls=%async_computation.10 | async-start | bytes 2785280 | tf_op jit(solution)/shard_map/all_gather | solution.py:648
  110.8 4.0 collective-permute-start
  161.2 5.6 copy-start.48
  161.5 5.4 copy-start.50
  170.9 139.3 %all-to-all-start = ((bf16[8,176,1024]{2,1,0:T(8,128)(2,1)}), bf16[8,176,1024]{2,1,0:T(8,128)(2,1)}, u32[]{:S(2)}, u32[]{:S(2)}) async-start(bf16[8,176,1024]{2,1,0:T(8,128)(2,1)} %fusion.32), calls=%async_computation | async-start | bytes 5767168 | tf_op jit(solution)/shard_map/all_to_all | solution.py:681
  189.2 3.3 copy-start.72
  192.5 5.1 copy-start.23
  197.6 35.7 %copy-start.16 = (bf16[1,128,2048]{2,1,0:T(8,128)(2,1)S(1)}, bf16[1,128,2048]{2,1,0:T(8,128)(2,1)}, u32[]{:S(2)}) copy-start(bf16[1,128,2048]{2,1,0:T(8,128)(2,1)} %param.15) | copy-start | bytes 1572868
  310.2 38.3 %all-to-all-start.1 = ((bf16[8,168,1024]{2,1,0:T(8,128)(2,1)}), bf16[8,168,1024]{2,1,0:T(8,128)(2,1)}, u32[]{:S(2)}, u32[]{:S(2)}) async-start(bf16[8,168,1024]{2,1,0:T(8,128)(2,1)} %get-tuple-element.46), calls=%async_computation.1 | async-start | bytes 5505024 | tf_op jit(solution)/shard_map/all_to_all | solution.py:682
  316.0 9.6 %copy-start.68 = (bf16[1,2048,768]{2,1,0:T(8,128)(2,1)S(1)}, bf16[1,2048,768]{2,1,0:T(8,128)(2,1)}, u32[]{:S(2)}) copy-start(bf16[1,2048,768]{2,1,0:T(8,128)(2,1)} %param.27) | copy-start | bytes 9437188
  324.9 6.6 copy-start.18
  325.6 6.0 copy-start.66
  348.6 3.5 copy-start.71
  352.1 3.9 copy-start.76
  356.0 8.1 copy-start.67
  364.1 3.4 copy-start.69
  371.5 38.1 %all-to-all-start.2 = ((bf16[8,168,1024]{2,1,0:T(8,128)(2,1)}), bf16[8,168,1024]{2,1,0:T(8,128)(2,1)}, u32[]{:S(2)}, u32[]{:S(2)}) async-start(bf16[8,168,1024]{2,1,0:T(8,128)(2,1)} %bitcast.278), calls=%async_computation.2 | async-start | bytes 5505024 | tf_op jit(solution)/shard_map/all_to_all | solution.py:769
  375.9 4.6 copy-start.70
  375.9 4.6 copy-start.75
  409.5 4.6 copy-start.49
  409.5 4.6 copy-start.51
  409.5 38.2 %all-to-all-start.3 = ((bf16[8,168,1024]{2,1,0:T(8,128)(2,1)}), bf16[8,168,1024]{2,1,0:T(8,128)(2,1)}, u32[]{:S(2)}, u32[]{:S(2)}) async-start(bf16[8,168,1024]{2,1,0:T(8,128)(2,1)} %bitcast.277), calls=%async_computation.4 | async-start | bytes 5505024 | tf_op jit(solution)/shard_map/all_to_all | solution.py:771
  414.1 47.8 %reduce-scatter.5.cloned.1.call-start = ((), (), s32[]{:S(2)}) async-start(), calls=%async_computation.12 | async-start | bytes 1310720 | tf_op jit(solution)/shard_map/reduce_scatter | solution.py:767
  418.8 59.1 %reduce-scatter.7.cloned.1.call-start = ((), (), s32[]{:S(2)}) async-start(), calls=%async_computation.13 | async-start | bytes 1310720 | tf_op jit(solution)/shard_map/reduce_scatter | solution.py:767
  479.3 25.5 %copy-start.58 = (f32[128]{0:T(128)}, f32[128]{0:T(128)S(1)}, u32[]{:S(2)}) copy-start(f32[128]{0:T(128)S(1)} %broadcast_multiply_fusion.4) | copy-start | bytes 1540
  504.9 73.4 %all-to-all-start.4 = ((bf16[8,168,2048]{2,1,0:T(8,128)(2,1)}), bf16[8,168,2048]{2,1,0:T(8,128)(2,1)}, u32[]{:S(2)}, u32[]{:S(2)}) async-start(bf16[8,168,2048]{2,1,0:T(8,128)(2,1)} %bitcast.254), calls=%async_computation.6 | async-start | bytes 11010048 | tf_op jit(solution)/shard_map/all_to_all | solution.py:673
  514.4 60.5 %copy-start.22 = (bf16[8,1,2,64,2048]{4,3,2,1,0:T(8,128)(2,1)S(1)}, bf16[8,1,2,64,2048]{4,3,2,1,0:T(8,128)(2,1)}, u32[]{:S(2)}) copy-start(bf16[8,1,2,64,2048]{4,3,2,1,0:T(8,128)(2,1)} %shard_map.250) | copy-start | bytes 12582916
  587.8 4.8 copy-start.37
  592.6 5.5 copy-start.26
  599.8 5.1 collective-permute-start.1
  602.1 4.0 copy-start.11
  606.1 30.2 %all-to-all-start.5 = ((bf16[4,1024,128]{2,1,0:T(8,128)(2,1)}), bf16[4,1024,128]{2,1,0:T(8,128)(2,1)}, u32[]{:S(2)}, u32[]{:S(2)}) async-start(bf16[4,1024,128]{2,1,0:T(8,128)(2,1)} %bitcast.270), calls=%async_computation.8 | async-start | bytes 2097152 | tf_op jit(solution)/shard_map/all_to_all | solution.py:812
  610.4 4.1 copy-start.10
  610.4 4.1 copy-start.33
  610.4 4.1 copy-start.55
  610.4 193.2 %reduce-scatter.11.cloned.1.call-start = ((), (), s32[]{:S(2)}) async-start(), calls=%async_computation.15 | async-start | bytes 4718592 | tf_op jit(solution)/shard_map/reduce_scatter | solution.py:833
  610.5 4.0 copy-start.12
  610.5 4.0 copy-start.15
  622.8 15.3 %copy-start.47 = (f32[1024]{0:T(1024)S(1)}, f32[1024]{0:T(1024)}, u32[]{:S(2)}) copy-start(f32[1024]{0:T(1024)} %copy-done.46) | copy-start | bytes 12292
  622.8 15.3 %copy-start.53 = (f32[128]{0:T(128)S(1)}, f32[128]{0:T(128)}, u32[]{:S(2)}) copy-start(f32[128]{0:T(128)} %copy-done.52) | copy-start | bytes 1540
  646.2 159.0 %reduce-scatter.9.cloned.1.call-start = ((), (), s32[]{:S(2)}) async-start(), calls=%async_computation.14 | async-start | bytes 2621440 | tf_op jit(solution)/shard_map/reduce_scatter | solution.py:783
  647.0 10.2 %copy-start.28 = (bf16[8,168,1024]{2,1,0:T(8,128)(2,1)S(1)}, bf16[8,168,1024]{2,1,0:T(8,128)(2,1)}, u32[]{:S(2)}) copy-start(bf16[8,168,1024]{2,1,0:T(8,128)(2,1)} %copy-done.27) | copy-start | bytes 8257540
  647.0 10.2 %copy-start.30 = (bf16[8,168,1024]{2,1,0:T(8,128)(2,1)S(1)}, bf16[8,168,1024]{2,1,0:T(8,128)(2,1)}, u32[]{:S(2)}) copy-start(bf16[8,168,1024]{2,1,0:T(8,128)(2,1)} %copy-done.29) | copy-start | bytes 8257540
  647.0 10.2 %copy-start.77 = (bf16[1344,768]{1,0:T(8,128)(2,1)S(1)}, bf16[1344,768]{1,0:T(8,128)(2,1)}, u32[]{:S(2)}) copy-start(bf16[1344,768]{1,0:T(8,128)(2,1)} %get-tuple-element.45) | copy-start | bytes 6193156
  664.5 10.0 %copy-start.39 = (bf16[128,8,4,128]{3,1,2,0:T(8,128)(2,1)S(1)}, bf16[128,8,4,128]{3,1,2,0:T(8,128)(2,1)}, u32[]{:S(2)}) copy-start(bf16[128,8,4,128]{3,1,2,0:T(8,128)(2,1)} %copy.151) | copy-start | bytes 3145732
  664.5 10.0 %copy-start.43 = (f32[1,2,8,128]{3,1,2,0:T(2,128)S(1)}, f32[1,2,8,128]{3,1,2,0:T(2,128)}, u32[]{:S(2)}) copy-start(f32[1,2,8,128]{3,1,2,0:T(2,128)} %copy-done.42) | copy-start | bytes 24580
  798.6 3.7 copy-start.13
  798.7 3.2 copy-start.5
  801.8 3.4 copy-start.31
  801.8 3.4 copy-start.59
  805.2 3.4 copy-start.3
  (28 other events, 59.4 us)
Sparse Core Ops, SparseCore 0:
  81.2 29.5 all-gather.4
  113.0 47.1 all-gather.2
  418.9 27.5 reduce-scatter.4
  452.5 25.3 reduce-scatter.6
  646.3 50.3 reduce-scatter.10
  698.9 65.4 reduce-scatter.8
